TPU v7x, 128 devices: a whole 4x4x4 slice. The times are simulated.
128 devices in a mesh: pod: 1, dp: 64 (over z, y, x), tp: 2 (over core).
Axes of the slice: x: 4, y: 4, z: 4, core: 2. Of those that a mesh axis runs over, the one named last changes fastest.
Arguments:
- x_in: bfloat16 [128, 1024, 1024], P(('pod', 'dp'))
- seg_ids: int32 [128, 1024], P(('pod', 'dp'))
- gain_one: bfloat16 [1024], replicated
- gain_two: bfloat16 [1024], replicated
- w_qkv: bfloat16 [1024, 3072], P(None, 'tp')
- w_out: bfloat16 [16, 64, 1024], P('tp')
- w_up: bfloat16 [1024, 4096], P(None, 'tp')
- w_down: bfloat16 [4096, 1024], P('tp')
- grad_y: bfloat16 [128, 1024, 1024], P(('pod', 'dp'))
Outputs:
- output 1: bfloat16 [128, 1024, 1024], P(('pod', 'dp'))
- output 2: bfloat16 [128, 1024, 1024], P(('pod', 'dp'))
- output 3: bfloat16 [1024], P('pod')
- output 4: bfloat16 [1024], P('pod')
- output 5: bfloat16 [1024, 3072], P('pod', 'tp')
- output 6: bfloat16 [16, 64, 1024], P(('pod', 'tp'))
- output 7: bfloat16 [1024, 4096], P('pod', 'tp')
- output 8: bfloat16 [4096, 1024], P(('pod', 'tp'))
All inputs are finite; a program needn't handle non-finite values.
Results may differ from a plain program's by a relative error of at most 0.02.
Values are sent between devices in bfloat16 or wider.
A program may use at most 1 GiB of HBM per device.

v0:
```python
import jax
import jax.numpy as jnp
from jax import lax
from jax.sharding import PartitionSpec as P

EPS_NORM = 1e-5
NEG_LARGE = -1e30


def gelu_tanh(values):
    return jax.nn.gelu(values, approximate=True)


def norm_forward(x_rows, gain_vec):
    x_f32 = x_rows.astype(jnp.float32)
    centered = x_f32 - jnp.mean(x_f32, axis=-1, keepdims=True)
    inv_std = lax.rsqrt(jnp.mean(centered * centered, axis=-1, keepdims=True) + EPS_NORM)
    x_hat = centered * inv_std
    return (x_hat * gain_vec.astype(jnp.float32)).astype(jnp.bfloat16), x_hat, inv_std


def norm_backward(grad_out, x_hat, inv_std, gain_vec):
    grad_f32 = grad_out.astype(jnp.float32)
    grad_gain = jnp.sum(grad_f32 * x_hat, axis=0)
    grad_hat = grad_f32 * gain_vec.astype(jnp.float32)
    mean_one = jnp.mean(grad_hat, axis=-1, keepdims=True)
    mean_two = jnp.mean(grad_hat * x_hat, axis=-1, keepdims=True)
    return inv_std * (grad_hat - mean_one - x_hat * mean_two), grad_gain


def matmul_nt(lhs, rhs):
    return lax.dot_general(lhs, rhs, (((1,), (1,)), ((), ())), preferred_element_type=jnp.float32)


def matmul_tn(lhs, rhs):
    return lax.dot_general(lhs, rhs, (((0,), (0,)), ((), ())), preferred_element_type=jnp.float32)


def attention_forward(q_blk, k_blk, v_blk, allowed, score_scale):
    scores = jnp.einsum("bqnd,bknd->bnqk", q_blk, k_blk, preferred_element_type=jnp.float32) * score_scale
    attn_probs = jax.nn.softmax(jnp.where(allowed, scores, NEG_LARGE), axis=-1)
    attn_out = jnp.einsum("bnqk,bknd->bqnd", attn_probs.astype(jnp.bfloat16), v_blk, preferred_element_type=jnp.float32)
    return attn_out.astype(jnp.bfloat16), attn_probs


def attention_backward(grad_out, q_blk, k_blk, v_blk, attn_probs, score_scale):
    grad_v = jnp.einsum("bnqk,bqnd->bknd", attn_probs.astype(jnp.bfloat16), grad_out, preferred_element_type=jnp.float32)
    grad_probs = jnp.einsum("bqnd,bknd->bnqk", grad_out, v_blk, preferred_element_type=jnp.float32)
    grad_scores = attn_probs * (grad_probs - jnp.sum(grad_probs * attn_probs, axis=-1, keepdims=True))
    grad_low = (grad_scores * score_scale).astype(jnp.bfloat16)
    grad_q = jnp.einsum("bnqk,bknd->bqnd", grad_low, k_blk, preferred_element_type=jnp.float32)
    grad_k = jnp.einsum("bnqk,bqnd->bknd", grad_low, q_blk, preferred_element_type=jnp.float32)
    return grad_q, grad_k, grad_v


def solution(mesh):
    batch_spec = P(("pod", "dp"), None, None)
    seg_spec = P(("pod", "dp"), None)

    def local_step(x_in, seg_ids, gain_one, gain_two, w_qkv, w_out, w_up, w_down, grad_y):
        batch_loc, seq_len, hidden = x_in.shape
        heads_loc = w_out.shape[0]
        head_dim = w_out.shape[1]
        score_scale = head_dim ** -0.5
        tokens = batch_loc * seq_len
        positions = jnp.arange(seq_len)
        allowed = (positions[:, None] >= positions[None, :])[None, None] & (seg_ids[:, None, :, None] == seg_ids[:, None, None, :])
        x_rows = x_in.reshape(tokens, hidden)
        normed_a, hat_a, inv_a = norm_forward(x_rows, gain_one)
        qkv_rows = jnp.dot(normed_a, w_qkv, preferred_element_type=jnp.float32).astype(jnp.bfloat16)
        qkv_rows = qkv_rows.reshape(batch_loc, seq_len, heads_loc, 3, head_dim)
        q_blk = qkv_rows[:, :, :, 0]
        k_blk = qkv_rows[:, :, :, 1]
        v_blk = qkv_rows[:, :, :, 2]
        attn_out, attn_probs = attention_forward(q_blk, k_blk, v_blk, allowed, score_scale)
        attn_rows = attn_out.reshape(tokens, heads_loc, head_dim)
        part_one = lax.dot_general(attn_rows, w_out, (((1, 2), (0, 1)), ((), ())), preferred_element_type=jnp.float32)
        sum_one = lax.psum(part_one.astype(jnp.bfloat16), "tp")
        x_one = (x_rows.astype(jnp.float32) + sum_one.astype(jnp.float32)).astype(jnp.bfloat16)
        normed_b, hat_b, inv_b = norm_forward(x_one, gain_two)
        pre_act = jnp.dot(normed_b, w_up, preferred_element_type=jnp.float32)
        act_val, gelu_pull = jax.vjp(gelu_tanh, pre_act)
        hidden_act = act_val.astype(jnp.bfloat16)
        part_two = jnp.dot(hidden_act, w_down, preferred_element_type=jnp.float32)
        sum_two = lax.psum(part_two.astype(jnp.bfloat16), "tp")
        y_rows = (x_one.astype(jnp.float32) + sum_two.astype(jnp.float32)).astype(jnp.bfloat16)

        grad_rows = grad_y.reshape(tokens, hidden)
        grad_down = matmul_tn(hidden_act, grad_rows)
        grad_hidden = matmul_nt(grad_rows, w_down).astype(jnp.bfloat16)
        grad_pre = gelu_pull(grad_hidden.astype(jnp.float32))[0].astype(jnp.bfloat16)
        grad_up = matmul_tn(normed_b, grad_pre)
        part_b = matmul_nt(grad_pre, w_up).astype(jnp.bfloat16)
        grad_norm_b = lax.psum(part_b, "tp")
        back_b, gain_grad_two = norm_backward(grad_norm_b, hat_b, inv_b, gain_two)
        grad_x_one = (grad_rows.astype(jnp.float32) + back_b).astype(jnp.bfloat16)
        grad_out_w = lax.dot_general(attn_rows, grad_x_one, (((0,), (0,)), ((), ())), preferred_element_type=jnp.float32)
        grad_attn = lax.dot_general(grad_x_one, w_out, (((1,), (2,)), ((), ())), preferred_element_type=jnp.float32).astype(jnp.bfloat16)
        grad_q, grad_k, grad_v = attention_backward(grad_attn.reshape(batch_loc, seq_len, heads_loc, head_dim), q_blk, k_blk, v_blk, attn_probs, score_scale)
        grad_qkv = jnp.stack([grad_q, grad_k, grad_v], axis=3).astype(jnp.bfloat16).reshape(tokens, 3 * heads_loc * head_dim)
        grad_wqkv = matmul_tn(normed_a, grad_qkv)
        part_a = matmul_nt(grad_qkv, w_qkv).astype(jnp.bfloat16)
        grad_norm_a = lax.psum(part_a, "tp")
        back_a, gain_grad_one = norm_backward(grad_norm_a, hat_a, inv_a, gain_one)
        grad_x = (grad_x_one.astype(jnp.float32) + back_a).astype(jnp.bfloat16)

        weight_grads = lax.psum(tuple(grad_mat.astype(jnp.bfloat16) for grad_mat in (grad_wqkv, grad_out_w, grad_up, grad_down)), "dp")
        gain_grads = lax.psum((gain_grad_one, gain_grad_two), "dp")
        return (
            y_rows.reshape(x_in.shape),
            grad_x.reshape(x_in.shape),
            gain_grads[0].astype(jnp.bfloat16),
            gain_grads[1].astype(jnp.bfloat16),
            weight_grads[0],
            weight_grads[1],
            weight_grads[2],
            weight_grads[3],
        )

    return jax.shard_map(
        local_step,
        mesh=mesh,
        in_specs=(batch_spec, seg_spec, P(None), P(None), P(None, "tp"), P("tp", None, None), P(None, "tp"), P("tp", None), batch_spec),
        out_specs=(batch_spec, batch_spec, P("pod"), P("pod"), P("pod", "tp"), P(("pod", "tp"), None, None), P("pod", "tp"), P(("pod", "tp"), None)),
        check_vma=False,
    )
```

profile of v0, /device:TPU:0, one launch (start us, length us, event | category | flops | bytes accessed | tf_op | source)
XLA Modules:
  0.0 777.0 jit_solution(16333146656590817499)
XLA Ops:
  18.2 8.5 %convolution_convert_fusion = bf16[2048,1536]{1,0:T(8,128)(2,1)} fusion(bf16[2048,1024]{1,0:T(8,128)(2,1)S(1)} %fusion.62, bf16[1024,1536]{1,0:T(8,128)(2,1)S(1)} %copy-done), kind=kOutput, calls=%fused_computation.83 | convolution fusion | flops 6445596672 | bytes 13631488 | tf_op jit(solution)/shard_map/dot_general | solution.py:70
  26.7 8.7 %copy.26 = bf16[2048,1536]{0,1:T(8,128)(2,1)} copy(bf16[2048,1536]{1,0:T(8,128)(2,1)} %convolution_convert_fusion) | data formatting | bytes 12582912 | tf_op jit(solution)/shard_map/convert_element_type | solution.py:70
  35.4 11.1 %reshape.151 = bf16[2,1024,8,3,64]{1,0,4,3,2:T(2,128)(2,1)} reshape(bf16[2048,1536]{0,1:T(8,128)(2,1)} %copy.26) | data formatting | bytes 12582912 | tf_op jit(solution)/shard_map/reshape | solution.py:71
  46.5 7.7 fusion.105
  56.8 31.0 %fusion.106 = (f32[2,8,1024]{2,1,0:T(8,128)S(1)}, f32[2,8,1024,1024]{2,3,1,0:T(8,128)}) fusion(pred[2,1024,1024]{1,2,0:T(8,128)(4,1)} %compare_and_fusion, bf16[2,1024,8,1,64]{1,0,4,3,2:T(2,128)(2,1)} %get-tuple-element.25, bf16[2,1024,8,1,64]{1,0,4,3,2:T(2,128)(2,1)} %get-tuple-element.24), kind=kOutput, calls=%fused_computation.130 | convolution fusion | flops 2214593536 | bytes 73465856 | tf_op jit(solution)/shard_map/sub | solution.py:41
  87.8 23.1 %convert_bitcast_fusion = bf16[2,8,8,8,1024]{4,3,2,1,0:T(8,128)(2,1)S(1)} fusion(bf16[2,1024,8,1,64]{1,0,4,3,2:T(2,128)(2,1)} %get-tuple-element.26, f32[2,8,1024,1024]{2,3,1,0:T(8,128)} %get-tuple-element.32, f32[2,8,1024]{2,1,0:T(8,128)S(1)} %get-tuple-element.31), kind=kOutput, calls=%fused_computation.105 | convolution fusion | flops 2182086656 | bytes 71368704 | tf_op jit(solution)/shard_map/bnqk,bknd->bqnd/dot_general | solution.py:42
  112.5 4.4 bitcast_convert_fusion
  117.0 35.4 %all-reduce.8.cloned.1.call-done = bf16[2048,1024]{1,0:T(8,128)(2,1)} async-done(((bf16[2048,1024]{1,0:T(8,128)(2,1)}), bf16[2048,1024]{1,0:T(8,128)(2,1)}) %all-reduce.8.cloned.1.call-update) | async-done | bytes 4194320 | tf_op jit(solution)/shard_map/psum | solution.py:78
  152.4 4.9 convert_reduce_fusion
  158.9 12.4 %fusion.102 = f32[2048,2048]{1,0:T(8,128)} fusion(bf16[1024,2048]{1,0:T(8,128)(2,1)S(1)} %copy-done.36, bf16[2048,1024]{1,0:T(8,128)(2,1)S(1)} %get-tuple-element.23, f32[1024]{0:T(1024)S(1)} %convert_element_type.153, f32[2048]{0:T(1024)S(1)} %add_rsqrt_fusion, f32[2048]{0:T(1024)S(1)} %broadcast_multiply_fusion.4), kind=kOutput, calls=%fused_computation.128 | convolution fusion | flops 8600420352 | bytes 25186304 | tf_op jit(solution)/shard_map/dot_general | solution.py:81
  171.4 22.7 %fusion.17 = bf16[2048,2048]{1,0:T(8,128)(2,1)} fusion(f32[2048,2048]{1,0:T(8,128)} %fusion.102, bf16[2048,1024]{1,0:T(8,128)(2,1)S(1)} %bitcast.124, bf16[2048,1024]{1,0:T(8,128)(2,1)} %param.16), kind=kOutput, calls=%fused_computation.20 | convolution fusion | flops 8682209280 | bytes 33554432 | tf_op jit(solution)/shard_map/dot_general | solution.py:32
  194.1 13.9 %convolution_convert_fusion.4 = bf16[2048,1024]{1,0:T(8,128)(2,1)} fusion(bf16[2048,2048]{1,0:T(8,128)(2,1)} %fusion.17, bf16[1024,2048]{1,0:T(8,128)(2,1)} %param.15), kind=kOutput, calls=%fused_computation.92 | convolution fusion | flops 8592031744 | bytes 16777216 | tf_op jit(solution)/shard_map/dot_general | solution.py:32
  208.0 16.5 %convolution_convert_fusion.5 = bf16[2048,1024]{1,0:T(8,128)(2,1)} fusion(bf16[2048,1024]{1,0:T(8,128)(2,1)} %param.16, f32[2048,2048]{1,0:T(8,128)} %fusion.102), kind=kOutput, calls=%fused_computation.93 | convolution fusion | flops 8629780480 | bytes 25165824 | tf_op jit(solution)/shard_map/dot_general | solution.py:84
  224.5 17.7 %all-reduce.10.cloned.1.call-done = bf16[2048,1024]{1,0:T(8,128)(2,1)} async-done(((bf16[2048,1024]{1,0:T(8,128)(2,1)}), bf16[2048,1024]{1,0:T(8,128)(2,1)}) %all-reduce.10.cloned.1.call-update) | async-done | bytes 4194320 | tf_op jit(solution)/shard_map/psum | solution.py:94
  242.3 6.5 fusion.46
  248.9 5.4 fusion.43
  254.3 3.7 fusion.70
  258.0 25.0 %fusion.73 = bf16[2,1024,8,1,64]{1,4,2,0,3:T(8,128)(2,1)} fusion(bf16[8,8,2,8,1024]{4,3,2,1,0:T(8,128)(2,1)} %bitcast.129, f32[2,8,1024,1024]{2,3,1,0:T(8,128)} %get-tuple-element.32, f32[2,8,1024]{2,1,0:T(8,128)S(1)} %get-tuple-element.31), kind=kOutput, calls=%fused_computation.96 | convolution fusion | flops 2181038080 | bytes 71368704 | tf_op jit(solution)/shard_map/bnqk,bqnd->bknd/dot_general | solution.py:47
  283.0 25.4 %fusion.83 = f32[2,8,1024,1024]{2,3,1,0:T(8,128)} fusion(bf16[2,1024,8,1,64]{1,0,4,3,2:T(2,128)(2,1)} %get-tuple-element.26, bf16[8,8,2,8,1024]{4,3,2,1,0:T(8,128)(2,1)} %bitcast.130), kind=kOutput, calls=%fused_computation.100 | convolution fusion | flops 2147483648 | bytes 71303168 | tf_op jit(solution)/shard_map/bqnd,bknd->bnqk/dot_general | solution.py:48
  308.4 83.0 %fusion.76 = bf16[2,1024,8,1,64]{1,4,2,0,3:T(8,128)(2,1)} fusion(f32[2,8,1024,1024]{2,3,1,0:T(8,128)} %fusion.83, bf16[2,1024,8,1,64]{1,0,4,3,2:T(2,128)(2,1)} %get-tuple-element.24, f32[2,8,1024,1024]{2,3,1,0:T(8,128)} %get-tuple-element.32, f32[2,8,1024]{2,1,0:T(8,128)S(1)} %get-tuple-element.31), kind=kOutput, calls=%fused_computation.97 | convolution fusion | flops 2264941568 | bytes 138477568 | tf_op jit(solution)/shard_map/bnqk,bknd->bqnd/dot_general | solution.py:51
  391.4 83.4 %fusion.79 = bf16[2,1024,8,1,64]{1,4,2,0,3:T(8,128)(2,1)} fusion(f32[2,8,1024,1024]{2,3,1,0:T(8,128)} %fusion.83, bf16[2,1024,8,1,64]{1,0,4,3,2:T(2,128)(2,1)} %get-tuple-element.25, f32[2,8,1024,1024]{2,3,1,0:T(8,128)} %get-tuple-element.32, f32[2,8,1024]{2,1,0:T(8,128)S(1)} %get-tuple-element.31), kind=kOutput, calls=%fused_computation.98 | convolution fusion | flops 2264941568 | bytes 138477568 | tf_op jit(solution)/shard_map/bnqk,bqnd->bknd/dot_general | solution.py:52
  478.3 15.0 %copy.37 = bf16[2,1024,8,3,64]{1,0,4,3,2:T(2,128)(2,1)S(1)} copy(bf16[2,1024,8,3,64]{1,4,2,0,3:T(8,128)(2,1)S(1)} %maximum_convert_fusion) | data formatting | bytes 12582912 | tf_op jit(solution)/shard_map/convert_element_type | solution.py:100
  498.5 8.6 %convolution_convert_fusion.2 = bf16[2048,1024]{1,0:T(8,128)(2,1)} fusion(bf16[2048,1536]{0,1:T(8,128)(2,1)S(1)} %bitcast.120, bf16[1024,1536]{1,0:T(8,128)(2,1)S(1)} %copy-done), kind=kOutput, calls=%fused_computation.90 | convolution fusion | flops 6444548096 | bytes 13631488 | tf_op jit(solution)/shard_map/dot_general | solution.py:32
  511.4 14.8 %convolution_convert_fusion.3 = bf16[1024,2048]{1,0:T(8,128)(2,1)} fusion(bf16[2048,2048]{1,0:T(8,128)(2,1)} %fusion.17, bf16[2048,1024]{1,0:T(8,128)(2,1)S(1)} %copy-done.5, f32[1024]{0:T(1024)S(1)} %copy-done.31, f32[2048]{0:T(1024)S(1)} %copy-done.27, f32[2048]{0:T(1024)S(1)} %copy-done.19), kind=kOutput, calls=%fused_computation.91 | convolution fusion | flops 8602517504 | bytes 16797696 | tf_op jit(solution)/shard_map/dot_general | solution.py:36
  526.3 16.4 %convolution_convert_fusion.6 = bf16[2048,1024]{1,0:T(8,128)(2,1)} fusion(bf16[2048,1024]{1,0:T(8,128)(2,1)S(1)} %bitcast.125, f32[2048,2048]{1,0:T(8,128)} %fusion.102), kind=kOutput, calls=%fused_computation.94 | convolution fusion | flops 8629780480 | bytes 25165824 | tf_op jit(solution)/shard_map/dot_general | solution.py:36
  542.7 5.0 fusion.90
  547.6 8.2 %convolution_convert_fusion.1 = bf16[1024,1536]{1,0:T(8,128)(2,1)} fusion(bf16[2048,1024]{1,0:T(8,128)(2,1)S(1)} %bitcast.128, bf16[2048,1536]{0,1:T(8,128)(2,1)S(1)} %bitcast.123), kind=kOutput, calls=%fused_computation.89 | convolution fusion | flops 6444023808 | bytes 13631488 | tf_op jit(solution)/shard_map/dot_general | solution.py:36
  556.6 5.8 fusion.52
  562.4 184.2 %all-reduce = (bf16[1024]{0:T(1024)(128)(2,1)}, bf16[1024]{0:T(1024)(128)(2,1)}) all-reduce(f32[1024]{0:T(1024)S(1)} %get-tuple-element.10, f32[1024]{0:T(1024)S(1)} %copy-done.34), channel_id=1, replica_groups=mesh['pod'=1,'dp'=64,'tp'=2] {'dp'}, use_global_device_ids=true, to_apply=%region_16.17 | all-reduce | flops 2048 | bytes 12288 | tf_op jit(solution)/shard_map/psum | solution.py:108
  746.6 7.8 %fusion.53 = bf16[2048,1024]{1,0:T(8,128)(2,1)} fusion(bf16[2048,1024]{1,0:T(8,128)(2,1)} %copy-done.3, bf16[2048,1024]{1,0:T(8,128)(2,1)} %get-tuple-element.20), kind=kLoop, calls=%fused_computation.65 | loop fusion | flops 8388608 | bytes 12582912 | tf_op jit(solution)/shard_map/convert_element_type | solution.py:86
  754.5 4.8 fusion.50
  759.3 3.9 copy.93
  (117 shorter events, 37.6 us)
Async XLA Ops:
  7.2 11.1 %copy-start = (bf16[1024,1536]{1,0:T(8,128)(2,1)S(1)}, bf16[1024,1536]{1,0:T(8,128)(2,1)}, u32[]{:S(2)}) copy-start(bf16[1024,1536]{1,0:T(8,128)(2,1)} %param.13) | copy-start | bytes 9437188
  7.2 145.2 %all-reduce.8.cloned.1.call-start = ((), (), s32[]{:S(2)}) async-start(), calls=%async_computation | async-start | bytes 8388608 | tf_op jit(solution)/shard_map/psum | solution.py:78
  7.2 9.6 %copy-start.1 = (bf16[2,1024,1024]{2,1,0:T(8,128)(2,1)S(1)}, bf16[2,1024,1024]{2,1,0:T(8,128)(2,1)}, u32[]{:S(2)}) copy-start(bf16[2,1024,1024]{2,1,0:T(8,128)(2,1)} %param.9) | copy-start | bytes 12582916
  9.7 8.5 %copy-start.24 = (f32[1024]{0:T(1024)}, f32[1024]{0:T(1024)S(1)}, u32[]{:S(2)}) copy-start(f32[1024]{0:T(1024)S(1)} %convert_element_type.143) | copy-start | bytes 12292
  46.5 7.7 copy-start.14
  46.5 7.7 copy-start.32
  87.8 24.6 %copy-start.37 = (bf16[8,64,1024]{2,1,0:T(8,128)(2,1)S(1)}, bf16[8,64,1024]{2,1,0:T(8,128)(2,1)}, u32[]{:S(2)}) copy-start(bf16[8,64,1024]{2,1,0:T(8,128)(2,1)} %param.14) | copy-start | bytes 3145732
  112.5 4.5 copy-start.35
  116.9 125.4 %all-reduce.10.cloned.1.call-start = ((), (), s32[]{:S(2)}) async-start(), calls=%async_computation.1 | async-start | bytes 8388608 | tf_op jit(solution)/shard_map/psum | solution.py:94
  117.0 131.9 %copy-start.30 = (f32[1024]{0:T(1024)}, f32[1024]{0:T(1024)S(1)}, u32[]{:S(2)}) copy-start(f32[1024]{0:T(1024)S(1)} %convert_element_type.153) | copy-start | bytes 12292
  152.4 6.6 copy-start.36
  157.2 14.1 %copy-start.3 = (bf16[2048,1024]{1,0:T(8,128)(2,1)}, bf16[2048,1024]{1,0:T(8,128)(2,1)S(1)}, u32[]{:S(2)}) copy-start(bf16[2048,1024]{1,0:T(8,128)(2,1)S(1)} %get-tuple-element.23) | copy-start | bytes 12582916
  157.3 91.6 %copy-start.18 = (f32[2048]{0:T(1024)}, f32[2048]{0:T(1024)S(1)}, u32[]{:S(2)}) copy-start(f32[2048]{0:T(1024)S(1)} %broadcast_multiply_fusion.4) | copy-start | bytes 24580
  158.9 89.9 %copy-start.26 = (f32[2048]{0:T(1024)}, f32[2048]{0:T(1024)S(1)}, u32[]{:S(2)}) copy-start(f32[2048]{0:T(1024)S(1)} %add_rsqrt_fusion) | copy-start | bytes 24580
  158.9 12.4 %copy-start.12 = (bf16[2,1024,1024]{2,1,0:T(8,128)(2,1)S(1)}, bf16[2,1024,1024]{2,1,0:T(8,128)(2,1)}, u32[]{:S(2)}) copy-start(bf16[2,1024,1024]{2,1,0:T(8,128)(2,1)} %param.17) | copy-start | bytes 12582916
  208.0 347.9 %all-reduce.14.cloned.1.call-start = ((), (), s32[]{:S(2)}) async-start(), calls=%async_computation.3 | async-start | bytes 16777216 | tf_op jit(solution)/shard_map/psum | solution.py:85
  242.3 6.6 copy-start.4
  242.3 6.6 copy-start.10
  248.9 5.4 copy-start.38
  507.1 4.3 copy-start.27
  507.1 4.3 copy-start.31
  507.1 252.1 %all-reduce.12.cloned.1.call-start = ((), (), s32[]{:S(2)}) async-start(), calls=%async_computation.2 | async-start | bytes 25165824 | tf_op jit(solution)/shard_map/psum | solution.py:107
  511.4 14.8 %copy-start.13 = (bf16[2,1024,1024]{2,1,0:T(8,128)(2,1)S(1)}, bf16[2,1024,1024]{2,1,0:T(8,128)(2,1)}, u32[]{:S(2)}) copy-start(bf16[2,1024,1024]{2,1,0:T(8,128)(2,1)} %param.17) | copy-start | bytes 12582916
  511.4 36.2 %slice-start = ((s8[6291456]{0:T(1024)(128)(4,1)}), s8[4194304]{0:T(1024)(128)(4,1)S(1)}, s32[]{:S(2)}) async-start(s8[6291456]{0:T(1024)(128)(4,1)} %bitcast.121), calls=%async_computation.4 | async-start | bytes 8388608
  526.2 16.4 %copy-start.7 = (bf16[2048,1024]{1,0:T(8,128)(2,1)S(1)}, bf16[2048,1024]{1,0:T(8,128)(2,1)}, u32[]{:S(2)}) copy-start(bf16[2048,1024]{1,0:T(8,128)(2,1)} %copy-done.6) | copy-start | bytes 12582916
  526.3 21.4 %slice-start.1 = ((s8[6291456]{0:T(1024)(128)(4,1)}), s8[2097152]{0:T(1024)(128)(4,1)S(1)}, s32[]{:S(2)}) async-start(s8[6291456]{0:T(1024)(128)(4,1)} %bitcast.121), calls=%async_computation.5 | async-start | bytes 4194304
  555.9 6.5 copy-start.34
  746.6 7.9 %copy-start.2 = (bf16[2,1024,1024]{2,1,0:T(8,128)(2,1)S(1)}, bf16[2,1024,1024]{2,1,0:T(8,128)(2,1)}, u32[]{:S(2)}) copy-start(bf16[2,1024,1024]{2,1,0:T(8,128)(2,1)} %param.9) | copy-start | bytes 12582916
  746.6 7.9 %copy-start.8 = (bf16[2048,1024]{1,0:T(8,128)(2,1)S(1)}, bf16[2048,1024]{1,0:T(8,128)(2,1)}, u32[]{:S(2)}) copy-start(bf16[2048,1024]{1,0:T(8,128)(2,1)} %copy-done.6) | copy-start | bytes 12582916
  746.6 7.9 %copy-start.9 = (bf16[2048,1024]{1,0:T(8,128)(2,1)S(1)}, bf16[2048,1024]{1,0:T(8,128)(2,1)}, u32[]{:S(2)}) copy-start(bf16[2048,1024]{1,0:T(8,128)(2,1)} %get-tuple-element.21) | copy-start | bytes 12582916
  759.2 6.8 copy-start.16
  759.2 8.8 %copy-start.15 = (bf16[2048,1024]{1,0:T(8,128)(2,1)S(1)}, bf16[2048,1024]{1,0:T(8,128)(2,1)}, u32[]{:S(2)}) copy-start(bf16[2048,1024]{1,0:T(8,128)(2,1)} %get-tuple-element.42) | copy-start | bytes 12582916
  (13 other events, 24.5 us)
Sparse Core Ops, SparseCore 0:
  117.0 35.3 all-reduce.7
  208.1 34.1 all-reduce.9
  507.3 43.4 all-reduce.13
  557.2 189.8 all-reduce.11
where the time goes:
time: 783 us; the launch traced here: 777 us
  matrix products  406 us (52%)
  blocking collectives  184 us (23%)
  local copies, waits for them, and re-layouts  62 us (8%)
  other arithmetic  56.9 us (7%)
  waiting for transfers between devices  53.2 us (7%)
  between operations  14.6 us (2%)
    psum x1, blocking collectives, local_step(): gain_grads = lax.psum((gain_grad_one, gain_grad_two), 'dp')  184 us
    dot_general x1, matrix products, attention_backward(): jnp.einsum('bnqk,bqnd->bknd', grad_low, q_blk, preferred_element_type=jnp...  83.4 us
    dot_general x1, matrix products, attention_backward(): jnp.einsum('bnqk,bknd->bqnd', grad_low, k_blk, preferred_element_type=jnp...  83 us
    dot_general x3, matrix products, matmul_nt(): lax.dot_general(lhs, rhs, (((1,), (1,)), ((), ())), preferred_element_typ...  45.1 us
    dot_general x3, matrix products, matmul_tn(): lax.dot_general(lhs, rhs, (((0,), (0,)), ((), ())), preferred_element_typ...  39.4 us
    psum x1, waiting for transfers between devices, local_step(): sum_one = lax.psum(part_one.astype(jnp.bfloat16), 'tp')  35.4 us
    sub x1, matrix products, attention_forward(): attn_probs = jax.nn.softmax(jnp.where(allowed, scores, NEG_LARGE), axis=-1)  31 us
    dot_general x1, matrix products, attention_backward(): jnp.einsum('bqnd,bknd->bnqk', grad_out, v_blk, preferred_element_type=jnp...  25.4 us
  transfers between devices with their start and end apart: 4, of which 2 were waited for; matrix products, arithmetic and copies ran while one was open for 11% of the time, Pallas kernels for 0%

commit v1 on v0

v1 whole, which is shorter than its diff:
```python
import functools
import math

import jax
import jax.numpy as jnp
from jax import lax
from jax.experimental import pallas as pl
from jax.experimental.pallas import tpu as pltpu
from jax.sharding import PartitionSpec as P

EPS_NORM = 1e-5
NEG_LARGE = -1e30
LOG2E = math.log2(math.e)
SWAP = [(0, 1), (1, 0)]
TILE = 256
BF16 = jnp.bfloat16
F32 = jnp.float32


def norm_stats(x_rows):
    x_f32 = x_rows.astype(F32)
    mean = jnp.mean(x_f32, axis=-1, keepdims=True)
    centered = x_f32 - mean
    inv_std = lax.rsqrt(jnp.mean(centered * centered, axis=-1, keepdims=True) + EPS_NORM)
    return mean, inv_std


def norm_apply(x_rows, mean, inv_std, gain_vec):
    return ((x_rows.astype(F32) - mean) * inv_std * gain_vec.astype(F32)).astype(BF16)


def norm_backward(grad_out, x_rows, mean, inv_std, gain_vec):
    grad_f32 = grad_out.astype(F32)
    x_hat = (x_rows.astype(F32) - mean) * inv_std
    grad_gain = jnp.sum(grad_f32 * x_hat, axis=0)
    grad_hat = grad_f32 * gain_vec.astype(F32)
    mean_one = jnp.mean(grad_hat, axis=-1, keepdims=True)
    mean_two = jnp.mean(grad_hat * x_hat, axis=-1, keepdims=True)
    return inv_std * (grad_hat - mean_one - x_hat * mean_two), grad_gain


def dot_nn(lhs, rhs):
    return lax.dot_general(lhs, rhs, (((1,), (0,)), ((), ())), preferred_element_type=F32)


def dot_nt(lhs, rhs):
    return lax.dot_general(lhs, rhs, (((1,), (1,)), ((), ())), preferred_element_type=F32)


def dot_tn(lhs, rhs):
    return lax.dot_general(lhs, rhs, (((0,), (0,)), ((), ())), preferred_element_type=F32)


def attn_fwd_kernel(dim, scale, start_ref, qkv_ref, out_ref, lse_ref):
    seq = qkv_ref.shape[0]
    block = qkv_ref[...]
    block_t = block.T
    start = start_ref[0:1, :]
    heads_t = []
    for head in range(2):
        base = 3 * dim * head
        k_rows = block[:, base + dim : base + 2 * dim]
        q_cols = block_t[base : base + dim]
        v_cols = block_t[base + 2 * dim : base + 3 * dim]
        strips = []
        for i in range(seq // TILE):
            lo, hi = i * TILE, (i + 1) * TILE
            scores = dot_nn(k_rows[:hi], q_cols[:, lo:hi]) * (scale * LOG2E)
            k_pos = lax.broadcasted_iota(jnp.int32, (hi, TILE), 0)
            allowed = k_pos >= start[:, lo:hi]
            q_pos = lax.broadcasted_iota(jnp.int32, (TILE, TILE), 1) + lo
            diag = jnp.where(allowed[lo:] & (k_pos[lo:] <= q_pos), scores[lo:], NEG_LARGE)
            if lo:
                body = jnp.where(allowed[:lo], scores[:lo], NEG_LARGE)
                scores = jnp.concatenate([body, diag], axis=0)
            else:
                scores = diag
            top = jnp.max(scores, axis=0, keepdims=True)
            probs = jnp.exp2(scores - top)
            total = jnp.sum(probs, axis=0, keepdims=True)
            probs = (probs * (1.0 / total)).astype(BF16)
            strips.append(dot_nn(v_cols[:, :hi], probs))
            lse_ref[0, head : head + 1, lo:hi] = top + jnp.log2(total)
        heads_t.append(jnp.concatenate(strips, axis=1))
    out_ref[...] = jnp.concatenate(heads_t, axis=0).T.astype(BF16)


def attn_bwd_kernel(dim, scale, start_ref, qkv_ref, out_ref, grad_ref, lse_ref, dqkv_ref):
    seq = qkv_ref.shape[0]
    block = qkv_ref[...]
    block_t = block.T
    grad = grad_ref[...]
    grad_t = grad.T
    prod_t = grad_t.astype(F32) * out_ref[...].T.astype(F32)
    start = start_ref[0:1, :]
    pieces = []
    for head in range(2):
        base = 3 * dim * head
        q_rows = block[:, base : base + dim]
        k_rows = block[:, base + dim : base + 2 * dim]
        v_rows = block[:, base + 2 * dim : base + 3 * dim]
        q_cols = block_t[base : base + dim]
        k_cols = block_t[base + dim : base + 2 * dim]
        do_rows = grad[:, head * dim : (head + 1) * dim]
        do_cols = grad_t[head * dim : (head + 1) * dim]
        delta = jnp.sum(prod_t[head * dim : (head + 1) * dim], axis=0, keepdims=True)
        lse = lse_ref[0, head : head + 1, :]
        dq_cols = None
        dk_parts, dv_parts = [], []
        for j in range(seq // TILE):
            lo, hi = j * TILE, (j + 1) * TILE
            width = seq - lo
            scores = dot_nn(k_rows[lo:hi], q_cols[:, lo:]) * (scale * LOG2E)
            grad_probs = dot_nn(v_rows[lo:hi], do_cols[:, lo:])
            k_pos = lax.broadcasted_iota(jnp.int32, (TILE, width), 0) + lo
            allowed = k_pos >= start[:, lo:]
            q_pos = lax.broadcasted_iota(jnp.int32, (TILE, TILE), 1) + lo
            probs = jnp.exp2(scores - lse[:, lo:])
            diag = jnp.where(allowed[:, :TILE] & (k_pos[:, :TILE] <= q_pos), probs[:, :TILE], 0.0)
            if width > TILE:
                body = jnp.where(allowed[:, TILE:], probs[:, TILE:], 0.0)
                probs = jnp.concatenate([diag, body], axis=1)
            else:
                probs = diag
            grad_scores = (probs * (grad_probs - delta[:, lo:]) * scale).astype(BF16)
            dv_parts.append(dot_nn(probs.astype(BF16), do_rows[lo:]))
            dk_parts.append(dot_nn(grad_scores, q_rows[lo:]))
            dq_part = dot_nn(k_cols[:, lo:hi], grad_scores)
            if dq_cols is None:
                dq_cols = dq_part
            else:
                dq_cols = jnp.concatenate([dq_cols[:, :lo], dq_cols[:, lo:] + dq_part], axis=1)
        pieces.append(dq_cols.T)
        pieces.append(jnp.concatenate(dk_parts, axis=0))
        pieces.append(jnp.concatenate(dv_parts, axis=0))
    dqkv_ref[...] = jnp.concatenate(pieces, axis=1).astype(BF16)


def attn_specs(seq, dim, width):
    pairs = width // (6 * dim)
    start_spec = pl.BlockSpec((8, seq), lambda i: (0, 0))
    qkv_spec = pl.BlockSpec((seq, 6 * dim), lambda i: (0, i))
    out_spec = pl.BlockSpec((seq, 2 * dim), lambda i: (0, i))
    lse_spec = pl.BlockSpec((1, 8, seq), lambda i: (i, 0, 0))
    return pairs, start_spec, qkv_spec, out_spec, lse_spec


VMEM_LIMIT = 56 * 1024 * 1024


def attention_forward(start, qkv, dim, scale):
    seq, width = qkv.shape
    pairs, start_spec, qkv_spec, out_spec, lse_spec = attn_specs(seq, dim, width)
    return pl.pallas_call(
        functools.partial(attn_fwd_kernel, dim, scale),
        grid=(pairs,),
        in_specs=[start_spec, qkv_spec],
        out_specs=[out_spec, lse_spec],
        out_shape=[
            jax.ShapeDtypeStruct((seq, pairs * 2 * dim), BF16),
            jax.ShapeDtypeStruct((pairs, 8, seq), F32),
        ],
        compiler_params=pltpu.CompilerParams(vmem_limit_bytes=VMEM_LIMIT),
        cost_estimate=pl.CostEstimate(flops=pairs * 8 * seq * seq * dim, bytes_accessed=8 * seq * width // 3, transcendentals=pairs * seq * seq),
        name="attn_fwd",
    )(start, qkv)


def attention_backward(start, qkv, out, grad, lse, dim, scale):
    seq, width = qkv.shape
    pairs, start_spec, qkv_spec, out_spec, lse_spec = attn_specs(seq, dim, width)
    return pl.pallas_call(
        functools.partial(attn_bwd_kernel, dim, scale),
        grid=(pairs,),
        in_specs=[start_spec, qkv_spec, out_spec, out_spec, lse_spec],
        out_specs=qkv_spec,
        out_shape=jax.ShapeDtypeStruct((seq, width), BF16),
        compiler_params=pltpu.CompilerParams(vmem_limit_bytes=VMEM_LIMIT),
        cost_estimate=pl.CostEstimate(flops=pairs * 20 * seq * seq * dim, bytes_accessed=16 * seq * width // 3, transcendentals=pairs * seq * seq),
        name="attn_bwd",
    )(start, qkv, out, grad, lse)


GELU_A = math.sqrt(2.0 / math.pi)
GELU_B = 0.044715


def mlp_mid_kernel(rows, b_ref, dy_ref, up_ref, down_ref, act_ref, dpre_ref):
    for r in range(b_ref.shape[0] // rows):
        span = pl.ds(r * rows, rows)
        pre = dot_nn(b_ref[span, :], up_ref[...])
        grad_h = dot_nt(dy_ref[span, :], down_ref[...]).astype(BF16).astype(F32)
        square = pre * pre
        tanh = jnp.tanh(pre * (GELU_A + (GELU_A * GELU_B) * square))
        cdf = 0.5 + 0.5 * tanh
        act_ref[span, :] = (pre * cdf).astype(BF16)
        slope = cdf + (0.5 * pre) * (1.0 - tanh * tanh) * (GELU_A + (3.0 * GELU_A * GELU_B) * square)
        dpre_ref[span, :] = (grad_h * slope).astype(BF16)


def mlp_mid(normed, grad_rows, w_up, w_down, tile_n=512, rows=256):
    tokens, hidden = normed.shape
    ffn = w_up.shape[1]
    return pl.pallas_call(
        functools.partial(mlp_mid_kernel, rows),
        grid=(ffn // tile_n,),
        in_specs=[
            pl.BlockSpec((tokens, hidden), lambda i: (0, 0)),
            pl.BlockSpec((tokens, hidden), lambda i: (0, 0)),
            pl.BlockSpec((hidden, tile_n), lambda i: (0, i)),
            pl.BlockSpec((tile_n, hidden), lambda i: (i, 0)),
        ],
        out_specs=[pl.BlockSpec((tokens, tile_n), lambda i: (0, i))] * 2,
        out_shape=[jax.ShapeDtypeStruct((tokens, ffn), BF16)] * 2,
        compiler_params=pltpu.CompilerParams(vmem_limit_bytes=VMEM_LIMIT),
        cost_estimate=pl.CostEstimate(flops=4 * tokens * hidden * ffn, bytes_accessed=2 * tokens * (2 * hidden + 2 * ffn) + 4 * hidden * ffn, transcendentals=tokens * ffn),
        name="mlp_mid",
    )(normed, grad_rows, w_up, w_down)


MESH_ID = pl.DeviceIdType.MESH
RING = 4
FLOW_ROWS = 1024
FLOW_COLS = 1024
STREAMS = 2
STREAM_COLS = FLOW_COLS // STREAMS
LEVEL_ROWS = (256, 64, 16)
LEVEL_SLOT = (0, 768, 960)
SLOT_ROWS = 1008
AXIS_STRIDE = (1, 4, 16)
FLOWS = tuple((tuple((first + k) % 3 for k in range(3)), sign) for first in range(3) for sign in (1, -1))
STEPS = 6 * (RING - 1)


def hbm_block(refs, flow, stream, row, rows):
    down, up, qkv, out = refs
    lane = stream * STREAM_COLS
    if flow < 2:
        return down.at[pl.ds(flow * FLOW_ROWS + row, rows), pl.ds(lane, STREAM_COLS)]
    if flow < 4:
        return up.at[pl.ds(row, rows), pl.ds((flow - 2) * FLOW_COLS + lane, STREAM_COLS)]
    if flow == 4:
        return qkv.at[pl.ds(row, rows), pl.ds(lane, STREAM_COLS)]
    if stream == 0:
        return qkv.at[pl.ds(row, rows), pl.ds(FLOW_COLS, STREAM_COLS)]
    half = row // 512
    return out.at[pl.ds(pl.multiple_of(row - half * 512, 256), rows), pl.ds(pl.multiple_of(half * STREAM_COLS, STREAM_COLS), STREAM_COLS)]


def all_reduce_kernel(*refs):
    ins, outs = refs[:4], refs[4:8]
    own, slots, full, send_sem, recv_sem, load_sem, store_sem = refs[8:]
    me = lax.axis_index("dp")
    coords = (lax.rem(me, 4), lax.rem(me // 4, 4), me // 16)

    def neighbour(axis, sign):
        moved = lax.rem(coords[axis] + sign + RING, RING)
        return me + (moved - coords[axis]) * AXIS_STRIDE[axis]

    barrier = pltpu.get_barrier_semaphore()
    for axis in range(3):
        for sign in (1, -1):
            pl.semaphore_signal(barrier, inc=1, device_id={"dp": neighbour(axis, sign)}, device_id_type=MESH_ID)

    place, bases = [], []
    for axes, sign in FLOWS:
        spots = [coords[a] if sign > 0 else lax.rem(RING - coords[a], RING) for a in axes]
        base = [0]
        for level in range(2):
            base.append(base[-1] + lax.rem(spots[level] + 1, RING) * LEVEL_ROWS[level])
        place.append(spots)
        bases.append(base)

    def chunk(flow, level, shift):
        index = lax.rem(place[flow][level] + shift + RING, RING)
        return pl.multiple_of(bases[flow][level] + index * LEVEL_ROWS[level], LEVEL_ROWS[level])

    def view(ref, flow, stream, row, rows):
        return ref.at[flow, pl.ds(row, rows), pl.ds(stream * STREAM_COLS, STREAM_COLS)]

    def load(flow, stream, turn):
        row = chunk(flow, 0, -turn)
        return pltpu.make_async_copy(
            hbm_block(ins, flow, stream, row, LEVEL_ROWS[0]), view(own, flow, stream, row, LEVEL_ROWS[0]), load_sem.at[flow, stream, turn])

    def store(flow, stream, turn):
        row = chunk(flow, 0, 1 - turn)
        return pltpu.make_async_copy(
            view(full, flow, stream, row, LEVEL_ROWS[0]), hbm_block(outs, flow, stream, row, LEVEL_ROWS[0]), store_sem.at[flow, stream, turn])

    def where(step):
        if step < 9:
            return step // 3, step % 3, False
        return 2 - (step - 9) // 3, step % 3, True

    def copy(flow, stream, step):
        level, turn, gathering = where(step)
        rows = LEVEL_ROWS[level]
        axes, sign = FLOWS[flow]
        if gathering:
            source = view(full, flow, stream, chunk(flow, level, 1 - turn), rows)
            target = source
        else:
            source = view(own, flow, stream, chunk(flow, level, -turn), rows)
            target = view(slots, flow, stream, LEVEL_SLOT[level] + turn * rows, rows)
        return pltpu.make_async_remote_copy(
            src_ref=source, dst_ref=target, send_sem=send_sem.at[flow, stream, step], recv_sem=recv_sem.at[flow, stream, step],
            device_id={"dp": neighbour(axes[level], sign)}, device_id_type=MESH_ID)

    def absorb(flow, stream, step):
        level, turn, gathering = where(step)
        copy(flow, stream, step).wait_recv()
        lanes = pl.ds(stream * STREAM_COLS, STREAM_COLS)
        if gathering:
            if level == 1 and turn == 2:
                store(flow, stream, 0).start()
            if level == 0:
                store(flow, stream, turn + 1).start()
            return
        if level == 0:
            load(flow, stream, turn + 1).wait()
        rows = LEVEL_ROWS[level]
        row = chunk(flow, level, -turn - 1)
        last = step == 8
        part = min(rows, 64)

        def add(i, carry):
            at = pl.ds(pl.multiple_of(row + i * part, 16), part)
            got = slots[flow, pl.ds(pl.multiple_of(LEVEL_SLOT[level] + turn * rows + i * part, 16), part), lanes]
            total = (own[flow, at, lanes].astype(F32) + got.astype(F32)).astype(BF16)
            if last:
                full[flow, at, lanes] = total
            else:
                own[flow, at, lanes] = total
            return carry

        if rows == part:
            add(0, 0)
        else:
            lax.fori_loop(0, rows // part, add, 0)

    for turn in range(4):
        for stream in range(STREAMS):
            for flow in range(6):
                load(flow, stream, turn).start()
    pl.semaphore_wait(barrier, 6)
    for step in range(STEPS + 1):
        for stream in range(STREAMS):
            for flow in range(6):
                if step == 0:
                    load(flow, stream, 0).wait()
                else:
                    absorb(flow, stream, step - 1)
            if step < STEPS:
                for flow in range(6):
                    copy(flow, stream, step).start()
    for stream in range(STREAMS):
        for flow in range(6):
            for step in range(STEPS):
                copy(flow, stream, step).wait_send()
            for turn in range(4):
                store(flow, stream, turn).wait()


def all_reduce_dp(arrays):
    any_spec = pl.BlockSpec(memory_space=pl.ANY)
    flow_shape = (6, FLOW_ROWS, FLOW_COLS)
    return pl.pallas_call(
        all_reduce_kernel,
        in_specs=[any_spec] * 4,
        out_specs=[any_spec] * 4,
        out_shape=[jax.ShapeDtypeStruct(a.shape, a.dtype) for a in arrays],
        scratch_shapes=[
            pltpu.VMEM(flow_shape, BF16),
            pltpu.VMEM((6, SLOT_ROWS, FLOW_COLS), BF16),
            pltpu.VMEM(flow_shape, BF16),
            pltpu.SemaphoreType.DMA((6, STREAMS, STEPS)),
            pltpu.SemaphoreType.DMA((6, STREAMS, STEPS)),
            pltpu.SemaphoreType.DMA((6, STREAMS, 4)),
            pltpu.SemaphoreType.DMA((6, STREAMS, 4)),
        ],
        compiler_params=pltpu.CompilerParams(collective_id=0, has_side_effects=True, vmem_limit_bytes=VMEM_LIMIT),
        name="all_reduce_dp",
    )(*arrays)


def solution(mesh):
    batch_spec = P(("pod", "dp"), None, None)
    seg_spec = P(("pod", "dp"), None)

    def local_step(x_in, seg_ids, gain_one, gain_two, w_qkv, w_out, w_up, w_down, grad_y):
        heads_loc, dim, hidden = w_out.shape
        scale = dim ** -0.5
        swap = lambda value: lax.ppermute(value, "tp", SWAP)
        mine = lax.axis_index("tp")
        own_row = lambda value: lax.dynamic_index_in_dim(value, mine, 0, keepdims=False)

        w_out = w_out.reshape(heads_loc * dim, hidden)
        wqkv_p = swap(w_qkv)
        wout_p = swap(w_out)
        wup_p = swap(w_up)
        wdown_p = swap(w_down)
        x_rows = own_row(x_in)
        grad_rows = own_row(grad_y)
        seg = own_row(seg_ids)
        seq = x_rows.shape[0]
        start = jnp.sum((seg[None, :] < seg[:, None]).astype(jnp.int32), axis=1)
        start = jnp.broadcast_to(start[None, :], (8, seq))

        mean_a, inv_a = norm_stats(x_rows)
        normed_a = norm_apply(x_rows, mean_a, inv_a, gain_one)
        qkv_o = dot_nn(normed_a, w_qkv).astype(BF16)
        attn_o, lse_o = attention_forward(start, qkv_o, dim, scale)
        qkv_p = dot_nn(normed_a, wqkv_p).astype(BF16)
        attn_p, lse_p = attention_forward(start, qkv_p, dim, scale)
        part_one = (dot_nn(attn_o, w_out) + dot_nn(attn_p, wout_p)).astype(BF16)
        x_one = (x_rows.astype(F32) + part_one.astype(F32)).astype(BF16)
        mean_b, inv_b = norm_stats(x_one)
        normed_b = norm_apply(x_one, mean_b, inv_b, gain_two)

        act_p, dpre_p = mlp_mid(normed_b, grad_rows, wup_p, wdown_p)
        act_o, dpre_o = mlp_mid(normed_b, grad_rows, w_up, w_down)
        sent_down = swap(dot_tn(act_p, grad_rows).astype(BF16))
        sent_up = swap(dot_tn(normed_b, dpre_p).astype(BF16))
        grad_down = (dot_tn(act_o, grad_rows) + sent_down.astype(F32)).astype(BF16)
        grad_up = (dot_tn(normed_b, dpre_o) + sent_up.astype(F32)).astype(BF16)

        grad_norm_b = (dot_nt(dpre_o, w_up) + dot_nt(dpre_p, wup_p)).astype(BF16)
        back_b, gain_grad_two = norm_backward(grad_norm_b, x_one, mean_b, inv_b, gain_two)
        grad_x_one = (grad_rows.astype(F32) + back_b).astype(BF16)
        dattn_o = dot_nt(grad_x_one, w_out).astype(BF16)
        dattn_p = dot_nt(grad_x_one, wout_p).astype(BF16)
        sent_out = swap(dot_tn(attn_p, grad_x_one).astype(BF16))
        grad_out_w = (dot_tn(attn_o, grad_x_one) + sent_out.astype(F32)).astype(BF16)
        dqkv_p = attention_backward(start, qkv_p, attn_p, dattn_p, lse_p, dim, scale)
        dqkv_o = attention_backward(start, qkv_o, attn_o, dattn_o, lse_o, dim, scale)
        sent_qkv = swap(dot_tn(normed_a, dqkv_p).astype(BF16))
        grad_wqkv = (dot_tn(normed_a, dqkv_o) + sent_qkv.astype(F32)).astype(BF16)

        part_two = (dot_nn(act_o, w_down) + dot_nn(act_p, wdown_p)).astype(BF16)
        y_rows = (x_one.astype(F32) + part_two.astype(F32)).astype(BF16)
        grad_norm_a = (dot_nt(dqkv_o, w_qkv) + dot_nt(dqkv_p, wqkv_p)).astype(BF16)
        back_a, gain_grad_one = norm_backward(grad_norm_a, x_rows, mean_a, inv_a, gain_one)
        grad_x = (grad_x_one.astype(F32) + back_a).astype(BF16)

        def both_rows(value):
            other = swap(value)
            first = mine == 0
            return jnp.stack([jnp.where(first, value, other), jnp.where(first, other, value)])

        sum_down, sum_up, sum_qkv, sum_out = all_reduce_dp((grad_down, grad_up, grad_wqkv, grad_out_w))
        weight_grads = (sum_qkv, sum_out, sum_up, sum_down)
        gain_grads = lax.psum((gain_grad_one, gain_grad_two), ("dp", "tp"))
        return (
            both_rows(y_rows),
            both_rows(grad_x),
            gain_grads[0].astype(BF16),
            gain_grads[1].astype(BF16),
            weight_grads[0],
            weight_grads[1].reshape(heads_loc, dim, hidden),
            weight_grads[2],
            weight_grads[3],
        )

    return jax.shard_map(
        local_step,
        mesh=mesh,
        in_specs=(batch_spec, seg_spec, P(None), P(None), P(None, "tp"), P("tp", None, None), P(None, "tp"), P("tp", None), batch_spec),
        out_specs=(batch_spec, batch_spec, P("pod"), P("pod"), P("pod", "tp"), P(("pod", "tp"), None, None), P("pod", "tp"), P(("pod", "tp"), None)),
        check_vma=False,
    )
```

time: 783 us -> 485 us (0.62)
  matrix products: 406 us -> 122 us
  Pallas kernels: 0 us -> 230 us
  blocking collectives: 184 us -> 69 us
  waiting for transfers between devices: 53.2 us -> 0.03 us
  local copies, waits for them, and re-layouts: 62 us -> 14.2 us
  other arithmetic: 56.9 us -> 37.7 us
  between operations: 14.6 us -> 1.16 us
    dot_general x17 -> x20, matrix products: 375 us -> 122 us  [the longest x8 49.1 us: dot_tn(): lax.dot_general(lhs, rhs, (((0,), (0,)), ((), ())), preferred_element_typ...]
    pallas_call x0 -> x7, Pallas kernels: none -> 230 us  [the longest x1 117 us: all_reduce_dp(): pl.pallas_call(all_reduce_kernel, in_specs=[any_spec] * 4, out_specs=[any...]
    psum x1, blocking collectives: 184 us -> 69 us  [local_step(): gain_grads = lax.psum((gain_grad_one, gain_grad_two), ('dp', 'tp'))]
    psum x4 -> x0, waiting for transfers between devices: 53.1 us -> none  [the longest x1 35.4 us: local_step(): sum_one = lax.psum(part_one.astype(jnp.bfloat16), 'tp')]
    sub x1 -> x0, matrix products: 31 us -> none  [attention_forward(): attn_probs = jax.nn.softmax(jnp.where(allowed, scores, NEG_LARGE), axis=-1)]
    convert_element_type x2 -> x0, local copies, waits for them, and re-layouts: 23.6 us -> none  [the longest x1 15 us: local_step(): jnp.stack([grad_q, grad_k, grad_v], axis=3).astype(jnp.bfloat16)]
    reduce_sum x6 -> x4, other arithmetic: 24.7 us -> 5.62 us  [the longest x2 2.98 us: norm_stats(): jnp.mean(centered * centered, axis=-1, keepdims=True) + EPS_NORM]
    reshape x2 -> x0, local copies, waits for them, and re-layouts: 11.3 us -> none  [the longest x1 11.1 us: local_step(): qkv_rows = qkv_rows.reshape(batch_loc, seq_len, heads_loc, 3, head_dim)]
  transfers between devices with their start and end apart: 4 -> 10, of which waited for: 2 -> 0; matrix products, arithmetic and copies ran while one was open for 11% -> 26% of each run, Pallas kernels for 0% -> 20%
where the time goes in v1:
time: 485 us; the launch traced here: 476 us
  Pallas kernels  230 us (47%)
  matrix products  122 us (25%)
  blocking collectives  69 us (14%)
  other arithmetic  37.7 us (8%)
  local copies, waits for them, and re-layouts  14.2 us (3%)
    pallas_call x1, Pallas kernels, all_reduce_dp(): pl.pallas_call(all_reduce_kernel, in_specs=[any_spec] * 4, out_specs=[any...  117 us
    psum x1, blocking collectives, local_step(): gain_grads = lax.psum((gain_grad_one, gain_grad_two), ('dp', 'tp'))  69 us
    dot_general x8, matrix products, dot_tn(): lax.dot_general(lhs, rhs, (((0,), (0,)), ((), ())), preferred_element_typ...  49.1 us
    pallas_call x2, Pallas kernels, attention_forward(): pl.pallas_call(functools.partial(attn_fwd_kernel, dim, scale), grid=(pair...  42.2 us
    dot_general x6, matrix products, dot_nn(): lax.dot_general(lhs, rhs, (((1,), (0,)), ((), ())), preferred_element_typ...  38.2 us
    pallas_call x2, Pallas kernels, attention_backward(): pl.pallas_call(functools.partial(attn_bwd_kernel, dim, scale), grid=(pair...  37.3 us
    dot_general x6, matrix products, dot_nt(): lax.dot_general(lhs, rhs, (((1,), (1,)), ((), ())), preferred_element_typ...  34.7 us
    pallas_call x2, Pallas kernels, mlp_mid(): pl.pallas_call(functools.partial(mlp_mid_kernel, rows), grid=(ffn // tile...  32.8 us
  transfers between devices with their start and end apart: 10, of which 0 were waited for; matrix products, arithmetic and copies ran while one was open for 26% of the time, Pallas kernels for 20%

profile of v1, /device:TPU:0, one launch (start us, length us, event | category | flops | bytes accessed | tf_op | source)
XLA Modules:
  0.0 476.5 jit_solution(4401471112661276558)
XLA Ops:
  7.4 7.1 %convolution_convert_fusion.2.qkv_ref = bf16[1024,1536]{1,0:T(8,128)(2,1)} fusion(bf16[1024,1536]{1,0:T(8,128)(2,1)} %param.13, f32[1024]{0:T(1024)S(1)} %convert_element_type.131, f32[1024]{0:T(1024)S(1)} %add_rsqrt_fusion.1, f32[1024]{0:T(1024)S(1)} %broadcast_multiply_fusion.5, bf16[2,1024,1024]{2,1,0:T(8,128)(2,1)S(1)} %copy-done.2, s32[]{:T(128)S(6)} %select_n.28), kind=kOutput, calls=%fused_computation.55 | convolution fusion | flops 3228041216 | bytes 8400900 | tf_op jit(solution)/shard_map/dot_general | solution.py:43
  15.1 20.9 %attn_fwd.2 = (bf16[1024,512]{1,0:T(8,128)(2,1)}, f32[4,8,1024]{2,1,0:T(8,128)}) custom-call(s32[8,1024]{1,0:T(8,128)} %broadcast_in_dim.2.start_ref, bf16[1024,1536]{1,0:T(8,128)(2,1)} %convolution_convert_fusion.2.qkv_ref), custom_call_target="tpu_custom_call" | custom-call | flops 2147483648 | bytes 4194304 | tf_op jit(solution)/shard_map/attn_fwd/pallas_call | solution.py:154
  36.0 4.6 fusion.41
  42.2 7.8 %convolution_convert_fusion.1.qkv_ref = bf16[1024,1536]{1,0:T(8,128)(2,1)} fusion(bf16[1024,1536]{1,0:T(8,128)(2,1)} %collective-permute-done, f32[1024]{0:T(1024)S(1)} %convert_element_type.131, f32[1024]{0:T(1024)S(1)} %add_rsqrt_fusion.1, f32[1024]{0:T(1024)S(1)} %broadcast_multiply_fusion.5, bf16[2,1024,1024]{2,1,0:T(8,128)(2,1)} %param.9, s32[]{:T(128)S(6)} %select_n.28), kind=kOutput, calls=%fused_computation.54 | convolution fusion | flops 3228041216 | bytes 8400900 | tf_op jit(solution)/shard_map/dot_general | solution.py:43
  50.0 21.3 %attn_fwd.3 = (bf16[1024,512]{1,0:T(8,128)(2,1)}, f32[4,8,1024]{2,1,0:T(8,128)}) custom-call(s32[8,1024]{1,0:T(8,128)} %broadcast_in_dim.2.start_ref, bf16[1024,1536]{1,0:T(8,128)(2,1)} %convolution_convert_fusion.1.qkv_ref), custom_call_target="tpu_custom_call" | custom-call | flops 2147483648 | bytes 4194304 | tf_op jit(solution)/shard_map/attn_fwd/pallas_call | solution.py:154
  71.3 4.4 convert_reduce_fusion
  78.4 16.5 %mlp_mid.2 = (bf16[1024,2048]{1,0:T(8,128)(2,1)}, bf16[1024,2048]{1,0:T(8,128)(2,1)}) custom-call(bf16[1024,1024]{1,0:T(8,128)(2,1)} %fusion.16.b_ref, bf16[1024,1024]{1,0:T(8,128)(2,1)} %dynamic-slice_bitcast_fusion.dy_ref, bf16[1024,2048]{1,0:T(8,128)(2,1)} %up_ref.1, bf16[2048,1024]{1,0:T(8,128)(2,1)} %down_ref.1), custom_call_target="tpu_custom_call" | custom-call | flops 8589934592 | bytes 20971520 | tf_op jit(solution)/shard_map/mlp_mid/pallas_call | solution.py:204
  94.9 9.2 %fusion.45 = f32[2048,1024]{1,0:T(8,128)} fusion(bf16[1024,2048]{1,0:T(8,128)(2,1)} %get-tuple-element.22, bf16[1024,1024]{1,0:T(8,128)(2,1)S(1)} %copy-done.12), kind=kOutput, calls=%fused_computation.81 | convolution fusion | flops 4294967296 | bytes 14680064 | tf_op jit(solution)/shard_map/dot_general | solution.py:51
  104.2 6.4 %fusion.42 = f32[1024,1024]{1,0:T(8,128)} fusion(bf16[1024,2048]{1,0:T(8,128)(2,1)S(1)} %copy-done.31, bf16[2048,1024]{1,0:T(8,128)(2,1)S(1)} %copy-done.20), kind=kOutput, calls=%fused_computation.78 | convolution fusion | flops 4294967296 | bytes 12582912 | tf_op jit(solution)/shard_map/dot_general | solution.py:43
  110.6 6.1 %fusion.43 = f32[1024,1024]{1,0:T(8,128)} fusion(bf16[1024,2048]{1,0:T(8,128)(2,1)S(1)} %copy-done.25, bf16[1024,2048]{1,0:T(8,128)(2,1)S(1)} %copy-done.19), kind=kOutput, calls=%fused_computation.79 | convolution fusion | flops 4294967296 | bytes 12582912 | tf_op jit(solution)/shard_map/dot_general | solution.py:47
  116.7 16.3 %mlp_mid.3 = (bf16[1024,2048]{1,0:T(8,128)(2,1)}, bf16[1024,2048]{1,0:T(8,128)(2,1)}) custom-call(bf16[1024,1024]{1,0:T(8,128)(2,1)} %fusion.16.b_ref, bf16[1024,1024]{1,0:T(8,128)(2,1)} %dynamic-slice_bitcast_fusion.dy_ref, bf16[1024,2048]{1,0:T(8,128)(2,1)} %collective-permute-done.2.up_ref, bf16[2048,1024]{1,0:T(8,128)(2,1)} %collective-permute-done.3.down_ref), custom_call_target="tpu_custom_call" | custom-call | flops 8589934592 | bytes 20971520 | tf_op jit(solution)/shard_map/mlp_mid/pallas_call | solution.py:204
  133.0 9.9 %fusion.30 = (f32[1024]{0:T(1024)S(1)}, f32[1024]{0:T(1024)S(1)}, f32[1024]{0:T(1024)S(1)}, bf16[1024,1024]{1,0:T(8,128)(2,1)S(1)}) fusion(bf16[1024,1024]{1,0:T(8,128)(2,1)S(1)} %get-tuple-element.45, f32[1024]{0:T(1024)S(1)} %add_rsqrt_fusion, f32[1024]{0:T(1024)S(1)} %broadcast_multiply_fusion.4, f32[1024]{0:T(1024)S(1)} %convert_element_type.139, ...), kind=kOutput, calls=%fused_computation.42 | convolution fusion | flops 4307547136 | bytes 16801792 | tf_op jit(solution)/shard_map/dot_general | solution.py:47
  149.8 6.2 %convolution_convert_fusion.4 = bf16[2048,1024]{1,0:T(8,128)(2,1)} fusion(bf16[1024,2048]{1,0:T(8,128)(2,1)S(1)} %copy-done.33, bf16[1024,1024]{1,0:T(8,128)(2,1)S(1)} %copy-done.13), kind=kOutput, calls=%fused_computation.57 | convolution fusion | flops 4297064448 | bytes 10485760 | tf_op jit(solution)/shard_map/dot_general | solution.py:51
  155.9 7.9 %fusion.33 = bf16[1024,1024]{1,0:T(8,128)(2,1)} fusion(bf16[1024,1024]{1,0:T(8,128)(2,1)S(1)} %get-tuple-element.45, f32[1024,1024]{1,0:T(8,128)S(1)} %copy-done.32, bf16[1024,2048]{1,0:T(8,128)(2,1)S(1)} %copy-done.33, bf16[2048,1024]{1,0:T(8,128)(2,1)} %collective-permute-done.3.down_ref), kind=kOutput, calls=%fused_computation.45 | convolution fusion | flops 4301258752 | bytes 16777216 | tf_op jit(solution)/shard_map/dot_general | solution.py:43
  164.0 18.6 %attn_bwd.2 = bf16[1024,1536]{1,0:T(8,128)(2,1)} custom-call(s32[8,1024]{1,0:T(8,128)} %broadcast_in_dim.2.start_ref, bf16[1024,1536]{1,0:T(8,128)(2,1)} %convolution_convert_fusion.2.qkv_ref, bf16[1024,512]{1,0:T(8,128)(2,1)} %get-tuple-element.20.out_ref, bf16[1024,512]{1,0:T(8,128)(2,1)} %convolution_convert_fusion.7.grad_ref, ...), custom_call_target="tpu_custom_call" | custom-call | flops 5368709120 | bytes 8388608 | tf_op jit(solution)/shard_map/attn_bwd/pallas_call | solution.py:172
  182.6 7.0 %fusion.44 = f32[1024,1024]{1,0:T(8,128)} fusion(bf16[1024,1536]{1,0:T(8,128)(2,1)} %attn_bwd.2, bf16[1024,1536]{1,0:T(8,128)(2,1)S(1)} %copy-done.21), kind=kOutput, calls=%fused_computation.80 | convolution fusion | flops 3221225472 | bytes 10485760 | tf_op jit(solution)/shard_map/dot_general | solution.py:47
  191.9 18.6 %attn_bwd.3 = bf16[1024,1536]{1,0:T(8,128)(2,1)} custom-call(s32[8,1024]{1,0:T(8,128)} %broadcast_in_dim.2.start_ref, bf16[1024,1536]{1,0:T(8,128)(2,1)} %convolution_convert_fusion.1.qkv_ref, bf16[1024,512]{1,0:T(8,128)(2,1)} %get-tuple-element.21.out_ref, bf16[1024,512]{1,0:T(8,128)(2,1)} %convolution_convert_fusion.6.grad_ref, ...), custom_call_target="tpu_custom_call" | custom-call | flops 5368709120 | bytes 8388608 | tf_op jit(solution)/shard_map/attn_bwd/pallas_call | solution.py:172
  210.5 7.2 %convolution_convert_fusion = bf16[1024,1536]{1,0:T(8,128)(2,1)} fusion(bf16[1024,1536]{1,0:T(8,128)(2,1)} %attn_bwd.3, f32[1024]{0:T(1024)S(1)} %convert_element_type.131, f32[1024]{0:T(1024)S(1)} %add_rsqrt_fusion.1, f32[1024]{0:T(1024)S(1)} %broadcast_multiply_fusion.5, bf16[2,1024,1024]{2,1,0:T(8,128)(2,1)S(1)} %copy-done.4, s32[]{:T(128)S(6)} %select_n.28), kind=kOutput, calls=%fused_computation.53 | convolution fusion | flops 3228041216 | bytes 8400900 | tf_op jit(solution)/shard_map/dot_general | solution.py:51
  217.7 7.0 %fusion.32 = (f32[1024]{0:T(1024)S(1)}, f32[1024]{0:T(1024)S(1)}, f32[1024]{0:T(1024)S(1)}, bf16[1024,1024]{1,0:T(8,128)(2,1)S(1)}) fusion(f32[1024]{0:T(1024)S(1)} %add_rsqrt_fusion.1, f32[1024]{0:T(1024)S(1)} %broadcast_multiply_fusion.5, bf16[2,1024,1024]{2,1,0:T(8,128)(2,1)S(1)} %copy-done.4, s32[]{:T(128)S(6)} %select_n.28, ...), kind=kOutput, calls=%fused_computation.44 | convolution fusion | flops 3233805312 | bytes 14704644 | tf_op jit(solution)/shard_map/dot_general | solution.py:47
  225.2 2.9 fusion.26
  228.8 6.3 %convolution_convert_fusion.3 = bf16[1024,2048]{1,0:T(8,128)(2,1)} fusion(bf16[1024,1024]{1,0:T(8,128)(2,1)S(1)} %copy-done.11, bf16[1024,2048]{1,0:T(8,128)(2,1)S(1)} %copy-done.27), kind=kOutput, calls=%fused_computation.56 | convolution fusion | flops 4297064448 | bytes 10485760 | tf_op jit(solution)/shard_map/dot_general | solution.py:51
  235.5 6.9 %fusion.46 = f32[1024,2048]{1,0:T(8,128)} fusion(bf16[1024,1024]{1,0:T(8,128)(2,1)S(1)} %copy-done.11, bf16[1024,2048]{1,0:T(8,128)(2,1)S(1)} %copy-done.26), kind=kOutput, calls=%fused_computation.82 | convolution fusion | flops 4294967296 | bytes 14680064 | tf_op jit(solution)/shard_map/dot_general | solution.py:51
  242.4 69.0 %all-reduce = (bf16[1024]{0:T(1024)(128)(2,1)}, bf16[1024]{0:T(1024)(128)(2,1)}) all-reduce(f32[1024]{0:T(1024)S(1)} %get-tuple-element.32, f32[1024]{0:T(1024)S(1)} %get-tuple-element.34), channel_id=1, replica_groups=mesh['pod'=1,'dp'=64,'tp'=2] {'dp','tp'}, use_global_device_ids=true, to_apply=%region_10.11 | all-reduce | flops 2048 | bytes 12288 | tf_op jit(solution)/shard_map/psum | solution.py:453
  311.4 3.8 add_convert_fusion.7.refs_3_
  315.2 2.5 select_bitcast_fusion.3
  320.1 2.6 select_bitcast_fusion.1
  322.8 2.5 pad_maximum_fusion.1
  326.6 7.3 %add_convert_fusion.2.refs_2_ = bf16[1024,1536]{1,0:T(8,128)(2,1)} fusion(bf16[1024,1536]{1,0:T(8,128)(2,1)} %collective-permute-done.8, bf16[1024,1536]{1,0:T(8,128)(2,1)S(1)} %copy-done.28, f32[1024]{0:T(1024)S(1)} %convert_element_type.131, f32[1024]{0:T(1024)S(1)} %add_rsqrt_fusion.1, f32[1024]{0:T(1024)S(1)} %broadcast_multiply_fusion.5, ...), kind=kOutput, calls=%fused_computation.2 | convolution fusion | flops 3231186944 | bytes 11546628 | tf_op jit(solution)/shard_map/dot_general | solution.py:51
  333.9 6.0 %add_convert_fusion.1.refs_0_ = bf16[2048,1024]{1,0:T(8,128)(2,1)} fusion(f32[2048,1024]{1,0:T(8,128)S(1)} %bitcast.94, bf16[2048,1024]{1,0:T(8,128)(2,1)} %collective-permute-done.6), kind=kLoop, calls=%fused_computation.1 | loop fusion | flops 6291456 | bytes 16777216 | tf_op jit(solution)/shard_map/convert_element_type | solution.py:425
  339.9 8.3 %add_convert_fusion.refs_1_ = bf16[1024,2048]{1,0:T(8,128)(2,1)} fusion(f32[1024,2048]{1,0:T(8,128)} %fusion.46, bf16[1024,2048]{1,0:T(8,128)(2,1)} %collective-permute-done.7), kind=kLoop, calls=%fused_computation | loop fusion | flops 6291456 | bytes 16777216 | tf_op jit(solution)/shard_map/convert_element_type | solution.py:426
  348.2 117.5 %all_reduce_dp.1 = (bf16[2048,1024]{1,0:T(8,128)(2,1)}, bf16[1024,2048]{1,0:T(8,128)(2,1)}, bf16[1024,1536]{1,0:T(8,128)(2,1)}, bf16[512,1024]{1,0:T(8,128)(2,1)}) custom-call(bf16[2048,1024]{1,0:T(8,128)(2,1)} %add_convert_fusion.1.refs_0_, bf16[1024,2048]{1,0:T(8,128)(2,1)} %add_convert_fusion.refs_1_, bf16[1024,1536]{1,0:T(8,128)(2,1)} %add_convert_fusion.2.refs_2_, ...), custom_call_target="tpu_custom_call" | custom-call | tf_op jit(solution)/shard_map/all_reduce_dp/pallas_call | solution.py:368
  465.7 3.9 copy.39
  (118 shorter events, 32.7 us)
Async XLA Ops:
  0.6 41.5 %collective-permute-start = (bf16[1024,1536]{1,0:T(8,128)(2,1)}, bf16[1024,1536]{1,0:T(8,128)(2,1)}, u32[]{:S(2)}, u32[]{:S(2)}) collective-permute-start(bf16[1024,1536]{1,0:T(8,128)(2,1)} %param.13), channel_id=1, source_target_pairs={{0,1},{1,0},{2,3},{3,2},{4,5},{5,4},{6,7},{7,6},{8,9},{9,8},{10,11... | collective-permute-start | bytes 9437192 | tf_op jit(solution)/shard_map/ppermute | solution.py:394
  0.7 70.5 %collective-permute-start.1 = (bf16[512,1024]{1,0:T(8,128)(2,1)}, bf16[512,1024]{1,0:T(8,128)(2,1)S(1)}, u32[]{:S(2)}, u32[]{:S(2)}) collective-permute-start(bf16[512,1024]{1,0:T(8,128)(2,1)} %bitcast.97), channel_id=1, source_target_pairs={{0,1},{1,0},{2,3},{3,2},{4,5},{5,4},{6,7},{7,6},{8,9},{9,8},{10,11... | collective-permute-start | bytes 3145736 | tf_op jit(solution)/shard_map/ppermute | solution.py:394
  1.2 115.5 %collective-permute-start.2 = (bf16[1024,2048]{1,0:T(8,128)(2,1)}, bf16[1024,2048]{1,0:T(8,128)(2,1)}, u32[]{:S(2)}, u32[]{:S(2)}) collective-permute-start(bf16[1024,2048]{1,0:T(8,128)(2,1)} %up_ref.1), channel_id=1, source_target_pairs={{0,1},{1,0},{2,3},{3,2},{4,5},{5,4},{6,7},{7,6},{8,9},{9,8},{10,11... | collective-permute-start | bytes 12582920 | tf_op jit(solution)/shard_map/ppermute | solution.py:394
  1.3 115.4 %collective-permute-start.3 = (bf16[2048,1024]{1,0:T(8,128)(2,1)}, bf16[2048,1024]{1,0:T(8,128)(2,1)}, u32[]{:S(2)}, u32[]{:S(2)}) collective-permute-start(bf16[2048,1024]{1,0:T(8,128)(2,1)} %down_ref.1), channel_id=1, source_target_pairs={{0,1},{1,0},{2,3},{3,2},{4,5},{5,4},{6,7},{7,6},{8,9},{9,8},{10,11... | collective-permute-start | bytes 12582920 | tf_op jit(solution)/shard_map/ppermute | solution.py:394
  2.4 5.0 %copy-start.2 = (bf16[2,1024,1024]{2,1,0:T(8,128)(2,1)S(1)}, bf16[2,1024,1024]{2,1,0:T(8,128)(2,1)}, u32[]{:S(2)}) copy-start(bf16[2,1024,1024]{2,1,0:T(8,128)(2,1)} %param.9) | copy-start | bytes 12582916
  14.5 21.5 %copy-start.22 = (bf16[8,64,1024]{2,1,0:T(8,128)(2,1)S(1)}, bf16[8,64,1024]{2,1,0:T(8,128)(2,1)}, u32[]{:S(2)}) copy-start(bf16[8,64,1024]{2,1,0:T(8,128)(2,1)} %param.14) | copy-start | bytes 3145732
  50.0 21.3 %copy-start.3 = (bf16[2,1024,1024]{2,1,0:T(8,128)(2,1)S(1)}, bf16[2,1024,1024]{2,1,0:T(8,128)(2,1)}, u32[]{:S(2)}) copy-start(bf16[2,1024,1024]{2,1,0:T(8,128)(2,1)} %param.9) | copy-start | bytes 12582916
  78.4 16.5 %copy-start.12 = (bf16[1024,1024]{1,0:T(8,128)(2,1)S(1)}, bf16[1024,1024]{1,0:T(8,128)(2,1)}, u32[]{:S(2)}) copy-start(bf16[1024,1024]{1,0:T(8,128)(2,1)} %dynamic-slice_bitcast_fusion.dy_ref) | copy-start | bytes 6291460
  94.9 9.2 %copy-start.20 = (bf16[2048,1024]{1,0:T(8,128)(2,1)S(1)}, bf16[2048,1024]{1,0:T(8,128)(2,1)}, u32[]{:S(2)}) copy-start(bf16[2048,1024]{1,0:T(8,128)(2,1)} %down_ref.1) | copy-start | bytes 12582916
  94.9 9.2 %copy-start.31 = (bf16[1024,2048]{1,0:T(8,128)(2,1)S(1)}, bf16[1024,2048]{1,0:T(8,128)(2,1)}, u32[]{:S(2)}) copy-start(bf16[1024,2048]{1,0:T(8,128)(2,1)} %get-tuple-element.22) | copy-start | bytes 12582916
  104.1 6.5 %copy-start.19 = (bf16[1024,2048]{1,0:T(8,128)(2,1)S(1)}, bf16[1024,2048]{1,0:T(8,128)(2,1)}, u32[]{:S(2)}) copy-start(bf16[1024,2048]{1,0:T(8,128)(2,1)} %up_ref.1) | copy-start | bytes 12582916
  104.2 6.4 %copy-start.25 = (bf16[1024,2048]{1,0:T(8,128)(2,1)S(1)}, bf16[1024,2048]{1,0:T(8,128)(2,1)}, u32[]{:S(2)}) copy-start(bf16[1024,2048]{1,0:T(8,128)(2,1)} %get-tuple-element.24) | copy-start | bytes 12582916
  133.0 10.0 %copy-start.10 = (bf16[2,1024,1024]{2,1,0:T(8,128)(2,1)S(1)}, bf16[2,1024,1024]{2,1,0:T(8,128)(2,1)}, u32[]{:S(2)}) copy-start(bf16[2,1024,1024]{2,1,0:T(8,128)(2,1)} %param.17) | copy-start | bytes 12582916
  149.8 6.2 %copy-start.32 = (f32[1024,1024]{1,0:T(8,128)S(1)}, f32[1024,1024]{1,0:T(8,128)}, u32[]{:S(2)}) copy-start(f32[1024,1024]{1,0:T(8,128)} %fusion.42) | copy-start | bytes 12582916
  163.9 151.3 %collective-permute-start.4 = (bf16[1024,1024]{1,0:T(8,128)(2,1)}, bf16[1024,1024]{1,0:T(8,128)(2,1)}, u32[]{:S(2)}, u32[]{:S(2)}) collective-permute-start(bf16[1024,1024]{1,0:T(8,128)(2,1)} %fusion.33), channel_id=1, source_target_pairs={{0,1},{1,0},{2,3},{3,2},{4,5},{5,4},{6,7},{7,6},{8,9},{9,8},{10,11... | collective-permute-start | bytes 6291464 | tf_op jit(solution)/shard_map/ppermute | solution.py:394
  164.0 18.7 %copy-start.21 = (bf16[1024,1536]{1,0:T(8,128)(2,1)S(1)}, bf16[1024,1536]{1,0:T(8,128)(2,1)}, u32[]{:S(2)}) copy-start(bf16[1024,1536]{1,0:T(8,128)(2,1)} %param.13) | copy-start | bytes 9437188
  182.6 7.0 %copy-start.15 = (bf16[512,1024]{1,0:T(8,128)(2,1)S(1)}, bf16[512,1024]{1,0:T(8,128)(2,1)}, u32[]{:S(2)}) copy-start(bf16[512,1024]{1,0:T(8,128)(2,1)} %copy-done.14) | copy-start | bytes 3145732
  191.9 18.6 %copy-start.4 = (bf16[2,1024,1024]{2,1,0:T(8,128)(2,1)S(1)}, bf16[2,1024,1024]{2,1,0:T(8,128)(2,1)}, u32[]{:S(2)}) copy-start(bf16[2,1024,1024]{2,1,0:T(8,128)(2,1)} %param.9) | copy-start | bytes 12582916
  210.5 7.2 %copy-start.29 = (bf16[1024,1536]{1,0:T(8,128)(2,1)S(1)}, bf16[1024,1536]{1,0:T(8,128)(2,1)}, u32[]{:S(2)}) copy-start(bf16[1024,1536]{1,0:T(8,128)(2,1)} %attn_bwd.3) | copy-start | bytes 9437188
  210.5 7.2 %copy-start.30 = (f32[1024,1024]{1,0:T(8,128)S(1)}, f32[1024,1024]{1,0:T(8,128)}, u32[]{:S(2)}) copy-start(f32[1024,1024]{1,0:T(8,128)} %fusion.44) | copy-start | bytes 12582916
  217.7 7.0 %copy-start.17 = (bf16[512,1024]{1,0:T(8,128)(2,1)S(1)}, bf16[512,1024]{1,0:T(8,128)(2,1)}, u32[]{:S(2)}) copy-start(bf16[512,1024]{1,0:T(8,128)(2,1)} %convolution_convert_fusion.5) | copy-start | bytes 3145732
  224.8 10.4 %collective-permute-start.9 = (bf16[512,1024]{1,0:T(8,128)(2,1)S(1)}, bf16[512,1024]{1,0:T(8,128)(2,1)S(1)}, u32[]{:S(2)}, u32[]{:S(2)}) collective-permute-start(bf16[512,1024]{1,0:T(8,128)(2,1)S(1)} %copy-done.17), channel_id=1, source_target_pairs={{0,1},{1,0},{2,3},{3,2},{4,5},{5,4},{6,7},{7,6},{8,9},{9,8},{10,11... | collective-permute-start | bytes 3145736 | tf_op jit(solution)/shard_map/ppermute | solution.py:394
  228.1 7.3 %copy-start.26 = (bf16[1024,2048]{1,0:T(8,128)(2,1)S(1)}, bf16[1024,2048]{1,0:T(8,128)(2,1)}, u32[]{:S(2)}) copy-start(bf16[1024,2048]{1,0:T(8,128)(2,1)} %get-tuple-element.24) | copy-start | bytes 12582916
  228.1 92.0 %collective-permute-start.5 = (bf16[1024,1024]{1,0:T(8,128)(2,1)}, bf16[1024,1024]{1,0:T(8,128)(2,1)}, u32[]{:S(2)}, u32[]{:S(2)}) collective-permute-start(bf16[1024,1024]{1,0:T(8,128)(2,1)} %fusion.26), channel_id=1, source_target_pairs={{0,1},{1,0},{2,3},{3,2},{4,5},{5,4},{6,7},{7,6},{8,9},{9,8},{10,11... | collective-permute-start | bytes 6291464 | tf_op jit(solution)/shard_map/ppermute | solution.py:394
  228.2 105.6 %collective-permute-start.6 = (bf16[2048,1024]{1,0:T(8,128)(2,1)}, bf16[2048,1024]{1,0:T(8,128)(2,1)}, u32[]{:S(2)}, u32[]{:S(2)}) collective-permute-start(bf16[2048,1024]{1,0:T(8,128)(2,1)} %convolution_convert_fusion.4), channel_id=1, source_target_pairs={{0,1},{1,0},{2,3},{3,2},{4,5},{5,4},{6,7},{7,6},{8,9},{9,8},{10,11... | collective-permute-start | bytes 12582920 | tf_op jit(solution)/shard_map/ppermute | solution.py:394
  228.6 96.6 %collective-permute-start.8 = (bf16[1024,1536]{1,0:T(8,128)(2,1)}, bf16[1024,1536]{1,0:T(8,128)(2,1)}, u32[]{:S(2)}, u32[]{:S(2)}) collective-permute-start(bf16[1024,1536]{1,0:T(8,128)(2,1)} %convolution_convert_fusion), channel_id=1, source_target_pairs={{0,1},{1,0},{2,3},{3,2},{4,5},{5,4},{6,7},{7,6},{8,9},{9,8},{10,11... | collective-permute-start | bytes 9437192 | tf_op jit(solution)/shard_map/ppermute | solution.py:394
  235.1 7.3 %copy-start.24 = (bf16[512,1024]{1,0:T(8,128)(2,1)}, bf16[512,1024]{1,0:T(8,128)(2,1)S(1)}, u32[]{:S(2)}) copy-start(bf16[512,1024]{1,0:T(8,128)(2,1)S(1)} %collective-permute-done.9) | copy-start | bytes 3145732
  235.1 104.8 %collective-permute-start.7 = (bf16[1024,2048]{1,0:T(8,128)(2,1)}, bf16[1024,2048]{1,0:T(8,128)(2,1)}, u32[]{:S(2)}, u32[]{:S(2)}) collective-permute-start(bf16[1024,2048]{1,0:T(8,128)(2,1)} %convolution_convert_fusion.3), channel_id=1, source_target_pairs={{0,1},{1,0},{2,3},{3,2},{4,5},{5,4},{6,7},{7,6},{8,9},{9,8},{10,11... | collective-permute-start | bytes 12582920 | tf_op jit(solution)/shard_map/ppermute | solution.py:394
  320.1 5.2 %copy-start.28 = (bf16[1024,1536]{1,0:T(8,128)(2,1)S(1)}, bf16[1024,1536]{1,0:T(8,128)(2,1)}, u32[]{:S(2)}) copy-start(bf16[1024,1536]{1,0:T(8,128)(2,1)} %attn_bwd.2) | copy-start | bytes 9437188
  322.7 11.1 %slice-start = ((s8[8388608]{0:T(1024)(128)(4,1)}), s8[4194304]{0:T(1024)(128)(4,1)S(1)}, s32[]{:S(2)}) async-start(s8[8388608]{0:T(1024)(128)(4,1)} %bitcast.93), calls=%async_computation | async-start | bytes 8388608
  325.3 8.6 %slice-start.1 = ((s8[8388608]{0:T(1024)(128)(4,1)}), s8[4194304]{0:T(1024)(128)(4,1)S(1)}, s32[]{:S(2)}) async-start(s8[8388608]{0:T(1024)(128)(4,1)} %bitcast.93), calls=%async_computation.1 | async-start | bytes 8388608
  470.6 5.7 %copy-start.1 = (s32[2,1024]{1,0:T(2,128)S(1)}, s32[2,1024]{1,0:T(2,128)}, u32[]{:S(2)}) copy-start(s32[2,1024]{1,0:T(2,128)} %param.10) | copy-start | bytes 24580
  (14 other events, 49.3 us)

commit v2 on v1

v2 whole, which is shorter than its diff:
```python
import functools
import math

import jax
import jax.numpy as jnp
from jax import lax
from jax.experimental import pallas as pl
from jax.experimental.pallas import tpu as pltpu
from jax.sharding import PartitionSpec as P

EPS_NORM = 1e-5
NEG_LARGE = -1e30
LOG2E = math.log2(math.e)
SWAP = [(0, 1), (1, 0)]
TILE = 256
BF16 = jnp.bfloat16
F32 = jnp.float32


def norm_stats(x_rows):
    x_f32 = x_rows.astype(F32)
    mean = jnp.mean(x_f32, axis=-1, keepdims=True)
    centered = x_f32 - mean
    inv_std = lax.rsqrt(jnp.mean(centered * centered, axis=-1, keepdims=True) + EPS_NORM)
    return mean, inv_std


def norm_apply(x_rows, mean, inv_std, gain_vec):
    return ((x_rows.astype(F32) - mean) * inv_std * gain_vec.astype(F32)).astype(BF16)


def norm_backward(grad_out, x_rows, mean, inv_std, gain_vec):
    grad_f32 = grad_out.astype(F32)
    x_hat = (x_rows.astype(F32) - mean) * inv_std
    grad_gain = jnp.sum(grad_f32 * x_hat, axis=0)
    grad_hat = grad_f32 * gain_vec.astype(F32)
    mean_one = jnp.mean(grad_hat, axis=-1, keepdims=True)
    mean_two = jnp.mean(grad_hat * x_hat, axis=-1, keepdims=True)
    return inv_std * (grad_hat - mean_one - x_hat * mean_two), grad_gain


def dot_nn(lhs, rhs):
    return lax.dot_general(lhs, rhs, (((1,), (0,)), ((), ())), preferred_element_type=F32)


def dot_nt(lhs, rhs):
    return lax.dot_general(lhs, rhs, (((1,), (1,)), ((), ())), preferred_element_type=F32)


def dot_tn(lhs, rhs):
    return lax.dot_general(lhs, rhs, (((0,), (0,)), ((), ())), preferred_element_type=F32)


VMEM_LIMIT = 56 * 1024 * 1024
TAIL_VMEM = 63 * 1024 * 1024


def attn_fwd_kernel(dim, scale, start_ref, normed_ref, wp_ref, wo_ref, qkv_ref, out_ref, lse_ref, normed_t_ref):
    seq = qkv_ref.shape[0]
    step = pl.program_id(0)
    half = pl.num_programs(0) // 2

    @pl.when(step == 0)
    def _():
        normed_t_ref[...] = normed_ref[...].T

    weight = jnp.where(step < half, wp_ref[...], wo_ref[...])
    block = dot_nn(normed_ref[...], weight).astype(BF16)
    qkv_ref[...] = block
    block_t = block.T
    start = start_ref[0:1, :]
    heads_t = []
    for head in range(2):
        base = 3 * dim * head
        k_rows = block[:, base + dim : base + 2 * dim]
        q_cols = block_t[base : base + dim]
        v_cols = block_t[base + 2 * dim : base + 3 * dim]
        strips = []
        for i in range(seq // TILE):
            lo, hi = i * TILE, (i + 1) * TILE
            scores = dot_nn(k_rows[:hi], q_cols[:, lo:hi]) * (scale * LOG2E)
            k_pos = lax.broadcasted_iota(jnp.int32, (hi, TILE), 0)
            allowed = k_pos >= start[:, lo:hi]
            q_pos = lax.broadcasted_iota(jnp.int32, (TILE, TILE), 1) + lo
            diag = jnp.where(allowed[lo:] & (k_pos[lo:] <= q_pos), scores[lo:], NEG_LARGE)
            if lo:
                body = jnp.where(allowed[:lo], scores[:lo], NEG_LARGE)
                scores = jnp.concatenate([body, diag], axis=0)
            else:
                scores = diag
            top = jnp.max(scores, axis=0, keepdims=True)
            probs = jnp.exp2(scores - top)
            total = jnp.sum(probs, axis=0, keepdims=True)
            probs = (probs * (1.0 / total)).astype(BF16)
            strips.append(dot_nn(v_cols[:, :hi], probs))
            lse_ref[0, head : head + 1, lo:hi] = top + jnp.log2(total)
        heads_t.append(jnp.concatenate(strips, axis=1))
    out_ref[...] = jnp.concatenate(heads_t, axis=0).T.astype(BF16)


def attention_forward(start, normed, w_peer, w_own, dim, scale):
    seq, hidden = normed.shape
    width = 6 * dim
    half = w_own.shape[1] // width
    pairs = 2 * half
    return pl.pallas_call(
        functools.partial(attn_fwd_kernel, dim, scale),
        grid=(pairs,),
        in_specs=[
            pl.BlockSpec((8, seq), lambda i: (0, 0)),
            pl.BlockSpec((seq, hidden), lambda i: (0, 0)),
            pl.BlockSpec((hidden, width), lambda i: (0, jnp.minimum(i, half - 1))),
            pl.BlockSpec((hidden, width), lambda i: (0, jnp.maximum(i - half, 0))),
        ],
        out_specs=[
            pl.BlockSpec((seq, width), lambda i: (0, i)),
            pl.BlockSpec((seq, 2 * dim), lambda i: (0, i)),
            pl.BlockSpec((1, 8, seq), lambda i: (i, 0, 0)),
            pl.BlockSpec((hidden, seq), lambda i: (0, 0)),
        ],
        out_shape=[
            jax.ShapeDtypeStruct((seq, pairs * width), BF16),
            jax.ShapeDtypeStruct((seq, pairs * 2 * dim), BF16),
            jax.ShapeDtypeStruct((pairs, 8, seq), F32),
            jax.ShapeDtypeStruct((hidden, seq), BF16),
        ],
        compiler_params=pltpu.CompilerParams(vmem_limit_bytes=VMEM_LIMIT),
        cost_estimate=pl.CostEstimate(flops=pairs * (8 * seq * seq * dim + 2 * seq * hidden * width), bytes_accessed=4 * seq * pairs * width, transcendentals=pairs * seq * seq),
        name="attn_fwd",
    )(start, normed, w_peer, w_own)


def attn_bwd_head(dim, scale, head, block, block_t, grad, grad_t, prod_t, start, lse):
    seq = block.shape[0]
    base = 3 * dim * head
    q_rows = block[:, base : base + dim]
    k_rows = block[:, base + dim : base + 2 * dim]
    v_rows = block[:, base + 2 * dim : base + 3 * dim]
    q_cols = block_t[base : base + dim]
    k_cols = block_t[base + dim : base + 2 * dim]
    do_rows = grad[:, head * dim : (head + 1) * dim]
    do_cols = grad_t[head * dim : (head + 1) * dim]
    delta = jnp.sum(prod_t[head * dim : (head + 1) * dim], axis=0, keepdims=True)
    dq_cols = None
    dk_parts, dv_parts = [], []
    for j in range(seq // TILE):
        lo, hi = j * TILE, (j + 1) * TILE
        width = seq - lo
        scores = dot_nn(k_rows[lo:hi], q_cols[:, lo:]) * (scale * LOG2E)
        grad_probs = dot_nn(v_rows[lo:hi], do_cols[:, lo:])
        k_pos = lax.broadcasted_iota(jnp.int32, (TILE, width), 0) + lo
        allowed = k_pos >= start[:, lo:]
        q_pos = lax.broadcasted_iota(jnp.int32, (TILE, TILE), 1) + lo
        probs = jnp.exp2(scores - lse[:, lo:])
        diag = jnp.where(allowed[:, :TILE] & (k_pos[:, :TILE] <= q_pos), probs[:, :TILE], 0.0)
        if width > TILE:
            body = jnp.where(allowed[:, TILE:], probs[:, TILE:], 0.0)
            probs = jnp.concatenate([diag, body], axis=1)
        else:
            probs = diag
        grad_scores = (probs * (grad_probs - delta[:, lo:]) * scale).astype(BF16)
        dv_parts.append(dot_nn(probs.astype(BF16), do_rows[lo:]))
        dk_parts.append(dot_nn(grad_scores, q_rows[lo:]))
        dq_part = dot_nn(k_cols[:, lo:hi], grad_scores)
        if dq_cols is None:
            dq_cols = dq_part
        else:
            dq_cols = jnp.concatenate([dq_cols[:, :lo], dq_cols[:, lo:] + dq_part], axis=1)
    return [dq_cols.T, jnp.concatenate(dk_parts, axis=0), jnp.concatenate(dv_parts, axis=0)]


GELU_A = math.sqrt(2.0 / math.pi)
GELU_B = 0.044715


def mlp_mid_kernel(rows, b_ref, dy_ref, up_ref, down_ref, act_ref, dpre_ref):
    for r in range(b_ref.shape[0] // rows):
        span = pl.ds(r * rows, rows)
        pre = dot_nn(b_ref[span, :], up_ref[...])
        grad_h = dot_nt(dy_ref[span, :], down_ref[...]).astype(BF16).astype(F32)
        square = pre * pre
        tanh = jnp.tanh(pre * (GELU_A + (GELU_A * GELU_B) * square))
        cdf = 0.5 + 0.5 * tanh
        act_ref[span, :] = (pre * cdf).astype(BF16)
        slope = cdf + (0.5 * pre) * (1.0 - tanh * tanh) * (GELU_A + (3.0 * GELU_A * GELU_B) * square)
        dpre_ref[span, :] = (grad_h * slope).astype(BF16)


def mlp_mid(normed, grad_rows, w_up, w_down, tile_n=512, rows=256):
    tokens, hidden = normed.shape
    ffn = w_up.shape[1]
    return pl.pallas_call(
        functools.partial(mlp_mid_kernel, rows),
        grid=(ffn // tile_n,),
        in_specs=[
            pl.BlockSpec((tokens, hidden), lambda i: (0, 0)),
            pl.BlockSpec((tokens, hidden), lambda i: (0, 0)),
            pl.BlockSpec((hidden, tile_n), lambda i: (0, i)),
            pl.BlockSpec((tile_n, hidden), lambda i: (i, 0)),
        ],
        out_specs=[pl.BlockSpec((tokens, tile_n), lambda i: (0, i))] * 2,
        out_shape=[jax.ShapeDtypeStruct((tokens, ffn), BF16)] * 2,
        compiler_params=pltpu.CompilerParams(vmem_limit_bytes=VMEM_LIMIT),
        cost_estimate=pl.CostEstimate(flops=4 * tokens * hidden * ffn, bytes_accessed=2 * tokens * (2 * hidden + 2 * ffn) + 4 * hidden * ffn, transcendentals=tokens * ffn),
        name="mlp_mid",
    )(normed, grad_rows, w_up, w_down)


MESH_ID = pl.DeviceIdType.MESH
RING = 4
FLOW_ROWS = 1024
UNIT = 128
BIG_UNITS = 6
SMALL_UNITS = 2
STREAMS = 2
LEVEL_ROWS = (256, 64, 16)
LEVEL_SLOT = (0, 768, 960)
SLOT_ROWS = 1008
AXIS_STRIDE = (1, 4, 16)
FLOWS = tuple((tuple((first + k) % 3 for k in range(3)), sign) for first in range(3) for sign in (1, -1))
STEPS = 6 * (RING - 1)
POINTS = 4
FREED = {4: 0, 7: 1, 9: 2}
PAIR_US = 7.5
HOP_US = 3.0
GRADS_UP, GRADS_DOWN, GRADS_OUT = range(3)


def big_pieces(flow):
    first = flow * BIG_UNITS
    bounds = ((GRADS_UP, 0, 16), (GRADS_DOWN, 16, 24), (GRADS_DOWN, 24, 32), (GRADS_OUT, 32, 36))
    pieces = []
    for array, begin, end in bounds:
        lo, hi = max(first, begin), min(first + BIG_UNITS, end)
        if lo < hi:
            origin = 16 if array == GRADS_DOWN else begin
            pieces.append((array, lo - origin, (lo - first) * UNIT, (hi - lo) * UNIT))
    return pieces


def hbm_block(refs, piece, row, rows):
    array, local, _, width = piece
    ref = refs[array]
    if array == GRADS_UP:
        return ref.at[pl.ds(row, rows), pl.ds(local * UNIT, width)]
    if array == GRADS_DOWN:
        return ref.at[pl.ds((local // 8) * FLOW_ROWS + row, rows), pl.ds((local % 8) * UNIT, width)]
    half = row // 512
    lane = pl.multiple_of(half * 512 + local * UNIT, UNIT)
    return ref.at[pl.ds(pl.multiple_of(row - half * 512, 256), rows), pl.ds(lane, width)]


def plan_ops(pairs):
    inside, after = {}, []
    for stream in range(STREAMS):
        unit = (0.0330, 0.0110)[stream]
        clock = (0.0, pairs * PAIR_US)[stream]
        for step in range(STEPS + 1):
            point = None
            for pair in range(pairs):
                for spot in range(POINTS):
                    at = (pair + (0.0, 0.33, 0.67, 0.84)[spot]) * PAIR_US
                    if point is None and at >= clock - 0.01:
                        point, when = (pair, spot), at
            if point is None:
                when = max(clock, pairs * PAIR_US)
                after.append((when, stream, step))
            else:
                inside.setdefault(point, []).append((stream, step))
            level = min(step // 3 if step < 9 else 2 - (step - 9) // 3, 2)
            clock = when + HOP_US + unit * LEVEL_ROWS[max(level, 0)]
    after.sort()
    return inside, [(stream, step) for _, stream, step in after]


def tail_kernel(dim, scale, pairs, *refs):
    (start_ref, qkv_ref, out_ref, grad_ref, lse_ref, wp_ref, wo_ref, normed_t_ref, x_ref, gx_ref, gain_ref, gain_two_ref) = refs[:12]
    ins, outs = refs[12:15], refs[15:18]
    qkv_sum, dx_out, gains_out = refs[18:21]
    (own, slots, small, small_slots, sent, da_acc, dx_buf, gains, send_sem, recv_sem, load_sem, store_sem, swap_send, swap_recv, dx_sem, gain_send, gain_recv, free_sem) = refs[21:]
    pid = pl.program_id(0)
    half = pairs // 2
    me = lax.axis_index("dp")
    core = lax.axis_index("tp")
    coords = (lax.rem(me, 4), lax.rem(me // 4, 4), me // 16)
    inside, after = plan_ops(pairs)

    def neighbour(axis, shift):
        moved = lax.rem(coords[axis] + shift + RING, RING)
        return {"dp": me + (moved - coords[axis]) * AXIS_STRIDE[axis]}

    partner = {"tp": 1 - core}
    place, bases = [], []
    for axes, sign in FLOWS:
        spots = [coords[a] if sign > 0 else lax.rem(RING - coords[a], RING) for a in axes]
        base = [0]
        for level in range(2):
            base.append(base[-1] + lax.rem(spots[level] + 1, RING) * LEVEL_ROWS[level])
        place.append(spots)
        bases.append(base)

    def chunk(flow, level, shift):
        index = lax.rem(place[flow][level] + shift + RING, RING)
        return pl.multiple_of(bases[flow][level] + index * LEVEL_ROWS[level], LEVEL_ROWS[level])

    def view(of_slots, flow, stream, row, rows):
        if stream == 0:
            return (slots if of_slots else own).at[flow, pl.ds(row, rows), :]
        return (small_slots if of_slots else small).at[pl.ds(SMALL_UNITS * flow, SMALL_UNITS), pl.ds(row, rows), :]

    def loads(flow, turn):
        row = chunk(flow, 0, -turn)
        copies = []
        for k, piece in enumerate(big_pieces(flow)):
            target = own.at[flow, pl.ds(row, LEVEL_ROWS[0]), pl.ds(piece[2], piece[3])]
            copies.append(pltpu.make_async_copy(hbm_block(ins, piece, row, LEVEL_ROWS[0]), target, load_sem.at[flow, turn, k]))
        return copies

    def stores(flow, stream, turn):
        row = chunk(flow, 0, 1 - turn)
        copies = []
        if stream == 1:
            for k in range(SMALL_UNITS):
                index = SMALL_UNITS * flow + k
                target = qkv_sum.at[pl.ds(row, LEVEL_ROWS[0]), pl.ds(index * UNIT, UNIT)]
                copies.append(pltpu.make_async_copy(small.at[index, pl.ds(row, LEVEL_ROWS[0]), :], target, store_sem.at[flow, stream, turn, k]))
            return copies
        for k, piece in enumerate(big_pieces(flow)):
            source = own.at[flow, pl.ds(row, LEVEL_ROWS[0]), pl.ds(piece[2], piece[3])]
            copies.append(pltpu.make_async_copy(source, hbm_block(outs, piece, row, LEVEL_ROWS[0]), store_sem.at[flow, stream, turn, k]))
        return copies

    def where(step):
        if step < 9:
            return step // 3, step % 3, False
        return 2 - (step - 9) // 3, step % 3, True

    def copy(flow, stream, step):
        level, turn, gathering = where(step)
        rows = LEVEL_ROWS[level]
        axes, sign = FLOWS[flow]
        if gathering:
            source = view(False, flow, stream, chunk(flow, level, 1 - turn), rows)
            target = source
        else:
            source = view(False, flow, stream, chunk(flow, level, -turn), rows)
            target = view(True, flow, stream, LEVEL_SLOT[level] + turn * rows, rows)
        return pltpu.make_async_remote_copy(
            src_ref=source, dst_ref=target, send_sem=send_sem.at[flow, stream, step], recv_sem=recv_sem.at[flow, stream, step],
            device_id=neighbour(axes[level], sign), device_id_type=MESH_ID)

    def absorb(flow, stream, step):
        level, turn, gathering = where(step)
        copy(flow, stream, step).wait_recv()
        if gathering:
            if level == 1 and turn == 2:
                for each in stores(flow, stream, 0):
                    each.start()
            if level == 0:
                for each in stores(flow, stream, turn + 1):
                    each.start()
            return
        if level == 0 and stream == 0:
            for each in loads(flow, turn + 1):
                each.wait()
        rows = LEVEL_ROWS[level]
        row = chunk(flow, level, -turn - 1)
        part = min(rows, 64)

        def add(i, carry):
            kept = view(False, flow, stream, pl.multiple_of(row + i * part, 16), part)
            got = view(True, flow, stream, pl.multiple_of(LEVEL_SLOT[level] + turn * rows + i * part, 16), part)
            kept[...] = (kept[...].astype(F32) + got[...].astype(F32)).astype(BF16)
            return carry

        if rows == part:
            add(0, 0)
        else:
            lax.fori_loop(0, rows // part, add, 0)

    def run_op(stream, step):
        for flow in range(6):
            if step > 0:
                absorb(flow, stream, step - 1)
            elif stream == 0:
                for each in loads(flow, 0):
                    each.wait()
        if step in FREED:
            level = FREED[step]
            for flow, (axes, sign) in enumerate(FLOWS):
                for turn in range(3):
                    copy(flow, stream, 3 * level + turn).wait_send()
                pl.semaphore_signal(free_sem.at[flow, stream, level], inc=1, device_id=neighbour(axes[level], -sign), device_id_type=MESH_ID)
        if step in (9, 12, 15):
            for flow in range(6):
                pl.semaphore_wait(free_sem.at[flow, stream, 2 - (step - 9) // 3], 1)
        if step < STEPS:
            for flow in range(6):
                copy(flow, stream, step).start()

    def run_point(spot):
        for pair in range(pairs):
            ops = inside.get((pair, spot), [])
            if ops:
                @pl.when(pid == pair)
                def _():
                    for stream, step in ops:
                        run_op(stream, step)

    def swap_copy(j):
        return pltpu.make_async_remote_copy(
            src_ref=sent.at[lax.rem(j, 2)], dst_ref=small.at[pl.ds(3 * j, 3)], send_sem=swap_send.at[j], recv_sem=swap_recv.at[j],
            device_id=partner, device_id_type=MESH_ID)

    @pl.when(pid == 0)
    def _():
        barrier = pltpu.get_barrier_semaphore()
        for axis in range(3):
            for shift in (1, 2, 3):
                pl.semaphore_signal(barrier, inc=1, device_id=neighbour(axis, shift), device_id_type=MESH_ID)
        pl.semaphore_signal(barrier, inc=1, device_id=partner, device_id_type=MESH_ID)
        for turn in range(4):
            for flow in range(6):
                for each in loads(flow, turn):
                    each.start()
        pl.semaphore_wait(barrier, 10)
        da_acc[...] = jnp.zeros_like(da_acc)

    run_point(0)
    block = qkv_ref[...]
    block_t = block.T
    grad = grad_ref[...]
    grad_t = grad.T
    prod_t = grad_t.astype(F32) * out_ref[...].T.astype(F32)
    start = start_ref[0:1, :]
    pieces = attn_bwd_head(dim, scale, 0, block, block_t, grad, grad_t, prod_t, start, lse_ref[0, 0:1, :])
    run_point(1)
    pieces += attn_bwd_head(dim, scale, 1, block, block_t, grad, grad_t, prod_t, start, lse_ref[0, 1:2, :])
    dqkv = jnp.concatenate(pieces, axis=1).astype(BF16)
    run_point(2)
    weight = jnp.where(pid < half, wp_ref[...], wo_ref[...])
    da_acc[...] += dot_nt(dqkv, weight)
    run_point(3)

    @pl.when(pid < half)
    def _():
        @pl.when(pid >= 2)
        def _():
            swap_copy(pid - 2).wait_send()

        dw = dot_nn(normed_t_ref[...], dqkv).astype(BF16)
        for k in range(3):
            sent[lax.rem(pid, 2), k] = dw[:, k * UNIT : (k + 1) * UNIT]
        swap_copy(pid).start()

    @pl.when(pid >= half)
    def _():
        j = pid - half

        @pl.when(j < 2)
        def _():
            swap_copy(j + half - 2).wait_send()

        swap_copy(j).wait_recv()
        dw = dot_nn(normed_t_ref[...], dqkv)
        for k in range(3):
            index = 3 * j + k
            small[index] = (dw[:, k * UNIT : (k + 1) * UNIT] + small[index].astype(F32)).astype(BF16)

    @pl.when(pid == pairs - 1)
    def _():
        queue = list(after)

        def advance(count):
            for _ in range(min(count, len(queue))):
                run_op(*queue.pop(0))

        advance(1)
        gain = gain_ref[0:1, :]
        tile = 128

        def norm_tile(i, total):
            at = pl.ds(pl.multiple_of(i * tile, tile), tile)
            x_f32 = x_ref[at, :].astype(F32)
            centered = x_f32 - jnp.mean(x_f32, axis=-1, keepdims=True)
            inv_std = lax.rsqrt(jnp.mean(centered * centered, axis=-1, keepdims=True) + EPS_NORM)
            x_hat = centered * inv_std
            grad_a = da_acc[at, :].astype(BF16).astype(F32)
            grad_hat = grad_a * gain
            mean_one = jnp.mean(grad_hat, axis=-1, keepdims=True)
            mean_two = jnp.mean(grad_hat * x_hat, axis=-1, keepdims=True)
            back = inv_std * (grad_hat - mean_one - x_hat * mean_two)
            dx_buf[at, :] = (gx_ref[at, :].astype(F32) + back).astype(BF16)
            return total + jnp.sum(grad_a * x_hat, axis=0, keepdims=True)

        gain_one = lax.fori_loop(0, x_ref.shape[0] // tile, norm_tile, jnp.zeros_like(gain))
        for k in range(8):
            gains[0, core, k : k + 1, :] = gain_one[:, k * UNIT : (k + 1) * UNIT]
            gains[0, core, k + 8 : k + 9, :] = gain_two_ref[0:1, k * UNIT : (k + 1) * UNIT]
        advance(1)
        dx_local = pltpu.make_async_copy(dx_buf, dx_out.at[core], dx_sem.at[0])
        dx_remote = pltpu.make_async_remote_copy(
            src_ref=dx_buf, dst_ref=dx_out.at[core], send_sem=dx_sem.at[1], recv_sem=dx_sem.at[2], device_id=partner, device_id_type=MESH_ID)
        dx_local.start()
        dx_remote.start()

        def gain_copy(stage, slot, where_to, lane):
            return pltpu.make_async_remote_copy(
                src_ref=gains.at[stage, slot], dst_ref=gains.at[stage, slot], send_sem=gain_send.at[stage, lane], recv_sem=gain_recv.at[stage, slot],
                device_id=where_to, device_id_type=MESH_ID)

        for stage in range(4):
            if stage == 0:
                members, spot = 2, core
                others = [(partner, 1 - core)]
            else:
                members, spot = RING, coords[stage - 1]
                others = [(neighbour(stage - 1, d), lax.rem(spot + d, RING)) for d in (1, 2, 3)]
            for lane, (target, _) in enumerate(others):
                gain_copy(stage, spot, target, lane).start()
            advance(3)
            for lane, (target, slot) in enumerate(others):
                gain_copy(stage, slot, target, lane).wait_recv()
                gain_copy(stage, spot, target, lane).wait_send()
            total = gains[stage, 0]
            for member in range(1, members):
                total = total + gains[stage, member]
            if stage < 3:
                gains[stage + 1, coords[stage]] = total
            else:
                gains_out[...] = total
        advance(len(queue))
        dx_local.wait()
        dx_remote.wait()
        for stream in range(STREAMS):
            for flow in range(6):
                for step in range(9, STEPS):
                    copy(flow, stream, step).wait_send()
                for turn in range(4):
                    for each in stores(flow, stream, turn):
                        each.wait()


def backward_tail(dim, scale, start, qkv, out, grad, lse, w_peer, w_own, normed_t, x_rows, gx_rows, gain_one, gain_two_grad, grads):
    seq, hidden = x_rows.shape
    width = 6 * dim
    half = w_own.shape[1] // width
    pairs = 2 * half
    any_spec = pl.BlockSpec(memory_space=pl.ANY)
    fixed = lambda shape: pl.BlockSpec(shape, lambda i: (0,) * len(shape), pipeline_mode=pl.Buffered(1))
    row = lambda value: jnp.broadcast_to(value.astype(F32)[None, :], (8, hidden))
    return pl.pallas_call(
        functools.partial(tail_kernel, dim, scale, pairs),
        grid=(pairs,),
        in_specs=[
            fixed((8, seq)),
            pl.BlockSpec((seq, width), lambda i: (0, i)),
            pl.BlockSpec((seq, 2 * dim), lambda i: (0, i)),
            pl.BlockSpec((seq, 2 * dim), lambda i: (0, i)),
            pl.BlockSpec((1, 8, seq), lambda i: (i, 0, 0)),
            pl.BlockSpec((hidden, width), lambda i: (0, jnp.minimum(i, half - 1))),
            pl.BlockSpec((hidden, width), lambda i: (0, jnp.maximum(i - half, 0))),
            fixed((hidden, seq)),
            fixed((seq, hidden)),
            fixed((seq, hidden)),
            fixed((8, hidden)),
            fixed((8, hidden)),
        ] + [any_spec] * 3,
        out_specs=[any_spec] * 5 + [pl.BlockSpec((16, UNIT), lambda i: (0, 0))],
        out_shape=[jax.ShapeDtypeStruct(g.shape, BF16) for g in grads] + [
            jax.ShapeDtypeStruct((hidden, half * width), BF16),
            jax.ShapeDtypeStruct((2, seq, hidden), BF16),
            jax.ShapeDtypeStruct((16, UNIT), F32),
        ],
        scratch_shapes=[
            pltpu.VMEM((6, FLOW_ROWS, BIG_UNITS * UNIT), BF16),
            pltpu.VMEM((6, SLOT_ROWS, BIG_UNITS * UNIT), BF16),
            pltpu.VMEM((12, FLOW_ROWS, UNIT), BF16),
            pltpu.VMEM((12, SLOT_ROWS, UNIT), BF16),
            pltpu.VMEM((2, 3, FLOW_ROWS, UNIT), BF16),
            pltpu.VMEM((seq, hidden), F32),
            pltpu.VMEM((seq, hidden), BF16),
            pltpu.VMEM((4, RING, 16, UNIT), F32),
            pltpu.SemaphoreType.DMA((6, STREAMS, STEPS)),
            pltpu.SemaphoreType.DMA((6, STREAMS, STEPS)),
            pltpu.SemaphoreType.DMA((6, 4, 3)),
            pltpu.SemaphoreType.DMA((6, STREAMS, 4, 3)),
            pltpu.SemaphoreType.DMA((half,)),
            pltpu.SemaphoreType.DMA((half,)),
            pltpu.SemaphoreType.DMA((3,)),
            pltpu.SemaphoreType.DMA((4, 3)),
            pltpu.SemaphoreType.DMA((4, RING)),
            pltpu.SemaphoreType.REGULAR((6, STREAMS, 3)),
        ],
        compiler_params=pltpu.CompilerParams(collective_id=0, has_side_effects=True, vmem_limit_bytes=TAIL_VMEM),
        cost_estimate=pl.CostEstimate(flops=pairs * (20 * seq * seq * dim + 4 * seq * hidden * width), bytes_accessed=32 * seq * width, transcendentals=pairs * seq * seq),
        name="backward_tail",
    )(start, qkv, out, grad, lse, w_peer, w_own, normed_t, x_rows, gx_rows, row(gain_one), row(gain_two_grad), *grads)


def solution(mesh):
    batch_spec = P(("pod", "dp"), None, None)
    seg_spec = P(("pod", "dp"), None)

    def local_step(x_in, seg_ids, gain_one, gain_two, w_qkv, w_out, w_up, w_down, grad_y):
        heads_loc, dim, hidden = w_out.shape
        scale = dim ** -0.5
        swap = lambda value: lax.ppermute(value, "tp", SWAP)
        mine = lax.axis_index("tp")
        own_row = lambda value: lax.dynamic_index_in_dim(value, mine, 0, keepdims=False)

        w_out = w_out.reshape(heads_loc * dim, hidden)
        wqkv_p = swap(w_qkv)
        wout_p = swap(w_out)
        wup_p = swap(w_up)
        wdown_p = swap(w_down)
        x_rows = own_row(x_in)
        grad_rows = own_row(grad_y)
        seg = own_row(seg_ids)
        seq = x_rows.shape[0]
        start = jnp.sum((seg[None, :] < seg[:, None]).astype(jnp.int32), axis=1)
        start = jnp.broadcast_to(start[None, :], (8, seq))

        mean_a, inv_a = norm_stats(x_rows)
        normed_a = norm_apply(x_rows, mean_a, inv_a, gain_one)
        qkv, attn, lse, normed_t = attention_forward(start, normed_a, wqkv_p, w_qkv, dim, scale)
        wout_all = jnp.concatenate([wout_p, w_out], axis=0)
        part_one = dot_nn(attn, wout_all).astype(BF16)
        x_one = (x_rows.astype(F32) + part_one.astype(F32)).astype(BF16)
        mean_b, inv_b = norm_stats(x_one)
        normed_b = norm_apply(x_one, mean_b, inv_b, gain_two)

        act_p, dpre_p = mlp_mid(normed_b, grad_rows, wup_p, wdown_p)
        act_o, dpre_o = mlp_mid(normed_b, grad_rows, w_up, w_down)
        sent_down = swap(dot_tn(act_p, grad_rows).astype(BF16))
        sent_up = swap(dot_tn(normed_b, dpre_p).astype(BF16))
        grad_down = (dot_tn(act_o, grad_rows) + sent_down.astype(F32)).astype(BF16)
        grad_up = (dot_tn(normed_b, dpre_o) + sent_up.astype(F32)).astype(BF16)

        grad_norm_b = (dot_nt(dpre_o, w_up) + dot_nt(dpre_p, wup_p)).astype(BF16)
        back_b, gain_grad_two = norm_backward(grad_norm_b, x_one, mean_b, inv_b, gain_two)
        grad_x_one = (grad_rows.astype(F32) + back_b).astype(BF16)
        grad_wout = dot_tn(attn, grad_x_one)
        rows_loc = heads_loc * dim
        sent_out = swap(grad_wout[:rows_loc].astype(BF16))
        grad_out_w = (grad_wout[rows_loc:] + sent_out.astype(F32)).astype(BF16)
        dattn = dot_nt(grad_x_one, wout_all).astype(BF16)

        part_two = (dot_nn(act_o, w_down) + dot_nn(act_p, wdown_p)).astype(BF16)
        y_rows = (x_one.astype(F32) + part_two.astype(F32)).astype(BF16)

        def both_rows(value):
            other = swap(value)
            first = mine == 0
            return jnp.stack([jnp.where(first, value, other), jnp.where(first, other, value)])

        sum_up, sum_down, sum_out, sum_qkv, grad_x, gain_sums = backward_tail(
            dim, scale, start, qkv, attn, dattn, lse, wqkv_p, w_qkv, normed_t, x_rows, grad_x_one, gain_one, gain_grad_two, (grad_up, grad_down, grad_out_w))
        gain_sums = gain_sums.reshape(2, hidden).astype(BF16)
        return (
            both_rows(y_rows),
            grad_x,
            gain_sums[0],
            gain_sums[1],
            sum_qkv,
            sum_out.reshape(heads_loc, dim, hidden),
            sum_up,
            sum_down,
        )

    return jax.shard_map(
        local_step,
        mesh=mesh,
        in_specs=(batch_spec, seg_spec, P(None), P(None), P(None, "tp"), P("tp", None, None), P(None, "tp"), P("tp", None), batch_spec),
        out_specs=(batch_spec, batch_spec, P("pod"), P("pod"), P("pod", "tp"), P(("pod", "tp"), None, None), P("pod", "tp"), P(("pod", "tp"), None)),
        check_vma=False,
    )
```

time: 485 us -> 382 us (0.79)
  blocking collectives: 69 us -> 0 us
  matrix products: 122 us -> 71.8 us
  Pallas kernels: 230 us -> 251 us
  other arithmetic: 37.7 us -> 28.7 us
  local copies, waits for them, and re-layouts: 14.2 us -> 22.3 us
    psum x1 -> x0, blocking collectives: 69 us -> none  [local_step(): gain_grads = lax.psum((gain_grad_one, gain_grad_two), ('dp', 'tp'))]
    dot_general x6 -> x3, matrix products: 38.2 us -> 17.6 us  [dot_nn(): lax.dot_general(lhs, rhs, (((1,), (0,)), ((), ())), preferred_element_typ...]
    dot_general x8 -> x5, matrix products: 49.1 us -> 33.9 us  [dot_tn(): lax.dot_general(lhs, rhs, (((0,), (0,)), ((), ())), preferred_element_typ...]
    dot_general x6 -> x3, matrix products: 34.7 us -> 20.2 us  [dot_nt(): lax.dot_general(lhs, rhs, (((1,), (1,)), ((), ())), preferred_element_typ...]
    pallas_call x3 -> x1, Pallas kernels: 155 us -> 168 us  [backward_tail(): pl.pallas_call(functools.partial(tail_kernel, dim, scale, pairs), grid=(p...]
    pallas_call x2 -> x1, Pallas kernels: 42.2 us -> 50.6 us  [attention_forward(): pl.pallas_call(functools.partial(attn_fwd_kernel, dim, scale), grid=(pair...]
    another operation x4 -> x2, other arithmetic: 10 us -> 2.77 us  [both_rows(): jnp.stack([jnp.where(first, value, other), jnp.where(first, other, value)])]
    unnamed x76 -> x61, local copies, waits for them, and re-layouts: 12.1 us -> 18.1 us
  transfers between devices with their start and end apart: 10 -> 8, of which waited for: 0 -> 0; matrix products, arithmetic and copies ran while one was open for 26% -> 21% of each run, Pallas kernels for 20% -> 18%
where the time goes in v2:
time: 382 us; the launch traced here: 378 us
  Pallas kernels  251 us (66%)
  matrix products  71.8 us (19%)
  other arithmetic  28.7 us (8%)
  local copies, waits for them, and re-layouts  22.3 us (6%)
    pallas_call x1, Pallas kernels, backward_tail(): pl.pallas_call(functools.partial(tail_kernel, dim, scale, pairs), grid=(p...  168 us
    pallas_call x1, Pallas kernels, attention_forward(): pl.pallas_call(functools.partial(attn_fwd_kernel, dim, scale), grid=(pair...  50.6 us
    dot_general x5, matrix products, dot_tn(): lax.dot_general(lhs, rhs, (((0,), (0,)), ((), ())), preferred_element_typ...  33.9 us
    pallas_call x2, Pallas kernels, mlp_mid(): pl.pallas_call(functools.partial(mlp_mid_kernel, rows), grid=(ffn // tile...  32.9 us
    dot_general x3, matrix products, dot_nt(): lax.dot_general(lhs, rhs, (((1,), (1,)), ((), ())), preferred_element_typ...  20.2 us
    unnamed x61, local copies, waits for them, and re-layouts  18.1 us
    dot_general x3, matrix products, dot_nn(): lax.dot_general(lhs, rhs, (((1,), (0,)), ((), ())), preferred_element_typ...  17.6 us
  transfers between devices with their start and end apart: 8, of which 0 were waited for; matrix products, arithmetic and copies ran while one was open for 21% of the time, Pallas kernels for 18%

profile of v2, /device:TPU:0, one launch (start us, length us, event | category | flops | bytes accessed | tf_op | source)
XLA Modules:
  0.0 377.8 jit_solution(4396912582483505032)
XLA Ops:
  2.5 2.1 convert_reduce_fusion.1
  5.3 1.7 dynamic-slice_bitcast_fusion.dy_ref
  7.7 2.0 fusion.17.normed_ref
  10.9 50.6 %attn_fwd.1 = (bf16[1024,3072]{1,0:T(8,128)(2,1)}, bf16[1024,1024]{1,0:T(8,128)(2,1)}, f32[8,8,1024]{2,1,0:T(8,128)}, bf16[1024,1024]{1,0:T(8,128)(2,1)}) custom-call(s32[8,1024]{1,0:T(8,128)} %broadcast_in_dim.6.start_ref.refs_0_, bf16[1024,1024]{1,0:T(8,128)(2,1)} %fusion.17.normed_ref, bf16[1024,1536]{1,0:T(8,128)(2,1)} %collective-permute-done.wp_ref.refs_5_, ...), custom_call_target="tpu_custom_call" | custom-call | flops 10737418240 | bytes 12582912 | tf_op jit(solution)/shard_map/attn_fwd/pallas_call | solution.py:106
  61.5 4.3 %convert_reduce_fusion = (f32[1024]{0:T(1024)S(1)}, bf16[1024,1024]{1,0:T(8,128)(2,1)S(1)}) fusion(bf16[1024,1024]{1,0:T(8,128)(2,1)} %get-tuple-element.22.refs_2_, bf16[512,1024]{1,0:T(8,128)(2,1)S(1)} %bitcast.43, bf16[512,1024]{1,0:T(8,128)(2,1)} %collective-permute-done.1, bf16[1024,1024]{1,0:T(8,128)(2,1)S(1)} %get-tuple-element.40.refs_8_), kind=kOutput, calls=%fused_computation.4 | convolution fusion | flops 2159016960 | bytes 8392704 | tf_op jit(solution)/shard_map/dot_general | solution.py:43
  66.5 2.0 fusion.9.b_ref
  68.5 16.5 %mlp_mid.2 = (bf16[1024,2048]{1,0:T(8,128)(2,1)}, bf16[1024,2048]{1,0:T(8,128)(2,1)}) custom-call(bf16[1024,1024]{1,0:T(8,128)(2,1)} %fusion.9.b_ref, bf16[1024,1024]{1,0:T(8,128)(2,1)} %dynamic-slice_bitcast_fusion.dy_ref, bf16[1024,2048]{1,0:T(8,128)(2,1)} %up_ref.1, bf16[2048,1024]{1,0:T(8,128)(2,1)} %down_ref.1), custom_call_target="tpu_custom_call" | custom-call | flops 8589934592 | bytes 20971520 | tf_op jit(solution)/shard_map/mlp_mid/pallas_call | solution.py:192
  85.0 9.7 %fusion.27 = f32[1024,2048]{1,0:T(8,128)} fusion(bf16[1024,1024]{1,0:T(8,128)(2,1)S(1)} %copy-done.8, bf16[1024,2048]{1,0:T(8,128)(2,1)} %get-tuple-element.26), kind=kOutput, calls=%fused_computation.60 | convolution fusion | flops 4294967296 | bytes 14680064 | tf_op jit(solution)/shard_map/dot_general | solution.py:51
  94.7 6.1 %fusion.26 = f32[1024,1024]{1,0:T(8,128)} fusion(bf16[1024,2048]{1,0:T(8,128)(2,1)S(1)} %copy-done.19, bf16[1024,2048]{1,0:T(8,128)(2,1)S(1)} %copy-done.16), kind=kOutput, calls=%fused_computation.59 | convolution fusion | flops 4294967296 | bytes 12582912 | tf_op jit(solution)/shard_map/dot_general | solution.py:47
  100.9 6.0 %fusion.25 = f32[1024,1024]{1,0:T(8,128)} fusion(bf16[1024,2048]{1,0:T(8,128)(2,1)S(1)} %copy-done.22, bf16[2048,1024]{1,0:T(8,128)(2,1)S(1)} %copy-done.17), kind=kOutput, calls=%fused_computation.58 | convolution fusion | flops 4294967296 | bytes 12582912 | tf_op jit(solution)/shard_map/dot_general | solution.py:43
  106.9 16.5 %mlp_mid.3 = (bf16[1024,2048]{1,0:T(8,128)(2,1)}, bf16[1024,2048]{1,0:T(8,128)(2,1)}) custom-call(bf16[1024,1024]{1,0:T(8,128)(2,1)} %fusion.9.b_ref, bf16[1024,1024]{1,0:T(8,128)(2,1)} %dynamic-slice_bitcast_fusion.dy_ref, bf16[1024,2048]{1,0:T(8,128)(2,1)} %collective-permute-done.2.up_ref, bf16[2048,1024]{1,0:T(8,128)(2,1)} %collective-permute-done.3.down_ref), custom_call_target="tpu_custom_call" | custom-call | flops 8589934592 | bytes 20971520 | tf_op jit(solution)/shard_map/mlp_mid/pallas_call | solution.py:192
  123.4 8.6 %convolution_convert_fusion = bf16[2048,1024]{1,0:T(8,128)(2,1)} fusion(bf16[1024,2048]{1,0:T(8,128)(2,1)} %get-tuple-element.24, bf16[1024,1024]{1,0:T(8,128)(2,1)S(1)} %copy-done.10), kind=kOutput, calls=%fused_computation.36 | convolution fusion | flops 4297064448 | bytes 10485760 | tf_op jit(solution)/shard_map/dot_general | solution.py:51
  132.0 7.3 %fusion.21 = bf16[1024,1024]{1,0:T(8,128)(2,1)S(1)} fusion(bf16[1024,1024]{1,0:T(8,128)(2,1)S(1)} %get-tuple-element.46, f32[1024,1024]{1,0:T(8,128)S(1)} %copy-done.24, bf16[1024,2048]{1,0:T(8,128)(2,1)S(1)} %copy-done.25, bf16[2048,1024]{1,0:T(8,128)(2,1)} %collective-permute-done.3.down_ref), kind=kOutput, calls=%fused_computation.31 | convolution fusion | flops 4301258752 | bytes 16777216 | tf_op jit(solution)/shard_map/dot_general | solution.py:43
  139.4 6.2 %convolution_convert_fusion.1 = bf16[1024,2048]{1,0:T(8,128)(2,1)} fusion(bf16[1024,1024]{1,0:T(8,128)(2,1)S(1)} %copy-done.9, bf16[1024,2048]{1,0:T(8,128)(2,1)S(1)} %copy-done.20), kind=kOutput, calls=%fused_computation.37 | convolution fusion | flops 4297064448 | bytes 10485760 | tf_op jit(solution)/shard_map/dot_general | solution.py:51
  146.2 9.2 %fusion.19 = (f32[1024]{0:T(1024)S(1)}, f32[1024]{0:T(1024)S(1)}, f32[1024]{0:T(1024)S(1)}, bf16[1024,1024]{1,0:T(8,128)(2,1)S(1)}) fusion(bf16[1024,1024]{1,0:T(8,128)(2,1)S(1)} %get-tuple-element.46, f32[1024]{0:T(1024)S(1)} %add_rsqrt_fusion, f32[1024]{0:T(1024)S(1)} %broadcast_multiply_fusion.2, f32[1024]{0:T(1024)S(1)} %convert_element_type.98, ...), kind=kOutput, calls=%fused_computation.29 | convolution fusion | flops 4307547136 | bytes 16801792 | tf_op jit(solution)/shard_map/dot_general | solution.py:47
  155.4 1.9 fusion.13.refs_9_
  157.3 2.4 fusion.29
  160.9 7.0 %fusion.28 = f32[2048,1024]{1,0:T(8,128)} fusion(bf16[1024,2048]{1,0:T(8,128)(2,1)S(1)} %copy-done.23, bf16[1024,1024]{1,0:T(8,128)(2,1)S(1)} %copy-done.11), kind=kOutput, calls=%fused_computation.61 | convolution fusion | flops 4294967296 | bytes 14680064 | tf_op jit(solution)/shard_map/dot_general | solution.py:51
  167.9 4.9 %convolution_convert_fusion.2.refs_3_ = bf16[1024,1024]{1,0:T(8,128)(2,1)} fusion(bf16[1024,1024]{1,0:T(8,128)(2,1)S(1)} %fusion.13.refs_9_, bf16[512,1024]{1,0:T(8,128)(2,1)S(1)} %bitcast.44, bf16[512,1024]{1,0:T(8,128)(2,1)} %collective-permute-done.1), kind=kOutput, calls=%fused_computation.46 | convolution fusion | flops 2152726528 | bytes 6291456 | tf_op jit(solution)/shard_map/dot_general | solution.py:47
  172.9 1.3 fusion.22.refs_14_
  174.5 2.5 pad_maximum_fusion
  177.9 1.4 slice-done.1
  179.3 6.0 %add_convert_fusion.1.refs_12_ = bf16[1024,2048]{1,0:T(8,128)(2,1)} fusion(f32[1024,2048]{1,0:T(8,128)S(1)} %bitcast.39, bf16[1024,2048]{1,0:T(8,128)(2,1)} %collective-permute-done.5), kind=kLoop, calls=%fused_computation.1 | loop fusion | flops 6291456 | bytes 16777216 | tf_op jit(solution)/shard_map/convert_element_type | solution.py:638
  185.3 7.2 %add_convert_fusion.refs_13_ = bf16[2048,1024]{1,0:T(8,128)(2,1)} fusion(f32[2048,1024]{1,0:T(8,128)} %fusion.28, bf16[2048,1024]{1,0:T(8,128)(2,1)S(1)} %collective-permute-done.6), kind=kLoop, calls=%fused_computation | loop fusion | flops 6291456 | bytes 16777216 | tf_op jit(solution)/shard_map/convert_element_type | solution.py:637
  193.7 167.8 %backward_tail.1 = (bf16[1024,2048]{1,0:T(8,128)(2,1)}, bf16[2048,1024]{1,0:T(8,128)(2,1)}, bf16[512,1024]{1,0:T(8,128)(2,1)}, bf16[1024,1536]{1,0:T(8,128)(2,1)...) custom-call(s32[8,1024]{1,0:T(8,128)} %broadcast_in_dim.6.start_ref.refs_0_, ...), custom_call_target="tpu_custom_call" | custom-call | flops 23622320128 | bytes 12582912 | tf_op jit(solution)/shard_map/backward_tail/pallas_call | solution.py:552
  362.8 4.8 %copy.31 = bf16[2,1024,1024]{2,1,0:T(8,128)(2,1)} copy(bf16[2,1024,1024]{2,1,0:T(8,128)(2,1)} %get-tuple-element.59) | data formatting | bytes 8388608
  367.6 1.7 copy.32
  369.6 1.0 copy.33
  370.5 1.1 copy-done.4
  371.6 2.1 copy.34
  373.8 1.6 copy-done.3
  375.3 2.0 copy.35
  (88 shorter events, 11.0 us)
Async XLA Ops:
  0.6 9.6 %collective-permute-start = (bf16[1024,1536]{1,0:T(8,128)(2,1)}, bf16[1024,1536]{1,0:T(8,128)(2,1)}, u32[]{:S(2)}, u32[]{:S(2)}) collective-permute-start(bf16[1024,1536]{1,0:T(8,128)(2,1)} %refs_6_.1), channel_id=1, source_target_pairs={{0,1},{1,0},{2,3},{3,2},{4,5},{5,4},{6,7},{7,6},{8,9},{9,8},{10,11... | collective-permute-start | bytes 9437192 | tf_op jit(solution)/shard_map/ppermute | solution.py:608
  0.7 60.8 %collective-permute-start.1 = (bf16[512,1024]{1,0:T(8,128)(2,1)}, bf16[512,1024]{1,0:T(8,128)(2,1)}, u32[]{:S(2)}, u32[]{:S(2)}) collective-permute-start(bf16[512,1024]{1,0:T(8,128)(2,1)} %bitcast.42), channel_id=1, source_target_pairs={{0,1},{1,0},{2,3},{3,2},{4,5},{5,4},{6,7},{7,6},{8,9},{9,8},{10,11... | collective-permute-start | bytes 3145736 | tf_op jit(solution)/shard_map/ppermute | solution.py:608
  1.2 105.6 %collective-permute-start.2 = (bf16[1024,2048]{1,0:T(8,128)(2,1)}, bf16[1024,2048]{1,0:T(8,128)(2,1)}, u32[]{:S(2)}, u32[]{:S(2)}) collective-permute-start(bf16[1024,2048]{1,0:T(8,128)(2,1)} %up_ref.1), channel_id=1, source_target_pairs={{0,1},{1,0},{2,3},{3,2},{4,5},{5,4},{6,7},{7,6},{8,9},{9,8},{10,11... | collective-permute-start | bytes 12582920 | tf_op jit(solution)/shard_map/ppermute | solution.py:608
  1.3 105.5 %collective-permute-start.3 = (bf16[2048,1024]{1,0:T(8,128)(2,1)}, bf16[2048,1024]{1,0:T(8,128)(2,1)}, u32[]{:S(2)}, u32[]{:S(2)}) collective-permute-start(bf16[2048,1024]{1,0:T(8,128)(2,1)} %down_ref.1), channel_id=1, source_target_pairs={{0,1},{1,0},{2,3},{3,2},{4,5},{5,4},{6,7},{7,6},{8,9},{9,8},{10,11... | collective-permute-start | bytes 12582920 | tf_op jit(solution)/shard_map/ppermute | solution.py:608
  5.3 56.2 %copy-start.2 = (bf16[1024,1024]{1,0:T(8,128)(2,1)}, bf16[1024,1024]{1,0:T(8,128)(2,1)S(1)}, u32[]{:S(2)}) copy-start(bf16[1024,1024]{1,0:T(8,128)(2,1)S(1)} %get-tuple-element.40.refs_8_) | copy-start | bytes 6291460
  6.9 3.3 copy-start.15
  10.9 50.6 %copy-start.18 = (bf16[8,64,1024]{2,1,0:T(8,128)(2,1)S(1)}, bf16[8,64,1024]{2,1,0:T(8,128)(2,1)}, u32[]{:S(2)}) copy-start(bf16[8,64,1024]{2,1,0:T(8,128)(2,1)} %param.14) | copy-start | bytes 3145732
  68.5 16.5 %copy-start.8 = (bf16[1024,1024]{1,0:T(8,128)(2,1)S(1)}, bf16[1024,1024]{1,0:T(8,128)(2,1)}, u32[]{:S(2)}) copy-start(bf16[1024,1024]{1,0:T(8,128)(2,1)} %fusion.9.b_ref) | copy-start | bytes 6291460
  85.0 9.7 %copy-start.16 = (bf16[1024,2048]{1,0:T(8,128)(2,1)S(1)}, bf16[1024,2048]{1,0:T(8,128)(2,1)}, u32[]{:S(2)}) copy-start(bf16[1024,2048]{1,0:T(8,128)(2,1)} %up_ref.1) | copy-start | bytes 12582916
  85.0 9.7 %copy-start.19 = (bf16[1024,2048]{1,0:T(8,128)(2,1)S(1)}, bf16[1024,2048]{1,0:T(8,128)(2,1)}, u32[]{:S(2)}) copy-start(bf16[1024,2048]{1,0:T(8,128)(2,1)} %get-tuple-element.26) | copy-start | bytes 12582916
  94.7 6.1 %copy-start.17 = (bf16[2048,1024]{1,0:T(8,128)(2,1)S(1)}, bf16[2048,1024]{1,0:T(8,128)(2,1)}, u32[]{:S(2)}) copy-start(bf16[2048,1024]{1,0:T(8,128)(2,1)} %down_ref.1) | copy-start | bytes 12582916
  94.7 6.1 %copy-start.22 = (bf16[1024,2048]{1,0:T(8,128)(2,1)S(1)}, bf16[1024,2048]{1,0:T(8,128)(2,1)}, u32[]{:S(2)}) copy-start(bf16[1024,2048]{1,0:T(8,128)(2,1)} %get-tuple-element.23) | copy-start | bytes 12582916
  106.9 16.5 %copy-start.10 = (bf16[1024,1024]{1,0:T(8,128)(2,1)S(1)}, bf16[1024,1024]{1,0:T(8,128)(2,1)}, u32[]{:S(2)}) copy-start(bf16[1024,1024]{1,0:T(8,128)(2,1)} %dynamic-slice_bitcast_fusion.dy_ref) | copy-start | bytes 6291460
  123.3 8.6 %copy-start.24 = (f32[1024,1024]{1,0:T(8,128)S(1)}, f32[1024,1024]{1,0:T(8,128)}, u32[]{:S(2)}) copy-start(f32[1024,1024]{1,0:T(8,128)} %fusion.25) | copy-start | bytes 12582916
  123.3 8.6 %copy-start.25 = (bf16[1024,2048]{1,0:T(8,128)(2,1)S(1)}, bf16[1024,2048]{1,0:T(8,128)(2,1)}, u32[]{:S(2)}) copy-start(bf16[1024,2048]{1,0:T(8,128)(2,1)} %get-tuple-element.24) | copy-start | bytes 12582916
  131.9 7.5 %copy-start.9 = (bf16[1024,1024]{1,0:T(8,128)(2,1)S(1)}, bf16[1024,1024]{1,0:T(8,128)(2,1)}, u32[]{:S(2)}) copy-start(bf16[1024,1024]{1,0:T(8,128)(2,1)} %fusion.9.b_ref) | copy-start | bytes 6291460
  131.9 7.5 %copy-start.20 = (bf16[1024,2048]{1,0:T(8,128)(2,1)S(1)}, bf16[1024,2048]{1,0:T(8,128)(2,1)}, u32[]{:S(2)}) copy-start(bf16[1024,2048]{1,0:T(8,128)(2,1)} %get-tuple-element.27) | copy-start | bytes 12582916
  139.3 34.9 %collective-permute-start.4 = (bf16[1024,1024]{1,0:T(8,128)(2,1)S(1)}, bf16[1024,1024]{1,0:T(8,128)(2,1)S(1)}, u32[]{:S(2)}, u32[]{:S(2)}) collective-permute-start(bf16[1024,1024]{1,0:T(8,128)(2,1)S(1)} %fusion.21), channel_id=1, source_target_pairs={{0,1},{1,0},{2,3},{3,2},{4,5},{5,4},{6,7},{7,6},{8,9},{9,8},{10,11... | collective-permute-start | bytes 6291464 | tf_op jit(solution)/shard_map/ppermute | solution.py:608
  145.7 9.7 %copy-start.6 = (bf16[2,1024,1024]{2,1,0:T(8,128)(2,1)S(1)}, bf16[2,1024,1024]{2,1,0:T(8,128)(2,1)}, u32[]{:S(2)}) copy-start(bf16[2,1024,1024]{2,1,0:T(8,128)(2,1)} %param.17) | copy-start | bytes 12582916
  145.7 31.4 %collective-permute-start.5 = (bf16[1024,2048]{1,0:T(8,128)(2,1)}, bf16[1024,2048]{1,0:T(8,128)(2,1)}, u32[]{:S(2)}, u32[]{:S(2)}) collective-permute-start(bf16[1024,2048]{1,0:T(8,128)(2,1)} %convolution_convert_fusion.1), channel_id=1, source_target_pairs={{0,1},{1,0},{2,3},{3,2},{4,5},{5,4},{6,7},{7,6},{8,9},{9,8},{10,11... | collective-permute-start | bytes 12582920 | tf_op jit(solution)/shard_map/ppermute | solution.py:608
  146.1 39.2 %collective-permute-start.6 = (bf16[2048,1024]{1,0:T(8,128)(2,1)}, bf16[2048,1024]{1,0:T(8,128)(2,1)S(1)}, u32[]{:S(2)}, u32[]{:S(2)}) collective-permute-start(bf16[2048,1024]{1,0:T(8,128)(2,1)} %convolution_convert_fusion), channel_id=1, source_target_pairs={{0,1},{1,0},{2,3},{3,2},{4,5},{5,4},{6,7},{7,6},{8,9},{9,8},{10,11... | collective-permute-start | bytes 12582920 | tf_op jit(solution)/shard_map/ppermute | solution.py:608
  157.3 10.6 %copy-start.12 = (bf16[1024,1024]{1,0:T(8,128)(2,1)}, bf16[1024,1024]{1,0:T(8,128)(2,1)S(1)}, u32[]{:S(2)}) copy-start(bf16[1024,1024]{1,0:T(8,128)(2,1)S(1)} %fusion.13.refs_9_) | copy-start | bytes 6291460
  157.3 3.1 copy-start.11
  157.3 3.6 copy-start.23
  160.0 12.9 %collective-permute-start.7 = (bf16[512,1024]{1,0:T(8,128)(2,1)S(1)}, bf16[512,1024]{1,0:T(8,128)(2,1)S(1)}, u32[]{:S(2)}, u32[]{:S(2)}) collective-permute-start(bf16[512,1024]{1,0:T(8,128)(2,1)S(1)} %slice.29), channel_id=1, source_target_pairs={{0,1},{1,0},{2,3},{3,2},{4,5},{5,4},{6,7},{7,6},{8,9},{9,8},{10,11... | collective-permute-start | bytes 3145736 | tf_op jit(solution)/shard_map/ppermute | solution.py:608
  174.2 3.7 slice-start
  174.5 4.8 %slice-start.1 = ((s8[8388608]{0:T(1024)(128)(4,1)}), s8[4194304]{0:T(1024)(128)(4,1)S(1)}, s32[]{:S(2)}) async-start(s8[8388608]{0:T(1024)(128)(4,1)} %bitcast.38), calls=%async_computation.1 | async-start | bytes 8388608
  185.3 7.2 %copy-start.14 = (bf16[1024]{0:T(1024)(128)(2,1)S(1)}, bf16[1024]{0:T(1024)(128)(2,1)}, u32[]{:S(2)}) copy-start(bf16[1024]{0:T(1024)(128)(2,1)} %param.11) | copy-start | bytes 6148
  362.8 4.8 %copy-start.7 = (bf16[1024,1536]{1,0:T(8,128)(2,1)S(1)}, bf16[1024,1536]{1,0:T(8,128)(2,1)}, u32[]{:S(2)}) copy-start(bf16[1024,1536]{1,0:T(8,128)(2,1)} %get-tuple-element.62) | copy-start | bytes 9437188
  367.6 4.0 %copy-start.4 = (bf16[1024,2048]{1,0:T(8,128)(2,1)S(1)}, bf16[1024,2048]{1,0:T(8,128)(2,1)}, u32[]{:S(2)}) copy-start(bf16[1024,2048]{1,0:T(8,128)(2,1)} %get-tuple-element.64) | copy-start | bytes 12582916
  371.6 3.7 copy-start.3
  371.6 5.7 %copy-start.1 = (s32[2,1024]{1,0:T(2,128)S(1)}, s32[2,1024]{1,0:T(2,128)}, u32[]{:S(2)}) copy-start(s32[2,1024]{1,0:T(2,128)} %param.10) | copy-start | bytes 24580
  (4 other events, 8.5 us)

commit v3 on v2

v3 whole, which is shorter than its diff:
```python
import functools
import math

import jax
import jax.numpy as jnp
from jax import lax
from jax.experimental import pallas as pl
from jax.experimental.pallas import tpu as pltpu
from jax.sharding import PartitionSpec as P

EPS_NORM = 1e-5
NEG_LARGE = -1e30
LOG2E = math.log2(math.e)
SWAP = [(0, 1), (1, 0)]
TILE = 256
FWD_TILE = 512
UNIT = 128
BF16 = jnp.bfloat16
F32 = jnp.float32
ALL = ...
ROW = dict(axis=-1, keepdims=True)
COL = dict(axis=0, keepdims=True)


def norm_stats(x_rows):
    x_f32 = x_rows.astype(F32)
    mean = jnp.mean(x_f32, **ROW)
    centered = x_f32 - mean
    inv_std = lax.rsqrt(jnp.mean(centered * centered, **ROW) + EPS_NORM)
    return mean, inv_std


def norm_apply(x_rows, mean, inv_std, gain_vec):
    return ((x_rows.astype(F32) - mean) * inv_std * gain_vec.astype(F32)).astype(BF16)


def norm_backward(grad_out, x_rows, mean, inv_std, gain_vec):
    grad_f32 = grad_out.astype(F32)
    x_hat = (x_rows.astype(F32) - mean) * inv_std
    grad_gain = jnp.sum(grad_f32 * x_hat, **COL)
    grad_hat = grad_f32 * gain_vec.astype(F32)
    mean_one = jnp.mean(grad_hat, **ROW)
    mean_two = jnp.mean(grad_hat * x_hat, **ROW)
    return inv_std * (grad_hat - mean_one - x_hat * mean_two), grad_gain


def cost(flops):
    return pl.CostEstimate(flops=flops, bytes_accessed=flops // UNIT, transcendentals=flops // UNIT)


def dot_nn(lhs, rhs):
    return lax.dot_general(lhs, rhs, (((1,), (0,)), ((), ())), preferred_element_type=F32)


def dot_nt(lhs, rhs):
    return lax.dot_general(lhs, rhs, (((1,), (1,)), ((), ())), preferred_element_type=F32)


def dot_tn(lhs, rhs):
    return lax.dot_general(lhs, rhs, (((0,), (0,)), ((), ())), preferred_element_type=F32)


FIRST = lambda i: (0, 0)
ACROSS = lambda i: (0, i)
VMEM_LIMIT = 56 * 1024 * 1024
TAIL_VMEM = 63 * 1024 * 1024


def head_parts(dim, head, width, take):
    base = head * (width // 2)
    return [take(lo, lo + dim) for lo in range(base, base + width // 2, dim)]


def attn_fwd_kernel(dim, scale, start_ref, normed_ref, wp_ref, wo_ref, qkv_ref, out_ref, lse_ref, normed_t_ref):
    seq = qkv_ref.shape[0]
    step = pl.program_id(0)
    half = pl.num_programs(0) // 2

    @pl.when(step == 0)
    def _():
        normed_t_ref[ALL] = normed_ref[ALL].T

    weight = jnp.where(step < half, wp_ref[ALL], wo_ref[ALL])
    block = dot_nn(normed_ref[ALL], weight).astype(BF16)
    qkv_ref[ALL] = block
    block_t = block.T
    start = start_ref[0:1, :]
    heads_t = []
    for head in range(2):
        _, k_rows, _ = head_parts(dim, head, block.shape[1], lambda lo, hi: block[:, lo:hi])
        q_cols, _, v_cols = head_parts(dim, head, block.shape[1], lambda lo, hi: block_t[lo:hi])
        strips = []
        for i in range(seq // FWD_TILE):
            lo, hi = i * FWD_TILE, (i + 1) * FWD_TILE
            scores = dot_nn(k_rows[:hi], q_cols[:, lo:hi]) * (scale * LOG2E)
            k_pos = lax.broadcasted_iota(jnp.int32, (hi, FWD_TILE), 0)
            allowed = k_pos >= start[:, lo:hi]
            q_pos = lax.broadcasted_iota(jnp.int32, (FWD_TILE, FWD_TILE), 1) + lo
            diag = jnp.where(allowed[lo:] & (k_pos[lo:] <= q_pos), scores[lo:], NEG_LARGE)
            if lo:
                body = jnp.where(allowed[:lo], scores[:lo], NEG_LARGE)
                scores = jnp.concatenate([body, diag], axis=0)
            else:
                scores = diag
            top = jnp.max(scores, **COL)
            probs = jnp.exp2(scores - top)
            total = jnp.sum(probs, **COL)
            probs = (probs * (1.0 / total)).astype(BF16)
            strips.append(dot_nn(v_cols[:, :hi], probs))
            lse_ref[0, head : head + 1, lo:hi] = top + jnp.log2(total)
        heads_t.append(jnp.concatenate(strips, axis=1))
    out_ref[ALL] = jnp.concatenate(heads_t, axis=0).T.astype(BF16)


def attention_forward(start, normed, w_peer, w_own, dim, scale):
    seq, hidden = normed.shape
    width = 6 * dim
    half = w_own.shape[1] // width
    pairs = 2 * half
    return pl.pallas_call(
        functools.partial(attn_fwd_kernel, dim, scale),
        grid=(pairs,),
        in_specs=[
            pl.BlockSpec((8, seq), FIRST),
            pl.BlockSpec((seq, hidden), FIRST),
            *half_specs((hidden, width), half, 1),
        ],
        out_specs=[
            pl.BlockSpec((seq, width), ACROSS),
            pl.BlockSpec((seq, 2 * dim), ACROSS),
            pl.BlockSpec((1, 8, seq), lambda i: (i, 0, 0)),
            pl.BlockSpec((hidden, seq), FIRST),
        ],
        out_shape=[
            jax.ShapeDtypeStruct((seq, pairs * width), BF16),
            jax.ShapeDtypeStruct((seq, pairs * 2 * dim), BF16),
            jax.ShapeDtypeStruct((pairs, 8, seq), F32),
            jax.ShapeDtypeStruct((hidden, seq), BF16),
        ],
        compiler_params=pltpu.CompilerParams(vmem_limit_bytes=VMEM_LIMIT),
        cost_estimate=cost(pairs * seq * seq * hidden),
        name="attn_fwd",
    )(start, normed, w_peer, w_own)


def attn_bwd_head(dim, scale, head, block, block_t, grad, grad_t, prod_t, start, lse):
    seq = block.shape[0]
    q_rows, k_rows, v_rows = head_parts(dim, head, block.shape[1], lambda lo, hi: block[:, lo:hi])
    q_cols, k_cols, _ = head_parts(dim, head, block.shape[1], lambda lo, hi: block_t[lo:hi])
    do_rows = grad[:, head * dim : (head + 1) * dim]
    do_cols = grad_t[head * dim : (head + 1) * dim]
    delta = jnp.sum(prod_t[head * dim : (head + 1) * dim], **COL)
    dq_cols = None
    dk_parts, dv_parts = [], []
    for j in range(seq // TILE):
        lo, hi = j * TILE, (j + 1) * TILE
        width = seq - lo
        scores = dot_nn(k_rows[lo:hi], q_cols[:, lo:]) * (scale * LOG2E)
        grad_probs = dot_nn(v_rows[lo:hi], do_cols[:, lo:])
        k_pos = lax.broadcasted_iota(jnp.int32, (TILE, width), 0) + lo
        allowed = k_pos >= start[:, lo:]
        q_pos = lax.broadcasted_iota(jnp.int32, (TILE, TILE), 1) + lo
        probs = jnp.exp2(scores - lse[:, lo:])
        diag = jnp.where(allowed[:, :TILE] & (k_pos[:, :TILE] <= q_pos), probs[:, :TILE], 0.0)
        if width > TILE:
            body = jnp.where(allowed[:, TILE:], probs[:, TILE:], 0.0)
            probs = jnp.concatenate([diag, body], axis=1)
        else:
            probs = diag
        grad_scores = (probs * (grad_probs - delta[:, lo:]) * scale).astype(BF16)
        dv_parts.append(dot_nn(probs.astype(BF16), do_rows[lo:]))
        dk_parts.append(dot_nn(grad_scores, q_rows[lo:]))
        dq_part = dot_nn(k_cols[:, lo:hi], grad_scores)
        if dq_cols is None:
            dq_cols = dq_part
        else:
            dq_cols = jnp.concatenate([dq_cols[:, :lo], dq_cols[:, lo:] + dq_part], axis=1)
    return [dq_cols.T, jnp.concatenate(dk_parts, axis=0), jnp.concatenate(dv_parts, axis=0)]


GELU_A = math.sqrt(2.0 / math.pi)
GELU_B = 0.044715


def mlp_mid_kernel(rows, b_ref, dy_ref, up_p_ref, up_o_ref, down_p_ref, down_o_ref, act_ref, dpre_ref):
    peer = pl.program_id(0) < pl.num_programs(0) // 2
    w_up = jnp.where(peer, up_p_ref[ALL], up_o_ref[ALL])
    w_down = jnp.where(peer, down_p_ref[ALL], down_o_ref[ALL])
    for r in range(b_ref.shape[0] // rows):
        span = pl.ds(r * rows, rows)
        pre = dot_nn(b_ref[span, :], w_up)
        grad_h = dot_nt(dy_ref[span, :], w_down).astype(BF16).astype(F32)
        square = pre * pre
        tanh = jnp.tanh(pre * (GELU_A + (GELU_A * GELU_B) * square))
        cdf = 0.5 + 0.5 * tanh
        act_ref[span, :] = (pre * cdf).astype(BF16)
        slope = cdf + (0.5 * pre) * (1.0 - tanh * tanh) * (GELU_A + (3.0 * GELU_A * GELU_B) * square)
        dpre_ref[span, :] = (grad_h * slope).astype(BF16)


def whole(shape):
    return pl.BlockSpec(shape, lambda i: (0,) * len(shape), pipeline_mode=pl.Buffered(1))


def half_specs(shape, half, axis):
    at = lambda index: (0, index) if axis else (index, 0)
    return [
        pl.BlockSpec(shape, lambda i: at(jnp.minimum(i, half - 1))),
        pl.BlockSpec(shape, lambda i: at(jnp.maximum(i - half, 0))),
    ]


def mlp_mid(normed, grad_rows, up_p, up_o, down_p, down_o, tile_n=512, rows=1024):
    tokens, hidden = normed.shape
    half = up_o.shape[1] // tile_n
    ffn = 2 * up_o.shape[1]
    return pl.pallas_call(
        functools.partial(mlp_mid_kernel, rows),
        grid=(2 * half,),
        in_specs=[pl.BlockSpec((tokens, hidden), FIRST)] * 2 + half_specs((hidden, tile_n), half, 1) + half_specs((tile_n, hidden), half, 0),
        out_specs=[pl.BlockSpec((tokens, tile_n), ACROSS)] * 2,
        out_shape=[jax.ShapeDtypeStruct((tokens, ffn), BF16)] * 2,
        compiler_params=pltpu.CompilerParams(vmem_limit_bytes=VMEM_LIMIT),
        cost_estimate=cost(tokens * hidden * ffn),
        name="mlp_mid",
    )(normed, grad_rows, up_p, up_o, down_p, down_o)


MESH_ID = pl.DeviceIdType.MESH
RING = 4
FLOW_ROWS = 1024
BIG_COLS = 6 * UNIT
BIG_BOUNDS = (0, 6, 12, 17, 22, 27, 32)
SMALL_BOUNDS = (None, (0, 2, 4, 6, 8, 9, 10), range(10, 17))
OUT_FIRST = 6
STREAMS = 3
LEVEL_ROWS = (256, 64, 16)
LEVEL_SLOT = (0, 768, 960)
SLOT_ROWS = 1008
BIG_SLOT_BASE = 768
AXIS_STRIDE = (1, 4, 16)
FLOWS = tuple((tuple((first + k) % 3 for k in range(3)), sign) for first in range(3) for sign in (1, -1))
FLOW_IDS = range(len(FLOWS))
PEERS = (1, 2, 3)
N_FLOWS = len(FLOWS)
TOP_ROWS, PART_ROWS = 256, 64
HALF_COLS = 512
STEPS = 10
SEMS = 18
POINTS = 4
FIRST_STEP = (3, 0, 0)
PAIR_US = 9.5
HOP_US = 3.2
STREAM_US = (1.4 * 6, 1.4 * 2, 1.4)
GRADS_UP, GRADS_DOWN = range(2)


def big_width(flow):
    return (BIG_BOUNDS[flow + 1] - BIG_BOUNDS[flow]) * UNIT


def big_pieces(flow):
    first, last = BIG_BOUNDS[flow], BIG_BOUNDS[flow + 1]
    pieces = []
    for array, begin, end in ((GRADS_UP, 0, 16), (GRADS_DOWN, 16, 24), (GRADS_DOWN, 24, 32)):
        lo, hi = max(first, begin), min(last, end)
        if lo < hi:
            pieces.append((array, lo - 16 if array == GRADS_DOWN else lo, (lo - first) * UNIT, (hi - lo) * UNIT))
    return pieces


def hbm_block(refs, piece, row, rows):
    array, local, _, width = piece
    ref = refs[array]
    if array == GRADS_UP:
        return ref.at[pl.ds(row, rows), pl.ds(local * UNIT, width)]
    return ref.at[pl.ds((local // 8) * FLOW_ROWS + row, rows), pl.ds((local % 8) * UNIT, width)]


def tell(semaphore, device):
    pl.semaphore_signal(semaphore, inc=1, device_id=device, device_id_type=MESH_ID)


def ring_tools():
    me = lax.axis_index("dp")
    coords = (lax.rem(me, 4), lax.rem(me // 4, 4), me // 16)

    def neighbour(axis, shift):
        moved = lax.rem(coords[axis] + shift + RING, RING)
        return {"dp": me + (moved - coords[axis]) * AXIS_STRIDE[axis]}

    place, bases = [], []
    for axes, sign in FLOWS:
        spots = [coords[a] if sign > 0 else lax.rem(RING - coords[a], RING) for a in axes]
        base = [0]
        for level in range(2):
            base.append(base[-1] + lax.rem(spots[level] + 1, RING) * LEVEL_ROWS[level])
        place.append(spots)
        bases.append(base)

    def chunk(flow, level, shift):
        index = lax.rem(place[flow][level] + shift + RING, RING)
        return pl.multiple_of(bases[flow][level] + index * LEVEL_ROWS[level], LEVEL_ROWS[level])

    return coords, neighbour, chunk


def mlp_out_kernel(steps, act_ref, dpre_ref, down_p_ref, down_o_ref, up_p_ref, up_o_ref, x_ref, up_hbm, down_hbm, db_ref, part_ref, y_out, own, slots, y_acc, b_acc, y_buf, send_sem, recv_sem, load_sem, y_sem):
    pid = pl.program_id(0)
    core = lax.axis_index("tp")
    partner = {"tp": 1 - core}
    coords, neighbour, chunk = ring_tools()
    ins = (up_hbm, down_hbm)
    rows = TOP_ROWS

    def lanes(flow, stream):
        middle = 3 * UNIT
        return pl.ds(0, middle) if stream == 0 else pl.ds(middle, big_width(flow) - middle)

    def loads(flow, turn):
        row = chunk(flow, 0, -turn)
        return [
            pltpu.make_async_copy(hbm_block(ins, piece, row, rows), own.at[flow, pl.ds(row, rows), pl.ds(piece[2], piece[3])], load_sem.at[flow, turn, k])
            for k, piece in enumerate(big_pieces(flow))
        ]

    def copy(flow, stream, turn):
        axes, sign = FLOWS[flow]
        return pltpu.make_async_remote_copy(
            src_ref=own.at[flow, pl.ds(chunk(flow, 0, -turn), rows), lanes(flow, stream)],
            dst_ref=slots.at[flow, pl.ds(turn * rows, rows), lanes(flow, stream)],
            send_sem=send_sem.at[flow, stream, turn], recv_sem=recv_sem.at[flow, stream, turn],
            device_id=neighbour(axes[0], sign), device_id_type=MESH_ID)

    def run_op(stream, step):
        for flow in FLOW_IDS:
            if step == 0:
                if stream == 0:
                    for each in loads(flow, 0):
                        each.wait()
                continue
            copy(flow, stream, step - 1).wait_recv()
            if stream == 0:
                for each in loads(flow, step):
                    each.wait()
            row = chunk(flow, 0, -step)

            def add(i, carry):
                at = (flow, pl.ds(pl.multiple_of(row + i * PART_ROWS, PART_ROWS), PART_ROWS), lanes(flow, stream))
                total = own[at].astype(F32) + slots[flow, pl.ds(pl.multiple_of((step - 1) * rows + i * PART_ROWS, PART_ROWS), PART_ROWS), lanes(flow, stream)].astype(F32)
                if step == 3:
                    part_ref[flow, pl.ds(pl.multiple_of(i * PART_ROWS, PART_ROWS), PART_ROWS), lanes(flow, stream)] = total.astype(BF16)
                else:
                    own[at] = total.astype(BF16)
                return carry

            lax.fori_loop(0, rows // PART_ROWS, add, 0)
        if step < 3:
            for flow in FLOW_IDS:
                copy(flow, stream, step).start()

    @pl.when(pid == 0)
    def _():
        barrier = pltpu.get_barrier_semaphore()
        for axis in range(3):
            for shift in (1, 3):
                tell(barrier, neighbour(axis, shift))
        tell(barrier, partner)
        for turn in range(4):
            for flow in FLOW_IDS:
                for each in loads(flow, turn):
                    each.start()
        pl.semaphore_wait(barrier, 7)
        y_acc[ALL] = jnp.zeros_like(y_acc)
        b_acc[ALL] = jnp.zeros_like(b_acc)
        run_op(0, 0)
        run_op(1, 0)

    @pl.when(pid == steps // 2)
    def _():
        run_op(0, 1)

    @pl.when(pid == steps - steps // 4)
    def _():
        run_op(1, 1)

    peer = pid < steps // 2
    y_acc[ALL] += dot_nn(act_ref[ALL], jnp.where(peer, down_p_ref[ALL], down_o_ref[ALL]))
    b_acc[ALL] += dot_nt(dpre_ref[ALL], jnp.where(peer, up_p_ref[ALL], up_o_ref[ALL]))

    @pl.when(pid == steps - 1)
    def _():
        run_op(0, 2)

        def tile(i, carry):
            at = pl.ds(pl.multiple_of(i * UNIT, UNIT), UNIT)
            y_buf[at, :] = (x_ref[at, :].astype(F32) + y_acc[at, :].astype(BF16).astype(F32)).astype(BF16)
            db_ref[at, :] = b_acc[at, :].astype(BF16)
            return carry

        lax.fori_loop(0, x_ref.shape[0] // UNIT, tile, 0)
        y_local = pltpu.make_async_copy(y_buf, y_out.at[core], y_sem.at[0])
        y_remote = pltpu.make_async_remote_copy(
            src_ref=y_buf, dst_ref=y_out.at[core], send_sem=y_sem.at[1], recv_sem=y_sem.at[2], device_id=partner, device_id_type=MESH_ID)
        y_local.start()
        y_remote.start()
        run_op(1, 2)
        run_op(0, 3)
        run_op(1, 3)
        y_local.wait()
        y_remote.wait()
        for flow in FLOW_IDS:
            for stream in range(2):
                for turn in range(3):
                    copy(flow, stream, turn).wait_send()


def mlp_out(act, dpre, down_p, down_o, up_p, up_o, x_one, grads, tile_n=1024):
    tokens, ffn = act.shape
    hidden = x_one.shape[1]
    steps = ffn // tile_n
    any_spec = pl.BlockSpec(memory_space=pl.ANY)
    return pl.pallas_call(
        functools.partial(mlp_out_kernel, steps),
        grid=(steps,),
        in_specs=[pl.BlockSpec((tokens, tile_n), ACROSS)] * 2
        + half_specs((tile_n, hidden), steps // 2, 0) + half_specs((hidden, tile_n), steps // 2, 1) + [whole((tokens, hidden)), any_spec, any_spec],
        out_specs=[whole((tokens, hidden)), whole((N_FLOWS, TOP_ROWS, BIG_COLS)), any_spec],
        out_shape=[
            jax.ShapeDtypeStruct((tokens, hidden), BF16),
            jax.ShapeDtypeStruct((N_FLOWS, TOP_ROWS, BIG_COLS), BF16),
            jax.ShapeDtypeStruct((2, tokens, hidden), BF16),
        ],
        scratch_shapes=[
            pltpu.VMEM((N_FLOWS, FLOW_ROWS, BIG_COLS), BF16),
            pltpu.VMEM((N_FLOWS, 3 * TOP_ROWS, BIG_COLS), BF16),
            pltpu.VMEM((tokens, hidden), F32),
            pltpu.VMEM((tokens, hidden), F32),
            pltpu.VMEM((tokens, hidden), BF16),
            pltpu.SemaphoreType.DMA((N_FLOWS, 2, 3)),
            pltpu.SemaphoreType.DMA((N_FLOWS, 2, 3)),
            pltpu.SemaphoreType.DMA((N_FLOWS, 4, 2)),
            pltpu.SemaphoreType.DMA((3,)),
        ],
        compiler_params=pltpu.CompilerParams(collective_id=1, has_side_effects=True, vmem_limit_bytes=TAIL_VMEM),
        cost_estimate=cost(tokens * hidden * ffn),
        name="mlp_out",
    )(act, dpre, down_p, down_o, up_p, up_o, x_one, *grads)


def plan_ops(pairs):
    inside, after = {}, []
    for stream in range(STREAMS):
        clock = (0.0, pairs // 2 * PAIR_US, pairs * PAIR_US)[stream]
        for step in range(FIRST_STEP[stream], STEPS + 1):
            point = None
            for pair in range(pairs):
                for spot in range(POINTS):
                    at = (pair + (0.0, 0.3, 0.55, 0.8)[spot]) * PAIR_US
                    if point is None and at >= clock - 0.01:
                        point, when = (pair, spot), at
            if point is None:
                when = max(clock, pairs * PAIR_US)
                after.append((when, stream, step))
            else:
                inside.setdefault(point, []).append((stream, step))
            if step < STEPS:
                clock = when + HOP_US + STREAM_US[stream]
    after.sort()
    return inside, [(stream, step) for _, stream, step in after]


def tail_kernel(dim, scale, pairs, *refs):
    (start_ref, qkv_ref, out_ref, grad_ref, lse_ref, wp_ref, wo_ref, normed_t_ref, x_ref, gx_ref, gain_ref, gain_two_ref) = refs[:12]
    (part_ref, out_hbm), outs = refs[12:14], refs[14:16]
    out_sum, qkv_sum, dx_out, gains_out = refs[16:20]
    (own, slots, small, small_slots, sent, da_acc, dx_buf, gains, send_sem, recv_sem, load_sem, store_sem, swap_send, swap_recv, dx_sem, gain_send, gain_recv, free_sem) = refs[20:]
    pid = pl.program_id(0)
    half = pairs // 2
    core = lax.axis_index("tp")
    coords, neighbour, chunk = ring_tools()
    inside, after = plan_ops(pairs)
    partner = {"tp": 1 - core}

    def view(of_slots, flow, stream, row, rows):
        if stream == 0:
            if of_slots:
                return slots.at[flow, pl.ds(row - BIG_SLOT_BASE, rows), pl.ds(0, big_width(flow))]
            return own.at[flow, pl.ds(row, rows), pl.ds(0, big_width(flow))]
        first, last = SMALL_BOUNDS[stream][flow : flow + 2]
        units = pl.ds(first, last - first)
        return (small_slots if of_slots else small).at[units, pl.ds(row, rows), :]

    def loads():
        copies = []
        for flow in FLOW_IDS:
            target = own.at[flow, pl.ds(chunk(flow, 0, 1), TOP_ROWS), :]
            copies.append(pltpu.make_async_copy(part_ref.at[flow], target, load_sem.at[flow]))
        for k in range(4):
            for side in range(2):
                source = out_hbm.at[:, pl.ds((4 * side + k) * UNIT, UNIT)]
                target = small.at[OUT_FIRST + k, pl.ds(side * 512, 512), :]
                copies.append(pltpu.make_async_copy(source, target, load_sem.at[6 + 2 * k + side]))
        return copies

    def stores(flow, stream, turn):
        row = chunk(flow, 0, 1 - turn)
        rows = TOP_ROWS
        copies = []
        if stream > 0:
            for k, index in enumerate(range(*SMALL_BOUNDS[stream][flow : flow + 2])):
                if OUT_FIRST <= index < OUT_FIRST + 4:
                    side = row // 512
                    lane = pl.multiple_of(side * 512 + (index - OUT_FIRST) * UNIT, UNIT)
                    target = out_sum.at[pl.ds(pl.multiple_of(row - side * 512, rows), rows), pl.ds(lane, UNIT)]
                else:
                    unit = index if index < OUT_FIRST else index - 4
                    target = qkv_sum.at[pl.ds(row, rows), pl.ds(unit * UNIT, UNIT)]
                copies.append(pltpu.make_async_copy(small.at[index, pl.ds(row, rows), :], target, store_sem.at[flow, stream, turn, k]))
            return copies
        for k, piece in enumerate(big_pieces(flow)):
            source = own.at[flow, pl.ds(row, rows), pl.ds(piece[2], piece[3])]
            copies.append(pltpu.make_async_copy(source, hbm_block(outs, piece, row, rows), store_sem.at[flow, stream, turn, k]))
        return copies

    def remote(flow, stream, source, target, index, axis, shift):
        return pltpu.make_async_remote_copy(
            src_ref=source, dst_ref=target, send_sem=send_sem.at[flow, stream, index], recv_sem=recv_sem.at[flow, stream, index],
            device_id=neighbour(axis, shift), device_id_type=MESH_ID)

    def direct_level(step):
        return step - 2 if step < 5 else 7 - step

    def copies(flow, stream, step):
        axes, sign = FLOWS[flow]
        if step < 3:
            rows = TOP_ROWS
            source = view(False, flow, stream, chunk(flow, 0, -step), rows)
            return [remote(flow, stream, source, view(True, flow, stream, step * rows, rows), step, axes[0], sign)]
        if step >= 7:
            source = view(False, flow, stream, chunk(flow, 0, 8 - step), TOP_ROWS)
            return [remote(flow, stream, source, source, step + 8, axes[0], sign)]
        level = direct_level(step)
        rows = LEVEL_ROWS[level]
        sends = []
        for d in PEERS:
            source = view(False, flow, stream, chunk(flow, level, d + 1 if step < 5 else 1), rows)
            target = view(True, flow, stream, LEVEL_SLOT[level] + (d - 1) * rows, rows) if step < 5 else source
            sends.append(remote(flow, stream, source, target, 3 * step - 7 + d, axes[level], sign * d))
        return sends

    def absorb(flow, stream, step):
        for each in copies(flow, stream, step):
            each.wait_recv()
        if step >= 6:
            for each in stores(flow, stream, step - 6):
                each.start()
        if step >= 5:
            return
        if step < 3:
            level, row, brought = 0, chunk(flow, 0, -step - 1), (step,)
        else:
            level = direct_level(step)
            row, brought = chunk(flow, level, 1), (0, 1, 2)
        rows = LEVEL_ROWS[level]
        part = min(rows, PART_ROWS)

        def add(i, carry):
            kept = view(False, flow, stream, pl.multiple_of(row + i * part, 16), part)
            total = kept[ALL].astype(F32)
            for slot in brought:
                total = total + view(True, flow, stream, pl.multiple_of(LEVEL_SLOT[level] + slot * rows + i * part, 16), part)[ALL].astype(F32)
            kept[ALL] = total.astype(BF16)
            return carry

        if rows == part:
            add(0, 0)
        else:
            lax.fori_loop(0, rows // part, add, 0)

    def give(flow, stream, level):
        axes, sign = FLOWS[flow]
        for step in (0, 1, 2) if level == 0 else (level + 2,):
            for each in copies(flow, stream, step):
                each.wait_send()
        for shift in (-sign,) if level == 0 else PEERS:
            tell(free_sem.at[flow, stream, level], neighbour(axes[level], shift))

    def run_op(stream, step):
        ring = stream > 0
        for flow in FLOW_IDS:
            if step > FIRST_STEP[stream]:
                absorb(flow, stream, step - 1)
        for flow in FLOW_IDS:
            if step == 4 and ring:
                give(flow, stream, 0)
            if step == 5:
                give(flow, stream, 1)
                give(flow, stream, 2)
        for flow in FLOW_IDS:
            if step == 5:
                pl.semaphore_wait(free_sem.at[flow, stream, 2], 3)
            if step == 6:
                pl.semaphore_wait(free_sem.at[flow, stream, 1], 3)
            if step == 7 and ring:
                pl.semaphore_wait(free_sem.at[flow, stream, 0], 1)
        if step < STEPS:
            for flow in FLOW_IDS:
                for each in copies(flow, stream, step):
                    each.start()

    def run_point(spot):
        for pair in range(pairs):
            ops = inside.get((pair, spot), [])
            if ops:
                @pl.when(pid == pair)
                def _():
                    for stream, step in ops:
                        run_op(stream, step)

    own_turn = lax.rem(pid, 2) == 1
    spot = pid // 2

    def slot_of(j):
        return 3 * j + 4 * (j // 2)

    def swap_copy(j):
        return pltpu.make_async_remote_copy(
            src_ref=sent.at[j % 2 if isinstance(j, int) else lax.rem(j, 2)], dst_ref=small.at[pl.ds(slot_of(j), 3)],
            send_sem=swap_send.at[j], recv_sem=swap_recv.at[j], device_id=partner, device_id_type=MESH_ID)

    @pl.when(pid == 0)
    def _():
        barrier = pltpu.get_barrier_semaphore()
        for axis in range(3):
            for shift in PEERS:
                tell(barrier, neighbour(axis, shift))
        tell(barrier, partner)
        for each in loads():
            each.start()
        pl.semaphore_wait(barrier, 10)
        for each in loads():
            each.wait()
        da_acc[ALL] = jnp.zeros_like(da_acc)

    run_point(0)
    block = qkv_ref[ALL]
    block_t = block.T
    grad = grad_ref[ALL]
    grad_t = grad.T
    prod_t = grad_t.astype(F32) * out_ref[ALL].T.astype(F32)
    start = start_ref[0:1, :]
    pieces = attn_bwd_head(dim, scale, 0, block, block_t, grad, grad_t, prod_t, start, lse_ref[0, 0:1, :])
    run_point(1)
    pieces += attn_bwd_head(dim, scale, 1, block, block_t, grad, grad_t, prod_t, start, lse_ref[0, 1:2, :])
    dqkv = jnp.concatenate(pieces, axis=1).astype(BF16)
    run_point(2)
    weight = jnp.where(own_turn, wo_ref[ALL], wp_ref[ALL])
    da_acc[ALL] += dot_nt(dqkv, weight)
    run_point(3)

    @pl.when(jnp.logical_not(own_turn))
    def _():
        @pl.when(spot >= 2)
        def _():
            swap_copy(spot - 2).wait_send()

        dw = dot_nn(normed_t_ref[ALL], dqkv).astype(BF16)
        for k in range(3):
            sent[lax.rem(spot, 2), k] = dw[:, k * UNIT : (k + 1) * UNIT]
        swap_copy(spot).start()

    @pl.when(own_turn)
    def _():
        dw = dot_nn(normed_t_ref[ALL], dqkv)
        swap_copy(spot).wait_recv()
        for k in range(3):
            index = slot_of(spot) + k
            small[index] = (dw[:, k * UNIT : (k + 1) * UNIT] + small[index].astype(F32)).astype(BF16)

    @pl.when(pid == pairs - 1)
    def _():
        queue = list(after)

        def advance(count):
            for _ in range(min(count, len(queue))):
                run_op(*queue.pop(0))

        advance(1)
        gain = gain_ref[0:1, :]

        def norm_tile(i, total):
            at = pl.ds(pl.multiple_of(i * UNIT, UNIT), UNIT)
            x_tile = x_ref[at, :]
            mean, inv_std = norm_stats(x_tile)
            back, gain_part = norm_backward(da_acc[at, :].astype(BF16), x_tile, mean, inv_std, gain)
            dx_buf[at, :] = (gx_ref[at, :].astype(F32) + back).astype(BF16)
            return total + gain_part

        gain_one = lax.fori_loop(0, x_ref.shape[0] // UNIT, norm_tile, jnp.zeros_like(gain))
        for k in range(8):
            gains[0, core, k : k + 1, :] = gain_one[:, k * UNIT : (k + 1) * UNIT]
            gains[0, core, k + 8 : k + 9, :] = gain_two_ref[0:1, k * UNIT : (k + 1) * UNIT]
        advance(1)
        dx_local = pltpu.make_async_copy(dx_buf, dx_out.at[core], dx_sem.at[0])
        dx_remote = pltpu.make_async_remote_copy(
            src_ref=dx_buf, dst_ref=dx_out.at[core], send_sem=dx_sem.at[1], recv_sem=dx_sem.at[2], device_id=partner, device_id_type=MESH_ID)
        dx_local.start()
        dx_remote.start()

        def gain_copy(stage, slot, where_to, lane):
            return pltpu.make_async_remote_copy(
                src_ref=gains.at[stage, slot], dst_ref=gains.at[stage, slot], send_sem=gain_send.at[stage, lane], recv_sem=gain_recv.at[stage, slot],
                device_id=where_to, device_id_type=MESH_ID)

        for stage in range(4):
            if stage == 0:
                members, spot = 2, core
                others = [(partner, 1 - core)]
            else:
                members, spot = RING, coords[stage - 1]
                others = [(neighbour(stage - 1, d), lax.rem(spot + d, RING)) for d in PEERS]
            for lane, (target, _) in enumerate(others):
                gain_copy(stage, spot, target, lane).start()
            advance(2)
            for lane, (target, slot) in enumerate(others):
                gain_copy(stage, slot, target, lane).wait_recv()
                gain_copy(stage, spot, target, lane).wait_send()
            total = gains[stage, 0]
            for member in range(1, members):
                total = total + gains[stage, member]
            if stage < 3:
                gains[stage + 1, coords[stage]] = total
            else:
                gains_out[ALL] = total
        advance(len(queue))
        swap_copy(half - 2).wait_send()
        swap_copy(half - 1).wait_send()
        dx_local.wait()
        dx_remote.wait()
        for stream in range(STREAMS):
            for flow in FLOW_IDS:
                for step in range(5, STEPS):
                    for each in copies(flow, stream, step):
                        each.wait_send()
                for turn in range(4):
                    for each in stores(flow, stream, turn):
                        each.wait()


def backward_tail(dim, scale, start, qkv, out, grad, lse, w_peer, w_own, normed_t, x_rows, gx_rows, gain_one, gain_two_grad, part, grads_out, big_shapes):
    seq, hidden = x_rows.shape
    width = 6 * dim
    half = w_own.shape[1] // width
    pairs = 2 * half
    any_spec = pl.BlockSpec(memory_space=pl.ANY)
    by_pair = lambda i: (0, order(i))
    order = lambda i: lax.rem(i, 2) * half + i // 2
    row = lambda value: jnp.broadcast_to(value.astype(F32), (8, hidden))
    return pl.pallas_call(
        functools.partial(tail_kernel, dim, scale, pairs),
        grid=(pairs,),
        in_specs=[
            whole((8, seq)),
            pl.BlockSpec((seq, width), by_pair),
            pl.BlockSpec((seq, 2 * dim), by_pair),
            pl.BlockSpec((seq, 2 * dim), by_pair),
            pl.BlockSpec((1, 8, seq), lambda i: (order(i), 0, 0)),
            *[pl.BlockSpec((hidden, width), lambda i: (0, i // 2))] * 2,
            whole((hidden, seq)),
            whole((seq, hidden)),
            whole((seq, hidden)),
            whole((8, hidden)),
            whole((8, hidden)),
        ] + [any_spec] * 2,
        out_specs=[any_spec] * 5 + [pl.BlockSpec((16, UNIT), FIRST)],
        out_shape=[jax.ShapeDtypeStruct(shape, BF16) for shape in (*big_shapes, grads_out.shape)] + [
            jax.ShapeDtypeStruct((hidden, half * width), BF16),
            jax.ShapeDtypeStruct((2, seq, hidden), BF16),
            jax.ShapeDtypeStruct((16, UNIT), F32),
        ],
        scratch_shapes=[
            pltpu.VMEM((N_FLOWS, FLOW_ROWS, BIG_COLS), BF16),
            pltpu.VMEM((N_FLOWS, SLOT_ROWS - BIG_SLOT_BASE, BIG_COLS), BF16),
            pltpu.VMEM((16, FLOW_ROWS, UNIT), BF16),
            pltpu.VMEM((16, SLOT_ROWS, UNIT), BF16),
            pltpu.VMEM((2, 3, FLOW_ROWS, UNIT), BF16),
            pltpu.VMEM((seq, hidden), F32),
            pltpu.VMEM((seq, hidden), BF16),
            pltpu.VMEM((4, RING, 16, UNIT), F32),
            pltpu.SemaphoreType.DMA((N_FLOWS, STREAMS, SEMS)),
            pltpu.SemaphoreType.DMA((N_FLOWS, STREAMS, SEMS)),
            pltpu.SemaphoreType.DMA((14,)),
            pltpu.SemaphoreType.DMA((N_FLOWS, STREAMS, 4, 3)),
            pltpu.SemaphoreType.DMA((half,)),
            pltpu.SemaphoreType.DMA((half,)),
            pltpu.SemaphoreType.DMA((3,)),
            pltpu.SemaphoreType.DMA((4, 3)),
            pltpu.SemaphoreType.DMA((4, RING)),
            pltpu.SemaphoreType.REGULAR((N_FLOWS, STREAMS, 3)),
        ],
        compiler_params=pltpu.CompilerParams(collective_id=0, has_side_effects=True, vmem_limit_bytes=TAIL_VMEM),
        cost_estimate=cost(pairs * seq * seq * hidden),
        name="backward_tail",
    )(start, qkv, out, grad, lse, w_peer, w_own, normed_t, x_rows, gx_rows, row(gain_one[None, :]), row(gain_two_grad), part, grads_out)


def solution(mesh):
    batch_spec = P(("pod", "dp"))
    columns = P(None, "tp")

    def local_step(x_in, seg_ids, gain_one, gain_two, w_qkv, w_out, w_up, w_down, grad_y):
        heads_loc, dim, hidden = w_out.shape
        scale = dim ** -0.5
        swap = lambda value: lax.ppermute(value, "tp", SWAP)
        mine = lax.axis_index("tp")
        own_row = lambda value: lax.dynamic_index_in_dim(value, mine, 0, keepdims=False)

        w_out = w_out.reshape(heads_loc * dim, hidden)
        wqkv_p = swap(w_qkv)
        wout_p = swap(w_out)
        wup_p = swap(w_up)
        wdown_p = swap(w_down)
        x_rows = own_row(x_in)
        grad_rows = own_row(grad_y)
        seg = own_row(seg_ids)
        seq = x_rows.shape[0]
        start = jnp.sum((seg[None, :] < seg[:, None]).astype(jnp.int32), axis=1)
        start = jnp.broadcast_to(start[None, :], (8, seq))

        mean_a, inv_a = norm_stats(x_rows)
        normed_a = norm_apply(x_rows, mean_a, inv_a, gain_one)
        qkv, attn, lse, normed_t = attention_forward(start, normed_a, wqkv_p, w_qkv, dim, scale)
        wout_all = jnp.concatenate([wout_p, w_out], axis=0)
        part_one = dot_nn(attn, wout_all).astype(BF16)
        x_one = (x_rows.astype(F32) + part_one.astype(F32)).astype(BF16)
        mean_b, inv_b = norm_stats(x_one)
        normed_b = norm_apply(x_one, mean_b, inv_b, gain_two)

        ffn_loc = w_up.shape[1]
        act, dpre = mlp_mid(normed_b, grad_rows, wup_p, w_up, wdown_p, w_down)
        sent_down = swap(dot_tn(act[:, :ffn_loc], grad_rows).astype(BF16))
        sent_up = swap(dot_tn(normed_b, dpre[:, :ffn_loc]).astype(BF16))
        grad_down = (dot_tn(act[:, ffn_loc:], grad_rows) + sent_down.astype(F32)).astype(BF16)
        grad_up = (dot_tn(normed_b, dpre[:, ffn_loc:]) + sent_up.astype(F32)).astype(BF16)
        grad_norm_b, part, y_out = mlp_out(act, dpre, wdown_p, w_down, wup_p, w_up, x_one, (grad_up, grad_down))
        back_b, gain_grad_two = norm_backward(grad_norm_b, x_one, mean_b, inv_b, gain_two)
        grad_x_one = (grad_rows.astype(F32) + back_b).astype(BF16)
        grad_wout = dot_tn(attn, grad_x_one)
        rows_loc = heads_loc * dim
        sent_out = swap(grad_wout[:rows_loc].astype(BF16))
        grad_out_w = (grad_wout[rows_loc:] + sent_out.astype(F32)).astype(BF16)
        dattn = dot_nt(grad_x_one, wout_all).astype(BF16)

        sum_up, sum_down, sum_out, sum_qkv, grad_x, gain_sums = backward_tail(
            dim, scale, start, qkv, attn, dattn, lse, wqkv_p, w_qkv, normed_t, x_rows, grad_x_one, gain_one, gain_grad_two, part, grad_out_w, (grad_up.shape, grad_down.shape))
        gain_sums = gain_sums.reshape(2, hidden).astype(BF16)
        return (
            y_out,
            grad_x,
            gain_sums[0],
            gain_sums[1],
            sum_qkv,
            sum_out.reshape(heads_loc, dim, hidden),
            sum_up,
            sum_down,
        )

    return jax.shard_map(
        local_step,
        mesh=mesh,
        in_specs=(batch_spec, batch_spec, P(), P(), columns, P("tp"), columns, P("tp"), batch_spec),
        out_specs=(batch_spec, batch_spec, P("pod"), P("pod"), P("pod", "tp"), P(("pod", "tp")), P("pod", "tp"), P(("pod", "tp"))),
        check_vma=False,
    )
```

time: 382 us -> 346 us (0.906)
  matrix products: 71.8 us -> 38.5 us
  other arithmetic: 28.7 us -> 17.9 us
  Pallas kernels: 251 us -> 256 us
    pallas_call x2, Pallas kernels: 32.9 us -> 72.1 us  [the longest x1 46.9 us: mlp_out(): pl.pallas_call(functools.partial(mlp_out_kernel, steps), grid=(steps,), i...]
    pallas_call x1, Pallas kernels: 168 us -> 146 us  [backward_tail(): pl.pallas_call(functools.partial(tail_kernel, dim, scale, pairs), grid=(p...]
    dot_general x3 -> x1, matrix products: 20.2 us -> 4.93 us  [dot_nt(): lax.dot_general(lhs, rhs, (((1,), (1,)), ((), ())), preferred_element_typ...]
    dot_general x3 -> x1, matrix products: 17.6 us -> 4.28 us  [dot_nn(): lax.dot_general(lhs, rhs, (((1,), (0,)), ((), ())), preferred_element_typ...]
    convert_element_type x2 -> x0, other arithmetic: 13.2 us -> none  [the longest x1 7.22 us: local_step(): grad_down = (dot_tn(act_o, grad_rows) + sent_down.astype(F32)).astype(BF16)]
    pallas_call x1, Pallas kernels: 50.6 us -> 38.7 us  [attention_forward(): pl.pallas_call(functools.partial(attn_fwd_kernel, dim, scale), grid=(pair...]
    dot_general x5, matrix products: 33.9 us -> 29.3 us  [dot_tn(): lax.dot_general(lhs, rhs, (((0,), (0,)), ((), ())), preferred_element_typ...]
    unnamed x61 -> x50, local copies, waits for them, and re-layouts: 18.1 us -> 20.1 us
  transfers between devices with their start and end apart: 8 -> 7, of which waited for: 0 -> 1; matrix products, arithmetic and copies ran while one was open for 21% -> 10% of each run, Pallas kernels for 18% -> 11%
where the time goes in v3:
time: 346 us; the launch traced here: 342 us
  Pallas kernels  256 us (74%)
  matrix products  38.5 us (11%)
  local copies, waits for them, and re-layouts  24.2 us (7%)
  other arithmetic  17.9 us (5%)
    pallas_call x1, Pallas kernels, backward_tail(): pl.pallas_call(functools.partial(tail_kernel, dim, scale, pairs), grid=(p...  146 us
    pallas_call x1, Pallas kernels, mlp_out(): pl.pallas_call(functools.partial(mlp_out_kernel, steps), grid=(steps,), i...  46.9 us
    pallas_call x1, Pallas kernels, attention_forward(): pl.pallas_call(functools.partial(attn_fwd_kernel, dim, scale), grid=(pair...  38.7 us
    dot_general x5, matrix products, dot_tn(): lax.dot_general(lhs, rhs, (((0,), (0,)), ((), ())), preferred_element_typ...  29.3 us
    pallas_call x1, Pallas kernels, mlp_mid(): pl.pallas_call(functools.partial(mlp_mid_kernel, rows), grid=(2 * half,),...  25.2 us
    unnamed x50, local copies, waits for them, and re-layouts  20.1 us
  transfers between devices with their start and end apart: 7, of which 1 were waited for; matrix products, arithmetic and copies ran while one was open for 10% of the time, Pallas kernels for 11%

profile of v3, /device:TPU:0, one launch (start us, length us, event | category | flops | bytes accessed | tf_op | source)
XLA Modules:
  0.0 342.1 jit_solution(13707750839914100717)
XLA Ops:
  2.4 1.9 convert_reduce_fusion
  4.4 0.7 fusion.9
  5.1 2.0 fusion.11.normed_ref
  8.1 1.5 dynamic-slice_bitcast_fusion.dy_ref
  10.3 1.0 copy-done.17
  11.3 38.7 %attn_fwd.1 = (bf16[1024,3072]{1,0:T(8,128)(2,1)}, bf16[1024,1024]{1,0:T(8,128)(2,1)}, f32[8,8,1024]{2,1,0:T(8,128)}, bf16[1024,1024]{1,0:T(8,128)(2,1)}) custom-call(s32[8,1024]{1,0:T(8,128)} %broadcast_in_dim.6.start_ref.refs_0_, bf16[1024,1024]{1,0:T(8,128)(2,1)} %fusion.11.normed_ref, bf16[1024,1536]{1,0:T(8,128)(2,1)} %copy-done.17, ...), custom_call_target="tpu_custom_call" | custom-call | flops 8589934592 | bytes 67108864 | tf_op jit(solution)/shard_map/attn_fwd/pallas_call | solution.py:120
  50.0 4.3 %convert_reduce_fusion.1 = (f32[1024]{0:T(1024)S(1)}, bf16[1024,1024]{1,0:T(8,128)(2,1)S(1)}) fusion(bf16[1024,1024]{1,0:T(8,128)(2,1)} %get-tuple-element.23.refs_2_, bf16[512,1024]{1,0:T(8,128)(2,1)S(1)} %bitcast.25, bf16[512,1024]{1,0:T(8,128)(2,1)} %collective-permute-done.1, bf16[1024,1024]{1,0:T(8,128)(2,1)S(1)} %get-tuple-element.42.refs_8_), kind=kOutput, calls=%fused_computation.11 | convolution fusion | flops 2159016960 | bytes 8392704 | tf_op jit(solution)/shard_map/dot_general | solution.py:52
  54.3 0.7 fusion.17
  55.7 2.0 fusion.12.b_ref
  57.7 25.2 %mlp_mid.1 = (bf16[1024,4096]{1,0:T(8,128)(2,1)}, bf16[1024,4096]{1,0:T(8,128)(2,1)}) custom-call(bf16[1024,1024]{1,0:T(8,128)(2,1)} %fusion.12.b_ref, bf16[1024,1024]{1,0:T(8,128)(2,1)} %dynamic-slice_bitcast_fusion.dy_ref, bf16[1024,2048]{1,0:T(8,128)(2,1)} %collective-permute-done.2.up_p_ref, bf16[1024,2048]{1,0:T(8,128)(2,1)} %up_o_ref.3, ...), custom_call_target="tpu_custom_call" | custom-call | flops 4294967296 | bytes 33554432 | tf_op jit(solution)/shard_map/mlp_mid/pallas_call | solution.py:217
  82.9 7.2 %fusion.32 = bf16[2048,1024]{1,0:T(8,128)(2,1)S(1)} fusion(bf16[1024,1024]{1,0:T(8,128)(2,1)S(1)} %copy-done.12, bf16[1024,4096]{1,0:T(8,128)(2,1)} %get-tuple-element.24.act_ref), kind=kOutput, calls=%fused_computation.40 | convolution fusion | flops 4297064448 | bytes 10485760 | tf_op jit(solution)/shard_map/dot_general | solution.py:60
  90.7 4.9 %fusion.29 = bf16[1024,2048]{1,0:T(8,128)(2,1)S(1)} fusion(bf16[1024,1024]{1,0:T(8,128)(2,1)S(1)} %copy-done.11, bf16[1024,4096]{1,0:T(8,128)(2,1)S(1)} %copy-done.21), kind=kOutput, calls=%fused_computation.39 | convolution fusion | flops 4297064448 | bytes 10485760 | tf_op jit(solution)/shard_map/dot_general | solution.py:60
  96.1 1.7 collective-permute-done.5
  97.8 8.5 %add_convert_fusion.down_hbm = bf16[2048,1024]{1,0:T(8,128)(2,1)} fusion(bf16[2048,1024]{1,0:T(8,128)(2,1)S(1)} %collective-permute-done.5, bf16[1024,1024]{1,0:T(8,128)(2,1)S(1)} %copy-done.12, bf16[1024,4096]{1,0:T(8,128)(2,1)} %get-tuple-element.24.act_ref), kind=kOutput, calls=%fused_computation | convolution fusion | flops 4301258752 | bytes 14680064 | tf_op jit(solution)/shard_map/dot_general | solution.py:60
  106.2 6.3 %add_convert_fusion.1.up_hbm = bf16[1024,2048]{1,0:T(8,128)(2,1)} fusion(bf16[1024,2048]{1,0:T(8,128)(2,1)S(1)} %collective-permute-done.4, bf16[1024,1024]{1,0:T(8,128)(2,1)S(1)} %copy-done.11, bf16[1024,4096]{1,0:T(8,128)(2,1)S(1)} %copy-done.21), kind=kOutput, calls=%fused_computation.1 | convolution fusion | flops 4301258752 | bytes 14680064 | tf_op jit(solution)/shard_map/dot_general | solution.py:60
  112.5 46.9 %mlp_out.1 = (bf16[1024,1024]{1,0:T(8,128)(2,1)}, bf16[6,256,768]{2,1,0:T(8,128)(2,1)}, bf16[2,1024,1024]{2,1,0:T(8,128)(2,1)}) custom-call(bf16[1024,4096]{1,0:T(8,128)(2,1)} %get-tuple-element.24.act_ref, bf16[1024,4096]{1,0:T(8,128)(2,1)} %get-tuple-element.25.dpre_ref, bf16[2048,1024]{1,0:T(8,128)(2,1)} %collective-permute-done.3.down_p_ref, ...), custom_call_target="tpu_custom_call" | custom-call | flops 4294967296 | bytes 33554432 | tf_op jit(solution)/shard_map/mlp_out/pallas_call | solution.py:423
  159.5 3.8 %fusion.19 = (f32[1024]{0:T(1024)S(1)}, f32[1024]{0:T(1024)S(1)}, f32[1024]{0:T(1024)S(1)}) fusion(bf16[1024,1024]{1,0:T(8,128)(2,1)} %copy-done.2, bf16[1024,1024]{1,0:T(8,128)(2,1)} %get-tuple-element.28, f32[1024]{0:T(1024)S(1)} %add_rsqrt_fusion, f32[1024]{0:T(1024)S(1)} %broadcast_multiply_fusion.2, f32[1024]{0:T(1024)S(1)} %convert_element_type.86), kind=kLoop, calls=%fused_computation.28 | loop fusion | flops 10482688 | bytes 4218880 | tf_op jit(solution)/shard_map/reduce_sum | solution.py:40
  163.3 3.5 %fusion.16.refs_9_ = bf16[1024,1024]{1,0:T(8,128)(2,1)S(1)} fusion(bf16[1024,1024]{1,0:T(8,128)(2,1)S(1)} %copy-done.3, bf16[1024,1024]{1,0:T(8,128)(2,1)S(1)} %copy-done.5, f32[1024]{0:T(1024)S(1)} %get-tuple-element.47, f32[1024]{0:T(1024)S(1)} %get-tuple-element.48, f32[1024]{0:T(1024)S(1)} %convert_element_type.86, f32[1024]{0:T(1024)S(1)} %add_rsqrt_fusion, ...), kind=kLoop, calls=%fused_computation.25 | loop fusion | flops 12582912 | bytes 8409092 | tf_op jit(solution)/shard_map/convert_element_type | solution.py:848
  166.8 2.4 fusion.42
  169.5 4.9 %convolution_convert_fusion.refs_3_ = bf16[1024,1024]{1,0:T(8,128)(2,1)} fusion(bf16[1024,1024]{1,0:T(8,128)(2,1)S(1)} %fusion.16.refs_9_, bf16[512,1024]{1,0:T(8,128)(2,1)S(1)} %bitcast.26, bf16[512,1024]{1,0:T(8,128)(2,1)} %collective-permute-done.1), kind=kOutput, calls=%fused_computation.47 | convolution fusion | flops 2152726528 | bytes 6291456 | tf_op jit(solution)/shard_map/dot_general | solution.py:56
  174.5 1.3 fusion.39.refs_13_
  177.1 145.6 %backward_tail.1 = (bf16[1024,2048]{1,0:T(8,128)(2,1)}, bf16[2048,1024]{1,0:T(8,128)(2,1)}, bf16[512,1024]{1,0:T(8,128)(2,1)}, bf16[1024,1536]{1,0:T(8,128)(2,1)...) custom-call(s32[8,1024]{1,0:T(8,128)} %broadcast_in_dim.6.start_ref.refs_0_, ...), custom_call_target="tpu_custom_call" | custom-call | flops 8589934592 | bytes 67108864 | tf_op jit(solution)/shard_map/backward_tail/pallas_call | solution.py:760
  322.6 0.7 convert_element_type.100
  323.9 4.8 %copy.26 = bf16[2,1024,1024]{2,1,0:T(8,128)(2,1)} copy(bf16[2,1024,1024]{2,1,0:T(8,128)(2,1)} %get-tuple-element.57) | data formatting | bytes 8388608
  328.8 2.1 copy.27
  330.9 1.3 copy-done.10
  332.2 1.7 copy.28
  334.1 1.0 copy.29
  335.1 1.1 copy-done.7
  336.2 2.1 copy.30
  338.3 1.6 copy-done.6
  339.9 2.0 copy.31
  (67 shorter events, 7.6 us)
Async XLA Ops:
  0.6 1.8 copy-start
  0.6 9.0 %collective-permute-start = (bf16[1024,1536]{1,0:T(8,128)(2,1)}, bf16[1024,1536]{1,0:T(8,128)(2,1)S(1)}, u32[]{:S(2)}, u32[]{:S(2)}) collective-permute-start(bf16[1024,1536]{1,0:T(8,128)(2,1)} %refs_6_.1), channel_id=1, source_target_pairs={{0,1},{1,0},{2,3},{3,2},{4,5},{5,4},{6,7},{7,6},{8,9},{9,8},{10,11... | collective-permute-start | bytes 9437192 | tf_op jit(solution)/shard_map/ppermute | solution.py:815
  0.7 57.0 %collective-permute-start.2 = (bf16[1024,2048]{1,0:T(8,128)(2,1)}, bf16[1024,2048]{1,0:T(8,128)(2,1)}, u32[]{:S(2)}, u32[]{:S(2)}) collective-permute-start(bf16[1024,2048]{1,0:T(8,128)(2,1)} %up_o_ref.3), channel_id=1, source_target_pairs={{0,1},{1,0},{2,3},{3,2},{4,5},{5,4},{6,7},{7,6},{8,9},{9,8},{10,11... | collective-permute-start | bytes 12582920 | tf_op jit(solution)/shard_map/ppermute | solution.py:815
  1.2 56.5 %collective-permute-start.3 = (bf16[2048,1024]{1,0:T(8,128)(2,1)}, bf16[2048,1024]{1,0:T(8,128)(2,1)}, u32[]{:S(2)}, u32[]{:S(2)}) collective-permute-start(bf16[2048,1024]{1,0:T(8,128)(2,1)} %down_o_ref.3), channel_id=1, source_target_pairs={{0,1},{1,0},{2,3},{3,2},{4,5},{5,4},{6,7},{7,6},{8,9},{9,8},{10,11... | collective-permute-start | bytes 12582920 | tf_op jit(solution)/shard_map/ppermute | solution.py:815
  1.3 48.7 %collective-permute-start.1 = (bf16[512,1024]{1,0:T(8,128)(2,1)}, bf16[512,1024]{1,0:T(8,128)(2,1)}, u32[]{:S(2)}, u32[]{:S(2)}) collective-permute-start(bf16[512,1024]{1,0:T(8,128)(2,1)} %bitcast.24), channel_id=1, source_target_pairs={{0,1},{1,0},{2,3},{3,2},{4,5},{5,4},{6,7},{7,6},{8,9},{9,8},{10,11... | collective-permute-start | bytes 3145736 | tf_op jit(solution)/shard_map/ppermute | solution.py:815
  4.4 45.6 %copy-start.4 = (bf16[1024,1024]{1,0:T(8,128)(2,1)}, bf16[1024,1024]{1,0:T(8,128)(2,1)S(1)}, u32[]{:S(2)}) copy-start(bf16[1024,1024]{1,0:T(8,128)(2,1)S(1)} %get-tuple-element.42.refs_8_) | copy-start | bytes 6291460
  4.4 3.3 copy-start.16
  4.4 3.7 %copy-start.9 = (bf16[2,1024,1024]{2,1,0:T(8,128)(2,1)S(1)}, bf16[2,1024,1024]{2,1,0:T(8,128)(2,1)}, u32[]{:S(2)}) copy-start(bf16[2,1024,1024]{2,1,0:T(8,128)(2,1)} %param.17) | copy-start | bytes 12582916
  9.6 1.7 copy-start.17
  11.3 38.7 %copy-start.18 = (bf16[8,64,1024]{2,1,0:T(8,128)(2,1)S(1)}, bf16[8,64,1024]{2,1,0:T(8,128)(2,1)}, u32[]{:S(2)}) copy-start(bf16[8,64,1024]{2,1,0:T(8,128)(2,1)} %param.14) | copy-start | bytes 3145732
  54.3 1.4 copy-start.2
  57.7 25.2 %copy-start.12 = (bf16[1024,1024]{1,0:T(8,128)(2,1)S(1)}, bf16[1024,1024]{1,0:T(8,128)(2,1)}, u32[]{:S(2)}) copy-start(bf16[1024,1024]{1,0:T(8,128)(2,1)} %dynamic-slice_bitcast_fusion.dy_ref) | copy-start | bytes 6291460
  82.9 7.8 %copy-start.11 = (bf16[1024,1024]{1,0:T(8,128)(2,1)S(1)}, bf16[1024,1024]{1,0:T(8,128)(2,1)}, u32[]{:S(2)}) copy-start(bf16[1024,1024]{1,0:T(8,128)(2,1)} %fusion.12.b_ref) | copy-start | bytes 6291460
  82.9 7.8 %copy-start.21 = (bf16[1024,4096]{1,0:T(8,128)(2,1)S(1)}, bf16[1024,4096]{1,0:T(8,128)(2,1)}, u32[]{:S(2)}) copy-start(bf16[1024,4096]{1,0:T(8,128)(2,1)} %get-tuple-element.25.dpre_ref) | copy-start | bytes 25165828
  90.1 7.6 %collective-permute-start.5 = (bf16[2048,1024]{1,0:T(8,128)(2,1)S(1)}, bf16[2048,1024]{1,0:T(8,128)(2,1)S(1)}, u32[]{:S(2)}, u32[]{:S(2)}) collective-permute-start(bf16[2048,1024]{1,0:T(8,128)(2,1)S(1)} %fusion.32), channel_id=1, source_target_pairs={{0,1},{1,0},{2,3},{3,2},{4,5},{5,4},{6,7},{7,6},{8,9},{9,8},{10,11... | collective-permute-start | bytes 12582920 | tf_op jit(solution)/shard_map/ppermute | solution.py:815
  95.6 10.6 %collective-permute-start.4 = (bf16[1024,2048]{1,0:T(8,128)(2,1)S(1)}, bf16[1024,2048]{1,0:T(8,128)(2,1)S(1)}, u32[]{:S(2)}, u32[]{:S(2)}) collective-permute-start(bf16[1024,2048]{1,0:T(8,128)(2,1)S(1)} %fusion.29), channel_id=1, source_target_pairs={{0,1},{1,0},{2,3},{3,2},{4,5},{5,4},{6,7},{7,6},{8,9},{9,8},{10,11... | collective-permute-start | bytes 12582920 | tf_op jit(solution)/shard_map/ppermute | solution.py:815
  159.5 3.8 %copy-start.3 = (bf16[1024,1024]{1,0:T(8,128)(2,1)S(1)}, bf16[1024,1024]{1,0:T(8,128)(2,1)}, u32[]{:S(2)}) copy-start(bf16[1024,1024]{1,0:T(8,128)(2,1)} %copy-done.2) | copy-start | bytes 6291460
  159.5 3.8 %copy-start.5 = (bf16[1024,1024]{1,0:T(8,128)(2,1)S(1)}, bf16[1024,1024]{1,0:T(8,128)(2,1)}, u32[]{:S(2)}) copy-start(bf16[1024,1024]{1,0:T(8,128)(2,1)} %get-tuple-element.28) | copy-start | bytes 6291460
  163.3 3.5 %copy-start.20 = (bf16[1024,1024]{1,0:T(8,128)(2,1)S(1)}, bf16[1024,1024]{1,0:T(8,128)(2,1)}, u32[]{:S(2)}) copy-start(bf16[1024,1024]{1,0:T(8,128)(2,1)} %get-tuple-element.23.refs_2_) | copy-start | bytes 6291460
  166.8 2.7 copy-start.13
  166.8 2.7 copy-start.19
  169.4 5.0 %collective-permute-start.6 = (bf16[512,1024]{1,0:T(8,128)(2,1)S(1)}, bf16[512,1024]{1,0:T(8,128)(2,1)S(1)}, u32[]{:S(2)}, u32[]{:S(2)}) collective-permute-start(bf16[512,1024]{1,0:T(8,128)(2,1)S(1)} %slice.61), channel_id=1, source_target_pairs={{0,1},{1,0},{2,3},{3,2},{4,5},{5,4},{6,7},{7,6},{8,9},{9,8},{10,11... | collective-permute-start | bytes 3145736 | tf_op jit(solution)/shard_map/ppermute | solution.py:815
  174.5 2.0 copy-start.15
  323.9 4.8 %copy-start.8 = (bf16[2,1024,1024]{2,1,0:T(8,128)(2,1)S(1)}, bf16[2,1024,1024]{2,1,0:T(8,128)(2,1)}, u32[]{:S(2)}) copy-start(bf16[2,1024,1024]{2,1,0:T(8,128)(2,1)} %get-tuple-element.58) | copy-start | bytes 12582916
  328.8 3.4 copy-start.10
  332.2 2.0 copy-start.14
  332.2 4.0 %copy-start.7 = (bf16[1024,2048]{1,0:T(8,128)(2,1)S(1)}, bf16[1024,2048]{1,0:T(8,128)(2,1)}, u32[]{:S(2)}) copy-start(bf16[1024,2048]{1,0:T(8,128)(2,1)} %get-tuple-element.63) | copy-start | bytes 12582916
  336.2 3.7 %copy-start.6 = (bf16[2048,1024]{1,0:T(8,128)(2,1)S(1)}, bf16[2048,1024]{1,0:T(8,128)(2,1)}, u32[]{:S(2)}) copy-start(bf16[2048,1024]{1,0:T(8,128)(2,1)} %get-tuple-element.64) | copy-start | bytes 12582916
  336.2 5.7 %copy-start.1 = (s32[2,1024]{1,0:T(2,128)S(1)}, s32[2,1024]{1,0:T(2,128)}, u32[]{:S(2)}) copy-start(s32[2,1024]{1,0:T(2,128)} %param.10) | copy-start | bytes 24580

commit v4 on v3

--- a/solution.py
+++ b/solution.py
@@ -376,37 +376,36 @@
         run_op(0, 0)
         run_op(1, 0)
 
-    @pl.when(pid == steps // 2)
-    def _():
-        run_op(0, 1)
-
-    @pl.when(pid == steps - steps // 4)
-    def _():
-        run_op(1, 1)
-
+    def run_ops(stream):
+        for turn in PEERS:
+            @pl.when(pid == turn)
+            def _():
+                run_op(stream, turn)
+
+    run_ops(0)
     peer = pid < steps // 2
     y_acc[ALL] += dot_nn(act_ref[ALL], jnp.where(peer, down_p_ref[ALL], down_o_ref[ALL]))
-    b_acc[ALL] += dot_nt(dpre_ref[ALL], jnp.where(peer, up_p_ref[ALL], up_o_ref[ALL]))
+    run_ops(1)
+    y_local = pltpu.make_async_copy(y_buf, y_out.at[core], y_sem.at[0])
+    y_remote = pltpu.make_async_remote_copy(
+        src_ref=y_buf, dst_ref=y_out.at[core], send_sem=y_sem.at[1], recv_sem=y_sem.at[2], device_id=partner, device_id_type=MESH_ID)
 
     @pl.when(pid == steps - 1)
     def _():
-        run_op(0, 2)
-
         def tile(i, carry):
             at = pl.ds(pl.multiple_of(i * UNIT, UNIT), UNIT)
             y_buf[at, :] = (x_ref[at, :].astype(F32) + y_acc[at, :].astype(BF16).astype(F32)).astype(BF16)
-            db_ref[at, :] = b_acc[at, :].astype(BF16)
             return carry
 
         lax.fori_loop(0, x_ref.shape[0] // UNIT, tile, 0)
-        y_local = pltpu.make_async_copy(y_buf, y_out.at[core], y_sem.at[0])
-        y_remote = pltpu.make_async_remote_copy(
-            src_ref=y_buf, dst_ref=y_out.at[core], send_sem=y_sem.at[1], recv_sem=y_sem.at[2], device_id=partner, device_id_type=MESH_ID)
         y_local.start()
         y_remote.start()
-        run_op(1, 2)
-        run_op(0, 3)
-        run_op(1, 3)
+
+    b_acc[ALL] += dot_nt(dpre_ref[ALL], jnp.where(peer, up_p_ref[ALL], up_o_ref[ALL]))
+
+    @pl.when(pid == steps - 1)
+    def _():
+        db_ref[ALL] = b_acc[ALL].astype(BF16)
         y_local.wait()
         y_remote.wait()
         for flow in FLOW_IDS:

time: 346 us -> 346 us (level)
  no operation moved by 1% of the time
where the time goes in v4:
time: 346 us; the launch traced here: 343 us
  Pallas kernels  257 us (74%)
  matrix products  38.5 us (11%)
  local copies, waits for them, and re-layouts  24.2 us (7%)
  other arithmetic  17.9 us (5%)
    pallas_call x1, Pallas kernels, backward_tail(): pl.pallas_call(functools.partial(tail_kernel, dim, scale, pairs), grid=(p...  145 us
    pallas_call x1, Pallas kernels, mlp_out(): pl.pallas_call(functools.partial(mlp_out_kernel, steps), grid=(steps,), i...  48.1 us
    pallas_call x1, Pallas kernels, attention_forward(): pl.pallas_call(functools.partial(attn_fwd_kernel, dim, scale), grid=(pair...  38.7 us
    dot_general x5, matrix products, dot_tn(): lax.dot_general(lhs, rhs, (((0,), (0,)), ((), ())), preferred_element_typ...  29.3 us
    pallas_call x1, Pallas kernels, mlp_mid(): pl.pallas_call(functools.partial(mlp_mid_kernel, rows), grid=(2 * half,),...  25.2 us
    unnamed x50, local copies, waits for them, and re-layouts  20.1 us
  transfers between devices with their start and end apart: 7, of which 1 were waited for; matrix products, arithmetic and copies ran while one was open for 10% of the time, Pallas kernels for 11%

profile of v4, /device:TPU:0, one launch (start us, length us, event | category | flops | bytes accessed | tf_op | source)
XLA Modules:
  0.0 342.8 jit_solution(6417119862093323638)
XLA Ops:
  2.4 1.9 convert_reduce_fusion
  4.4 0.7 fusion.9
  5.1 2.0 fusion.11.normed_ref
  8.1 1.5 dynamic-slice_bitcast_fusion.dy_ref
  10.3 1.0 copy-done.17
  11.3 38.7 %attn_fwd.1 = (bf16[1024,3072]{1,0:T(8,128)(2,1)}, bf16[1024,1024]{1,0:T(8,128)(2,1)}, f32[8,8,1024]{2,1,0:T(8,128)}, bf16[1024,1024]{1,0:T(8,128)(2,1)}) custom-call(s32[8,1024]{1,0:T(8,128)} %broadcast_in_dim.6.start_ref.refs_0_, bf16[1024,1024]{1,0:T(8,128)(2,1)} %fusion.11.normed_ref, bf16[1024,1536]{1,0:T(8,128)(2,1)} %copy-done.17, ...), custom_call_target="tpu_custom_call" | custom-call | flops 8589934592 | bytes 67108864 | tf_op jit(solution)/shard_map/attn_fwd/pallas_call | solution.py:120
  50.0 4.3 %convert_reduce_fusion.1 = (f32[1024]{0:T(1024)S(1)}, bf16[1024,1024]{1,0:T(8,128)(2,1)S(1)}) fusion(bf16[1024,1024]{1,0:T(8,128)(2,1)} %get-tuple-element.23.refs_2_, bf16[512,1024]{1,0:T(8,128)(2,1)S(1)} %bitcast.25, bf16[512,1024]{1,0:T(8,128)(2,1)} %collective-permute-done.1, bf16[1024,1024]{1,0:T(8,128)(2,1)S(1)} %get-tuple-element.42.refs_8_), kind=kOutput, calls=%fused_computation.11 | convolution fusion | flops 2159016960 | bytes 8392704 | tf_op jit(solution)/shard_map/dot_general | solution.py:52
  54.3 0.7 fusion.17
  55.7 2.0 fusion.12.b_ref
  57.7 25.2 %mlp_mid.1 = (bf16[1024,4096]{1,0:T(8,128)(2,1)}, bf16[1024,4096]{1,0:T(8,128)(2,1)}) custom-call(bf16[1024,1024]{1,0:T(8,128)(2,1)} %fusion.12.b_ref, bf16[1024,1024]{1,0:T(8,128)(2,1)} %dynamic-slice_bitcast_fusion.dy_ref, bf16[1024,2048]{1,0:T(8,128)(2,1)} %collective-permute-done.2.up_p_ref, bf16[1024,2048]{1,0:T(8,128)(2,1)} %up_o_ref.3, ...), custom_call_target="tpu_custom_call" | custom-call | flops 4294967296 | bytes 33554432 | tf_op jit(solution)/shard_map/mlp_mid/pallas_call | solution.py:217
  82.9 7.2 %fusion.32 = bf16[2048,1024]{1,0:T(8,128)(2,1)S(1)} fusion(bf16[1024,1024]{1,0:T(8,128)(2,1)S(1)} %copy-done.12, bf16[1024,4096]{1,0:T(8,128)(2,1)} %get-tuple-element.24.act_ref), kind=kOutput, calls=%fused_computation.40 | convolution fusion | flops 4297064448 | bytes 10485760 | tf_op jit(solution)/shard_map/dot_general | solution.py:60
  90.7 4.9 %fusion.29 = bf16[1024,2048]{1,0:T(8,128)(2,1)S(1)} fusion(bf16[1024,1024]{1,0:T(8,128)(2,1)S(1)} %copy-done.11, bf16[1024,4096]{1,0:T(8,128)(2,1)S(1)} %copy-done.21), kind=kOutput, calls=%fused_computation.39 | convolution fusion | flops 4297064448 | bytes 10485760 | tf_op jit(solution)/shard_map/dot_general | solution.py:60
  96.1 1.7 collective-permute-done.5
  97.8 8.5 %add_convert_fusion.down_hbm = bf16[2048,1024]{1,0:T(8,128)(2,1)} fusion(bf16[2048,1024]{1,0:T(8,128)(2,1)S(1)} %collective-permute-done.5, bf16[1024,1024]{1,0:T(8,128)(2,1)S(1)} %copy-done.12, bf16[1024,4096]{1,0:T(8,128)(2,1)} %get-tuple-element.24.act_ref), kind=kOutput, calls=%fused_computation | convolution fusion | flops 4301258752 | bytes 14680064 | tf_op jit(solution)/shard_map/dot_general | solution.py:60
  106.2 6.3 %add_convert_fusion.1.up_hbm = bf16[1024,2048]{1,0:T(8,128)(2,1)} fusion(bf16[1024,2048]{1,0:T(8,128)(2,1)S(1)} %collective-permute-done.4, bf16[1024,1024]{1,0:T(8,128)(2,1)S(1)} %copy-done.11, bf16[1024,4096]{1,0:T(8,128)(2,1)S(1)} %copy-done.21), kind=kOutput, calls=%fused_computation.1 | convolution fusion | flops 4301258752 | bytes 14680064 | tf_op jit(solution)/shard_map/dot_general | solution.py:60
  112.5 48.1 %mlp_out.1 = (bf16[1024,1024]{1,0:T(8,128)(2,1)}, bf16[6,256,768]{2,1,0:T(8,128)(2,1)}, bf16[2,1024,1024]{2,1,0:T(8,128)(2,1)}) custom-call(bf16[1024,4096]{1,0:T(8,128)(2,1)} %get-tuple-element.24.act_ref, bf16[1024,4096]{1,0:T(8,128)(2,1)} %get-tuple-element.25.dpre_ref, bf16[2048,1024]{1,0:T(8,128)(2,1)} %collective-permute-done.3.down_p_ref, ...), custom_call_target="tpu_custom_call" | custom-call | flops 4294967296 | bytes 33554432 | tf_op jit(solution)/shard_map/mlp_out/pallas_call | solution.py:422
  160.7 3.8 %fusion.19 = (f32[1024]{0:T(1024)S(1)}, f32[1024]{0:T(1024)S(1)}, f32[1024]{0:T(1024)S(1)}) fusion(bf16[1024,1024]{1,0:T(8,128)(2,1)} %copy-done.2, bf16[1024,1024]{1,0:T(8,128)(2,1)} %get-tuple-element.28, f32[1024]{0:T(1024)S(1)} %add_rsqrt_fusion, f32[1024]{0:T(1024)S(1)} %broadcast_multiply_fusion.2, f32[1024]{0:T(1024)S(1)} %convert_element_type.86), kind=kLoop, calls=%fused_computation.28 | loop fusion | flops 10482688 | bytes 4218880 | tf_op jit(solution)/shard_map/reduce_sum | solution.py:40
  164.6 3.5 %fusion.16.refs_9_ = bf16[1024,1024]{1,0:T(8,128)(2,1)S(1)} fusion(bf16[1024,1024]{1,0:T(8,128)(2,1)S(1)} %copy-done.3, bf16[1024,1024]{1,0:T(8,128)(2,1)S(1)} %copy-done.5, f32[1024]{0:T(1024)S(1)} %get-tuple-element.47, f32[1024]{0:T(1024)S(1)} %get-tuple-element.48, f32[1024]{0:T(1024)S(1)} %convert_element_type.86, f32[1024]{0:T(1024)S(1)} %add_rsqrt_fusion, ...), kind=kLoop, calls=%fused_computation.25 | loop fusion | flops 12582912 | bytes 8409092 | tf_op jit(solution)/shard_map/convert_element_type | solution.py:847
  168.1 2.4 fusion.42
  171.1 4.9 %convolution_convert_fusion.refs_3_ = bf16[1024,1024]{1,0:T(8,128)(2,1)} fusion(bf16[1024,1024]{1,0:T(8,128)(2,1)S(1)} %fusion.16.refs_9_, bf16[512,1024]{1,0:T(8,128)(2,1)S(1)} %bitcast.26, bf16[512,1024]{1,0:T(8,128)(2,1)} %collective-permute-done.1), kind=kOutput, calls=%fused_computation.47 | convolution fusion | flops 2152726528 | bytes 6291456 | tf_op jit(solution)/shard_map/dot_general | solution.py:56
  176.0 1.3 fusion.39.refs_13_
  178.6 144.8 %backward_tail.1 = (bf16[1024,2048]{1,0:T(8,128)(2,1)}, bf16[2048,1024]{1,0:T(8,128)(2,1)}, bf16[512,1024]{1,0:T(8,128)(2,1)}, bf16[1024,1536]{1,0:T(8,128)(2,1)...) custom-call(s32[8,1024]{1,0:T(8,128)} %broadcast_in_dim.6.start_ref.refs_0_, ...), custom_call_target="tpu_custom_call" | custom-call | flops 8589934592 | bytes 67108864 | tf_op jit(solution)/shard_map/backward_tail/pallas_call | solution.py:759
  323.4 0.7 convert_element_type.100
  324.6 4.8 %copy.26 = bf16[2,1024,1024]{2,1,0:T(8,128)(2,1)} copy(bf16[2,1024,1024]{2,1,0:T(8,128)(2,1)} %get-tuple-element.57) | data formatting | bytes 8388608
  329.5 2.1 copy.27
  331.6 1.3 copy-done.10
  332.9 1.7 copy.28
  334.8 1.0 copy.29
  335.8 1.1 copy-done.7
  336.9 2.1 copy.30
  339.0 1.6 copy-done.6
  340.6 2.0 copy.31
  (67 shorter events, 7.9 us)
Async XLA Ops:
  0.6 1.8 copy-start
  0.6 9.0 %collective-permute-start = (bf16[1024,1536]{1,0:T(8,128)(2,1)}, bf16[1024,1536]{1,0:T(8,128)(2,1)S(1)}, u32[]{:S(2)}, u32[]{:S(2)}) collective-permute-start(bf16[1024,1536]{1,0:T(8,128)(2,1)} %refs_6_.1), channel_id=1, source_target_pairs={{0,1},{1,0},{2,3},{3,2},{4,5},{5,4},{6,7},{7,6},{8,9},{9,8},{10,11... | collective-permute-start | bytes 9437192 | tf_op jit(solution)/shard_map/ppermute | solution.py:814
  0.7 57.0 %collective-permute-start.2 = (bf16[1024,2048]{1,0:T(8,128)(2,1)}, bf16[1024,2048]{1,0:T(8,128)(2,1)}, u32[]{:S(2)}, u32[]{:S(2)}) collective-permute-start(bf16[1024,2048]{1,0:T(8,128)(2,1)} %up_o_ref.3), channel_id=1, source_target_pairs={{0,1},{1,0},{2,3},{3,2},{4,5},{5,4},{6,7},{7,6},{8,9},{9,8},{10,11... | collective-permute-start | bytes 12582920 | tf_op jit(solution)/shard_map/ppermute | solution.py:814
  1.2 56.5 %collective-permute-start.3 = (bf16[2048,1024]{1,0:T(8,128)(2,1)}, bf16[2048,1024]{1,0:T(8,128)(2,1)}, u32[]{:S(2)}, u32[]{:S(2)}) collective-permute-start(bf16[2048,1024]{1,0:T(8,128)(2,1)} %down_o_ref.3), channel_id=1, source_target_pairs={{0,1},{1,0},{2,3},{3,2},{4,5},{5,4},{6,7},{7,6},{8,9},{9,8},{10,11... | collective-permute-start | bytes 12582920 | tf_op jit(solution)/shard_map/ppermute | solution.py:814
  1.3 48.7 %collective-permute-start.1 = (bf16[512,1024]{1,0:T(8,128)(2,1)}, bf16[512,1024]{1,0:T(8,128)(2,1)}, u32[]{:S(2)}, u32[]{:S(2)}) collective-permute-start(bf16[512,1024]{1,0:T(8,128)(2,1)} %bitcast.24), channel_id=1, source_target_pairs={{0,1},{1,0},{2,3},{3,2},{4,5},{5,4},{6,7},{7,6},{8,9},{9,8},{10,11... | collective-permute-start | bytes 3145736 | tf_op jit(solution)/shard_map/ppermute | solution.py:814
  4.4 45.6 %copy-start.4 = (bf16[1024,1024]{1,0:T(8,128)(2,1)}, bf16[1024,1024]{1,0:T(8,128)(2,1)S(1)}, u32[]{:S(2)}) copy-start(bf16[1024,1024]{1,0:T(8,128)(2,1)S(1)} %get-tuple-element.42.refs_8_) | copy-start | bytes 6291460
  4.4 3.3 copy-start.16
  4.4 3.7 %copy-start.9 = (bf16[2,1024,1024]{2,1,0:T(8,128)(2,1)S(1)}, bf16[2,1024,1024]{2,1,0:T(8,128)(2,1)}, u32[]{:S(2)}) copy-start(bf16[2,1024,1024]{2,1,0:T(8,128)(2,1)} %param.17) | copy-start | bytes 12582916
  9.6 1.7 copy-start.17
  11.3 38.7 %copy-start.18 = (bf16[8,64,1024]{2,1,0:T(8,128)(2,1)S(1)}, bf16[8,64,1024]{2,1,0:T(8,128)(2,1)}, u32[]{:S(2)}) copy-start(bf16[8,64,1024]{2,1,0:T(8,128)(2,1)} %param.14) | copy-start | bytes 3145732
  54.3 1.4 copy-start.2
  57.7 25.2 %copy-start.12 = (bf16[1024,1024]{1,0:T(8,128)(2,1)S(1)}, bf16[1024,1024]{1,0:T(8,128)(2,1)}, u32[]{:S(2)}) copy-start(bf16[1024,1024]{1,0:T(8,128)(2,1)} %dynamic-slice_bitcast_fusion.dy_ref) | copy-start | bytes 6291460
  82.9 7.8 %copy-start.11 = (bf16[1024,1024]{1,0:T(8,128)(2,1)S(1)}, bf16[1024,1024]{1,0:T(8,128)(2,1)}, u32[]{:S(2)}) copy-start(bf16[1024,1024]{1,0:T(8,128)(2,1)} %fusion.12.b_ref) | copy-start | bytes 6291460
  82.9 7.8 %copy-start.21 = (bf16[1024,4096]{1,0:T(8,128)(2,1)S(1)}, bf16[1024,4096]{1,0:T(8,128)(2,1)}, u32[]{:S(2)}) copy-start(bf16[1024,4096]{1,0:T(8,128)(2,1)} %get-tuple-element.25.dpre_ref) | copy-start | bytes 25165828
  90.1 7.6 %collective-permute-start.5 = (bf16[2048,1024]{1,0:T(8,128)(2,1)S(1)}, bf16[2048,1024]{1,0:T(8,128)(2,1)S(1)}, u32[]{:S(2)}, u32[]{:S(2)}) collective-permute-start(bf16[2048,1024]{1,0:T(8,128)(2,1)S(1)} %fusion.32), channel_id=1, source_target_pairs={{0,1},{1,0},{2,3},{3,2},{4,5},{5,4},{6,7},{7,6},{8,9},{9,8},{10,11... | collective-permute-start | bytes 12582920 | tf_op jit(solution)/shard_map/ppermute | solution.py:814
  95.6 10.6 %collective-permute-start.4 = (bf16[1024,2048]{1,0:T(8,128)(2,1)S(1)}, bf16[1024,2048]{1,0:T(8,128)(2,1)S(1)}, u32[]{:S(2)}, u32[]{:S(2)}) collective-permute-start(bf16[1024,2048]{1,0:T(8,128)(2,1)S(1)} %fusion.29), channel_id=1, source_target_pairs={{0,1},{1,0},{2,3},{3,2},{4,5},{5,4},{6,7},{7,6},{8,9},{9,8},{10,11... | collective-permute-start | bytes 12582920 | tf_op jit(solution)/shard_map/ppermute | solution.py:814
  160.7 3.8 %copy-start.3 = (bf16[1024,1024]{1,0:T(8,128)(2,1)S(1)}, bf16[1024,1024]{1,0:T(8,128)(2,1)}, u32[]{:S(2)}) copy-start(bf16[1024,1024]{1,0:T(8,128)(2,1)} %copy-done.2) | copy-start | bytes 6291460
  160.7 3.8 %copy-start.5 = (bf16[1024,1024]{1,0:T(8,128)(2,1)S(1)}, bf16[1024,1024]{1,0:T(8,128)(2,1)}, u32[]{:S(2)}) copy-start(bf16[1024,1024]{1,0:T(8,128)(2,1)} %get-tuple-element.28) | copy-start | bytes 6291460
  164.6 3.5 %copy-start.20 = (bf16[1024,1024]{1,0:T(8,128)(2,1)S(1)}, bf16[1024,1024]{1,0:T(8,128)(2,1)}, u32[]{:S(2)}) copy-start(bf16[1024,1024]{1,0:T(8,128)(2,1)} %get-tuple-element.23.refs_2_) | copy-start | bytes 6291460
  168.0 3.0 copy-start.13
  168.1 3.0 copy-start.19
  170.6 5.3 %collective-permute-start.6 = (bf16[512,1024]{1,0:T(8,128)(2,1)S(1)}, bf16[512,1024]{1,0:T(8,128)(2,1)S(1)}, u32[]{:S(2)}, u32[]{:S(2)}) collective-permute-start(bf16[512,1024]{1,0:T(8,128)(2,1)S(1)} %slice.61), channel_id=1, source_target_pairs={{0,1},{1,0},{2,3},{3,2},{4,5},{5,4},{6,7},{7,6},{8,9},{9,8},{10,11... | collective-permute-start | bytes 3145736 | tf_op jit(solution)/shard_map/ppermute | solution.py:814
  176.0 2.0 copy-start.15
  324.6 4.8 %copy-start.8 = (bf16[2,1024,1024]{2,1,0:T(8,128)(2,1)S(1)}, bf16[2,1024,1024]{2,1,0:T(8,128)(2,1)}, u32[]{:S(2)}) copy-start(bf16[2,1024,1024]{2,1,0:T(8,128)(2,1)} %get-tuple-element.58) | copy-start | bytes 12582916
  329.5 3.4 copy-start.10
  332.9 2.0 copy-start.14
  332.9 4.0 %copy-start.7 = (bf16[1024,2048]{1,0:T(8,128)(2,1)S(1)}, bf16[1024,2048]{1,0:T(8,128)(2,1)}, u32[]{:S(2)}) copy-start(bf16[1024,2048]{1,0:T(8,128)(2,1)} %get-tuple-element.63) | copy-start | bytes 12582916
  336.9 3.7 %copy-start.6 = (bf16[2048,1024]{1,0:T(8,128)(2,1)S(1)}, bf16[2048,1024]{1,0:T(8,128)(2,1)}, u32[]{:S(2)}) copy-start(bf16[2048,1024]{1,0:T(8,128)(2,1)} %get-tuple-element.64) | copy-start | bytes 12582916
  336.9 5.7 %copy-start.1 = (s32[2,1024]{1,0:T(2,128)S(1)}, s32[2,1024]{1,0:T(2,128)}, u32[]{:S(2)}) copy-start(s32[2,1024]{1,0:T(2,128)} %param.10) | copy-start | bytes 24580
